TPU v7x, 1024 devices: a whole 8x8x8 slice. The times are simulated.
1024 devices in a mesh: gx: 32 (over z, x_lo, core), gz: 32 (over x_hi, y).
Axes of the slice: x: 8 (x_hi: 4, x_lo: 2; x = x_hi * 2 + x_lo), y: 8, z: 8, core: 2. Of those that a mesh axis runs over, the one named last changes fastest.
Arguments:
- populations: float32 [19, 8, 256, 4096], P(None, None, 'gz', 'gx'), may hold values from 0.001 to 0.6, as said below
- solid: int32 [8, 256, 4096], P(None, 'gz', 'gx'), may hold values from 0 to 1, as said below
- top_inflow: float32 [5, 256, 4096], P(None, 'gz', 'gx'), may hold values from 0.005 to 0.1
Outputs:
- advanced: float32 [19, 8, 256, 4096], P(None, None, 'gz', 'gx')
Inputs may be any that keep to these rules, and one draw needn't show every extreme that they name: Positive populations near equilibrium. Only the two planes nearest the wall hold solid nodes.
All inputs are finite; a program needn't handle non-finite values.
Results may differ from a plain program's by a relative error of at most 0.0003.
Values sent between devices are 32-bit elements; how exact they have to be, the bound alone decides.
No kernel may reach another device: no remote copies, remote signals or barrier semaphores. Data moves between devices by JAX's collectives and lax.ppermute only.
A program may use at most 32 MiB of HBM per device.

v0:
```python
from functools import reduce
import functools

import jax
import jax.numpy as jnp
import numpy as np
from jax import lax
from jax.sharding import Mesh
from jax.sharding import PartitionSpec as P

STEPS = 2
GX_GZ = ("gx_0", "gx_1", "gx_2", "gz_0", "gz_1")
GX = ("gx_0", "gx_1", "gx_2")
GZ = ("gz_0", "gz_1")


lattice = np.array(
    [
        [0, 0, 0],
        [1, 0, 0],
        [-1, 0, 0],
        [0, 1, 0],
        [0, -1, 0],
        [0, 0, 1],
        [0, 0, -1],
        [1, 1, 0],
        [-1, -1, 0],
        [1, -1, 0],
        [-1, 1, 0],
        [1, 0, 1],
        [-1, 0, -1],
        [1, 0, -1],
        [-1, 0, 1],
        [0, 1, 1],
        [0, -1, -1],
        [0, 1, -1],
        [0, -1, 1],
    ]
)
lattice_weights = [1.0 / 3.0] + [1.0 / 18.0] * 6 + [1.0 / 36.0] * 12
opposite = [0, 2, 1, 4, 3, 6, 5, 8, 7, 10, 9, 12, 11, 14, 13, 16, 15, 18, 17]
incoming = [4, 8, 9, 16, 18]
base_drive = 0.0001
drive_gain = 1.0
target_flow = 0.1


def by_axis(shard, axes):
    return functools.reduce(lax.psum, axes, shard)


def extended(block, sides, width):
    for axis, dim in sides:
        count = lax.axis_size(axis)
        forward = [(i, i + 1) for i in range(count - 1)]
        forward.append((count - 1, 0))
        backward = [(target, source) for source, target in forward]
        low = lax.ppermute(
            lax.slice_in_dim(block, block.shape[dim] - width, None, axis=dim), axis, forward
        )
        high = lax.ppermute(lax.slice_in_dim(block, 0, width, axis=dim), axis, backward)
        block = jnp.concatenate([low, block, high], axis=dim)
    return block


def invert_rows(matrix):
    order = len(matrix)
    work = [
        list(matrix[row]) + [1.0 if col == row else 0.0 for col in range(order)]
        for row in range(order)
    ]
    for col in range(order):
        pivot = max(range(col, order), key=lambda row: abs(work[row][col]))
        work[col], work[pivot] = (work[pivot], work[col])
        lead = work[col][col]
        work[col] = [value / lead for value in work[col]]
        for row in range(order):
            if row != col:
                factor = work[row][col]
                if factor != 0.0:
                    work[row] = [
                        value - factor * other for value, other in zip(work[row], work[col])
                    ]
    return [line[order:] for line in work]


def collide_matrix():
    moment_rows = []
    for power in [
        (0, 0, 0),
        (1, 0, 0),
        (0, 1, 0),
        (0, 0, 1),
        (1, 1, 0),
        (1, 0, 1),
        (0, 1, 1),
        (2, 0, 0),
        (0, 2, 0),
        (0, 0, 2),
        (1, 2, 0),
        (1, 0, 2),
        (2, 1, 0),
        (0, 1, 2),
        (2, 0, 1),
        (0, 2, 1),
        (2, 2, 0),
        (2, 0, 2),
        (0, 2, 2),
    ]:
        moment_rows.append(
            [
                float(
                    int(lattice[q, 0]) ** power[0]
                    * int(lattice[q, 1]) ** power[1]
                    * int(lattice[q, 2]) ** power[2]
                )
                for q in range(19)
            ]
        )
    rates = [0.0] * 4 + [1.8] * 6 + [1.2] * 6 + [1.1] * 3
    inverse = invert_rows(moment_rows)
    result = [
        [
            sum((inverse[row][mid] * rates[mid] * moment_rows[mid][col] for mid in range(19)))
            for col in range(19)
        ]
        for row in range(19)
    ]
    return np.array(result, dtype=np.float32)


def signed_sum(populations, component):
    plus_terms = [populations[index] for index in range(19) if lattice[index, component] == 1]
    minus_terms = [populations[index] for index in range(19) if lattice[index, component] == -1]
    return reduce(lambda left, right: left + right, plus_terms) - reduce(
        lambda left, right: left + right, minus_terms
    )


def moments(populations):
    density = jnp.sum(populations, axis=0)
    momentum = (signed_sum(populations, 0), signed_sum(populations, 1), signed_sum(populations, 2))
    return (density, momentum)


def project(index, velocity):
    result = jnp.zeros_like(velocity[0])
    for component in range(3):
        factor = int(lattice[index, component])
        if factor == 1:
            result = result + velocity[component]
        elif factor == -1:
            result = result - velocity[component]
    return result


def equilibrium(density, velocity):
    speed_square = velocity[0] * velocity[0] + velocity[1] * velocity[1] + velocity[2] * velocity[2]
    terms = []
    for index in range(19):
        along = project(index, velocity)
        terms.append(
            lattice_weights[index]
            * density
            * (1.0 + 3.0 * along + 4.5 * along * along - 1.5 * speed_square)
        )
    return jnp.stack(terms)


def collide(current, density, momentum, driving):
    velocity = tuple((part_value / density for part_value in momentum))
    base_state = equilibrium(density, velocity)
    pushed = equilibrium(density, (velocity[0] + driving / density, velocity[1], velocity[2]))
    relaxed = jnp.tensordot(
        jnp.asarray(collide_matrix()), current - base_state, axes=1, precision=lax.Precision.HIGHEST
    )
    return current - relaxed + pushed - base_state


def shift_planes(carried, blocked, step_y):
    if step_y == 1:
        carried = jnp.concatenate([jnp.zeros_like(carried[:1]), carried[:-1]], axis=0)
        blocked = jnp.concatenate([jnp.ones_like(blocked[:1]), blocked[:-1]], axis=0)
    elif step_y == -1:
        carried = jnp.concatenate([carried[1:], jnp.zeros_like(carried[:1])], axis=0)
        blocked = jnp.concatenate([blocked[1:], jnp.zeros_like(blocked[:1])], axis=0)
    return (carried, blocked)


def trim(array, cut):
    if cut == 0:
        return array
    return array[..., cut:-cut, cut:-cut]


def stream_block(padded, solid_padded, top_inflow, before):
    planes = padded.shape[1]
    width_z = padded.shape[2] - 2
    width_x = padded.shape[3] - 2
    collided = trim(padded, 1)
    solid = trim(solid_padded, 1)
    results = []
    for index in range(19):
        step_x = int(lattice[index, 0])
        step_y = int(lattice[index, 1])
        step_z = int(lattice[index, 2])
        carried = padded[
            index, :, 1 - step_z : 1 - step_z + width_z, 1 - step_x : 1 - step_x + width_x
        ]
        blocked = solid_padded[
            :, 1 - step_z : 1 - step_z + width_z, 1 - step_x : 1 - step_x + width_x
        ]
        carried, blocked = shift_planes(carried, blocked, step_y)
        arrived = jnp.where(blocked == 1, collided[opposite[index]], carried)
        if step_y == -1:
            arrived = arrived.at[planes - 1].set(top_inflow[incoming.index(index)])
        results.append(arrived)
    return jnp.where(solid[None] == 1, before, jnp.stack(results))


def total_flow(local_sum, node_total):
    return by_axis(local_sum, GX_GZ) / node_total


def local(populations, solid, top_inflow):
    node_total = float(
        populations.shape[1]
        * populations.shape[2]
        * populations.shape[3]
        * lax.axis_size(GX)
        * lax.axis_size(GZ)
    )
    fluid_nodes = (1 - solid).astype(jnp.float32)
    planes = populations.shape[1]
    inflow_count = top_inflow.shape[0]
    inflow_planes = jnp.concatenate(
        [top_inflow, jnp.zeros((planes - inflow_count,) + top_inflow.shape[1:], jnp.float32)],
        axis=0,
    )
    stacked = jnp.concatenate(
        [populations, solid.astype(jnp.float32)[None], inflow_planes[None]], axis=0
    )
    wide = extended(stacked, ((GX, 3), (GZ, 2)), STEPS)
    solid_wide = jnp.where(wide[19] == 1.0, 1, 0).astype(jnp.int32)
    inflow_wide = wide[20, :inflow_count]
    current = wide[:19]
    for step_index in range(STEPS):
        margin = STEPS - step_index
        density, momentum = moments(current)
        if step_index == 0:
            local_sum = jnp.sum(signed_sum(populations, 0) * fluid_nodes)
        else:
            local_sum = jnp.sum(trim(momentum[0], margin) * fluid_nodes)
        bulk_flow = total_flow(local_sum, node_total)
        driving = base_drive + drive_gain * (target_flow - bulk_flow)
        collided = collide(current, density, momentum, driving)
        current = stream_block(
            collided,
            trim(solid_wide, STEPS - margin),
            trim(inflow_wide, STEPS - margin + 1),
            trim(current, 1),
        )
    return current


def solution(mesh):
    finer = Mesh(mesh.devices.reshape(8, 2, 2, 4, 8), ("gx_0", "gx_1", "gx_2", "gz_0", "gz_1"))
    placed = (P(None, None, GZ, GX), P(None, GZ, GX), P(None, GZ, GX))
    return jax.shard_map(
        local, mesh=finer, in_specs=placed, out_specs=P(None, None, GZ, GX), check_vma=False
    )
```

profile of v0, /device:TPU:2, one launch (start us, length us, event | category | flops | bytes accessed | tf_op | source)
XLA Modules:
  0.0 199.7 jit_solution(2879697278570369971)
XLA Ops:
  0.0 1.2 copy_dynamic-update-slice_fusion
  1.2 0.8 convert_bitcast_fusion
  2.0 0.7 pad_bitcast_fusion
  3.5 1.9 collective-permute-start
  6.0 3.6 %collective-permute-start.1 = (f32[21,8,8,2]{0,2,3,1:T(8,128)S(1)}, f32[21,8,8,2]{0,2,3,1:T(8,128)S(1)}, u32[]{:S(2)}, u32[]{:S(2)}) collective-permute-start(f32[21,8,8,2]{0,2,3,1:T(8,128)S(1)} %copy.2182), channel_id=1, source_target_pairs={{32,0},{64,32},{96,64},{128,96},{160,128},{192,160},{224,192},{256... | collective-permute-start | bytes 32264 | tf_op jit(solution)/shard_map/ppermute | solution.py:61
  9.7 0.8 copy.2183
  10.5 1.6 collective-permute-done.1
  12.0 0.8 copy.2184
  12.8 1.2 pad_maximum_fusion.3
  14.0 3.6 %collective-permute-start.2 = (f32[21,8,2,132]{3,1,2,0:T(8,128)}, f32[21,8,2,132]{3,1,2,0:T(8,128)S(1)}, u32[]{:S(2)}, u32[]{:S(2)}) collective-permute-start(f32[21,8,2,132]{3,1,2,0:T(8,128)} %get-tuple-element.145), channel_id=1, source_target_pairs={{0,1},{1,2},{2,3},{3,4},{4,5},{5,6},{6,7},{7,8},{8,9},{9,10},{10,1... | collective-permute-start | bytes 532232 | tf_op jit(solution)/shard_map/ppermute | solution.py:58
  17.6 7.7 %collective-permute-start.3 = (f32[21,8,2,132]{3,1,2,0:T(8,128)}, f32[21,8,2,132]{3,1,2,0:T(8,128)}, u32[]{:S(2)}, u32[]{:S(2)}) collective-permute-start(f32[21,8,2,132]{3,1,2,0:T(8,128)} %get-tuple-element.146), channel_id=1, source_target_pairs={{1,0},{2,1},{3,2},{4,3},{5,4},{6,5},{7,6},{8,7},{9,8},{10,9},{11,1... | collective-permute-start | bytes 532232 | tf_op jit(solution)/shard_map/ppermute | solution.py:61
  26.0 28.8 %psum.70 = f32[]{:T(128)} all-reduce(f32[]{:T(128)} %fusion.229), channel_id=1, replica_groups=mesh['gx_0'=8,'gx_1'=2,'gx_2'=2,'gz_0'=4,'gz_1'=8] {'gx_0'}, use_global_device_ids=true, to_apply=%region_2.3 | all-reduce | flops 1 | bytes 8 | tf_op jit(solution)/shard_map/psum | solution.py:49
  54.8 9.0 %psum.71 = f32[]{:T(128)} all-reduce(f32[]{:T(128)} %psum.70), channel_id=1, replica_groups=mesh['gx_0'=8,'gx_1'=2,'gx_2'=2,'gz_0'=4,'gz_1'=8] {'gx_1'}, use_global_device_ids=true, to_apply=%region_3.4 | all-reduce | flops 1 | bytes 8 | tf_op jit(solution)/shard_map/psum | solution.py:49
  63.8 3.1 %psum.72 = f32[]{:T(128)} all-reduce(f32[]{:T(128)} %psum.71), channel_id=1, replica_groups=mesh['gx_0'=8,'gx_1'=2,'gx_2'=2,'gz_0'=4,'gz_1'=8] {'gx_2'}, use_global_device_ids=true, to_apply=%region_4.5 | all-reduce | flops 1 | bytes 8 | tf_op jit(solution)/shard_map/psum | solution.py:49
  66.9 9.3 %psum.73 = f32[]{:T(128)} all-reduce(f32[]{:T(128)} %psum.72), channel_id=1, replica_groups=mesh['gx_0'=8,'gx_1'=2,'gx_2'=2,'gz_0'=4,'gz_1'=8] {'gz_0'}, use_global_device_ids=true, to_apply=%region_5.6 | all-reduce | flops 1 | bytes 8 | tf_op jit(solution)/shard_map/psum | solution.py:49
  76.1 17.5 %psum.74 = f32[]{:T(128)} all-reduce(f32[]{:T(128)} %psum.73), channel_id=1, replica_groups=mesh['gx_0'=8,'gx_1'=2,'gx_2'=2,'gz_0'=4,'gz_1'=8] {'gz_1'}, use_global_device_ids=true, to_apply=%region_6.7 | all-reduce | flops 1 | bytes 8 | tf_op jit(solution)/shard_map/psum | solution.py:49
  94.3 2.0 %pad_maximum_fusion = f32[21,8,12,132]{3,1,2,0:T(8,128)S(1)} fusion(f32[21,8,2,132]{3,1,2,0:T(8,128)} %collective-permute-done.3, f32[21,8,8,2]{3,1,2,0:T(8,128)} %copy-done.3, f32[21,8,8,128]{3,1,2,0:T(8,128)S(1)} %constant_dynamic-update-slice_fusion, f32[21,8,8,2]{3,1,2,0:T(8,128)} %copy-done.2, f32[21,8,2,132]{3,1,2,0:T(8,128)S(1)} %collective-permute-done.2), kind=kLoop, calls=%fused_computation.2 | loop fusion | flops 1064448 | bytes 2128896 | tf_op jit(solution)/shard_map/concatenate | solution.py:62
  98.8 2.9 %fusion = f32[19,8,12,132]{3,0,2,1:T(8,128)S(1)} fusion(f32[19,19,1,1]{1,0,3,2:T(8,128)S(1)} %copy-done.19, f32[19,8,12,132]{3,1,2,0:T(8,128)S(1)} %slice_subtract_fusion), kind=kOutput, calls=%fused_computation | convolution fusion | flops 54895104 | bytes 1927588 | tf_op jit(solution)/shard_map/dot_general | solution.py:174
  101.8 1.4 fusion.5
  103.2 1.2 slice_bitcast_fusion.1
  104.6 1.0 slice_bitcast_fusion.27
  107.8 0.7 copy.2237
  109.3 0.7 copy.2221
  114.0 1.6 scatter.40
  115.6 1.6 scatter.39
  117.1 1.6 scatter.36
  118.7 1.6 scatter.35
  120.2 1.5 scatter.34
  121.8 1.3 fusion.9
  126.2 0.9 copy-done.4
  128.4 1.2 copy-done
  130.3 16.8 %psum.75 = f32[]{:T(128)} all-reduce(f32[]{:T(128)} %fusion.210), channel_id=1, replica_groups=mesh['gx_0'=8,'gx_1'=2,'gx_2'=2,'gz_0'=4,'gz_1'=8] {'gx_0'}, use_global_device_ids=true, to_apply=%region_9.10 | all-reduce | flops 1 | bytes 8 | tf_op jit(solution)/shard_map/psum | solution.py:49
  147.1 5.8 %psum.76 = f32[]{:T(128)} all-reduce(f32[]{:T(128)} %psum.75), channel_id=1, replica_groups=mesh['gx_0'=8,'gx_1'=2,'gx_2'=2,'gz_0'=4,'gz_1'=8] {'gx_1'}, use_global_device_ids=true, to_apply=%region_10.11 | all-reduce | flops 1 | bytes 8 | tf_op jit(solution)/shard_map/psum | solution.py:49
  152.9 3.1 %psum.77 = f32[]{:T(128)} all-reduce(f32[]{:T(128)} %psum.76), channel_id=1, replica_groups=mesh['gx_0'=8,'gx_1'=2,'gx_2'=2,'gz_0'=4,'gz_1'=8] {'gx_2'}, use_global_device_ids=true, to_apply=%region_11.12 | all-reduce | flops 1 | bytes 8 | tf_op jit(solution)/shard_map/psum | solution.py:49
  156.0 9.6 %psum.78 = f32[]{:T(128)} all-reduce(f32[]{:T(128)} %psum.77), channel_id=1, replica_groups=mesh['gx_0'=8,'gx_1'=2,'gx_2'=2,'gz_0'=4,'gz_1'=8] {'gz_0'}, use_global_device_ids=true, to_apply=%region_12.13 | all-reduce | flops 1 | bytes 8 | tf_op jit(solution)/shard_map/psum | solution.py:49
  165.6 16.7 %psum.79 = f32[]{:T(128)} all-reduce(f32[]{:T(128)} %psum.78), channel_id=1, replica_groups=mesh['gx_0'=8,'gx_1'=2,'gx_2'=2,'gz_0'=4,'gz_1'=8] {'gz_1'}, use_global_device_ids=true, to_apply=%region_13.14 | all-reduce | flops 1 | bytes 8 | tf_op jit(solution)/shard_map/psum | solution.py:49
  183.0 1.6 constant_dynamic-update-slice_fusion.96
  185.8 1.1 copy-done.1
  187.7 2.4 %fusion.2 = f32[19,8,10,130]{3,0,2,1:T(8,128)S(1)} fusion(f32[19,19,1,1]{1,0,3,2:T(8,128)S(1)} %copy-done.20, f32[19,8,10,130]{3,1,2,0:T(8,128)S(1)} %sub.845), kind=kOutput, calls=%fused_computation.3 | convolution fusion | flops 45052800 | bytes 1582244 | tf_op jit(solution)/shard_map/dot_general | solution.py:174
  190.1 1.2 fusion.7
  191.6 0.7 fusion.240
  193.6 0.7 scatter.49
  194.3 0.7 scatter.46
  195.0 0.7 scatter.45
  195.7 0.7 scatter.44
  196.4 0.7 scatter.41
  197.3 0.8 fusion.226
  198.7 0.9 copy.2328
  (212 shorter events, 20.2 us)
Async XLA Ops:
  3.5 6.1 %collective-permute-start = (f32[21,8,8,2]{0,2,3,1:T(8,128)S(1)}, f32[21,8,8,2]{0,2,3,1:T(8,128)S(1)}, u32[]{:S(2)}, u32[]{:S(2)}) collective-permute-start(f32[21,8,8,2]{0,2,3,1:T(8,128)S(1)} %copy.2181), channel_id=1, source_target_pairs={{0,32},{32,64},{64,96},{96,128},{128,160},{160,192},{192,224},{224... | collective-permute-start | bytes 32264 | tf_op jit(solution)/shard_map/ppermute | solution.py:58
  6.0 6.0 %collective-permute-start.1 = (f32[21,8,8,2]{0,2,3,1:T(8,128)S(1)}, f32[21,8,8,2]{0,2,3,1:T(8,128)S(1)}, u32[]{:S(2)}, u32[]{:S(2)}) collective-permute-start(f32[21,8,8,2]{0,2,3,1:T(8,128)S(1)} %copy.2182), channel_id=1, source_target_pairs={{32,0},{64,32},{96,64},{128,96},{160,128},{192,160},{224,192},{256... | collective-permute-start | bytes 32264 | tf_op jit(solution)/shard_map/ppermute | solution.py:61
  10.5 3.6 %copy-start.2 = (f32[21,8,8,2]{3,1,2,0:T(8,128)}, f32[21,8,8,2]{3,1,2,0:T(8,128)S(1)}, u32[]{:S(2)}) copy-start(f32[21,8,8,2]{3,1,2,0:T(8,128)S(1)} %copy.2183) | copy-start | bytes 32260
  12.8 13.2 %copy-start.3 = (f32[21,8,8,2]{3,1,2,0:T(8,128)}, f32[21,8,8,2]{3,1,2,0:T(8,128)S(1)}, u32[]{:S(2)}) copy-start(f32[21,8,8,2]{3,1,2,0:T(8,128)S(1)} %copy.2184) | copy-start | bytes 32260
  12.8 12.5 %copy-start.5 = (f32[19,8,8,128]{3,2,1,0:T(8,128)S(1)}, f32[19,8,8,128]{3,2,1,0:T(8,128)}, u32[]{:S(2)}) copy-start(f32[19,8,8,128]{3,2,1,0:T(8,128)} %param.25) | copy-start | bytes 1867780
  12.8 12.5 %copy-start.17 = (s32[8,8,128]{2,1,0:T(8,128)S(1)}, s32[8,8,128]{2,1,0:T(8,128)}, u32[]{:S(2)}) copy-start(s32[8,8,128]{2,1,0:T(8,128)} %param.26) | copy-start | bytes 98308
  14.0 80.3 %collective-permute-start.2 = (f32[21,8,2,132]{3,1,2,0:T(8,128)}, f32[21,8,2,132]{3,1,2,0:T(8,128)S(1)}, u32[]{:S(2)}, u32[]{:S(2)}) collective-permute-start(f32[21,8,2,132]{3,1,2,0:T(8,128)} %get-tuple-element.145), channel_id=1, source_target_pairs={{0,1},{1,2},{2,3},{3,4},{4,5},{5,6},{6,7},{7,8},{8,9},{9,10},{10,1... | collective-permute-start | bytes 532232 | tf_op jit(solution)/shard_map/ppermute | solution.py:58
  17.6 76.7 %collective-permute-start.3 = (f32[21,8,2,132]{3,1,2,0:T(8,128)}, f32[21,8,2,132]{3,1,2,0:T(8,128)}, u32[]{:S(2)}, u32[]{:S(2)}) collective-permute-start(f32[21,8,2,132]{3,1,2,0:T(8,128)} %get-tuple-element.146), channel_id=1, source_target_pairs={{1,0},{2,1},{3,2},{4,3},{5,4},{6,5},{7,6},{8,7},{9,8},{10,9},{11,1... | collective-permute-start | bytes 532232 | tf_op jit(solution)/shard_map/ppermute | solution.py:61
  98.1 0.7 copy-start.19
  121.8 3.4 %copy-start.16 = (f32[1,8,10,130]{3,1,2,0:T(8,128)S(1)}, f32[1,8,10,130]{3,1,2,0:T(8,128)}, u32[]{:S(2)}) copy-start(f32[1,8,10,130]{3,1,2,0:T(8,128)} %scatter.34) | copy-start | bytes 124804
  121.8 4.0 %copy-start.6 = (f32[8,10,130]{2,0,1:T(8,128)S(1)}, f32[8,10,130]{2,0,1:T(8,128)}, u32[]{:S(2)}) copy-start(f32[8,10,130]{2,0,1:T(8,128)} %get-tuple-element.167) | copy-start | bytes 124804
  121.8 4.0 %copy-start.7 = (f32[8,10,130]{2,0,1:T(8,128)S(1)}, f32[8,10,130]{2,0,1:T(8,128)}, u32[]{:S(2)}) copy-start(f32[8,10,130]{2,0,1:T(8,128)} %get-tuple-element.168) | copy-start | bytes 124804
  121.8 4.0 %copy-start.8 = (f32[8,10,130]{2,0,1:T(8,128)S(1)}, f32[8,10,130]{2,0,1:T(8,128)}, u32[]{:S(2)}) copy-start(f32[8,10,130]{2,0,1:T(8,128)} %get-tuple-element.173) | copy-start | bytes 124804
  121.8 4.0 %copy-start.9 = (f32[8,10,130]{2,0,1:T(8,128)S(1)}, f32[8,10,130]{2,0,1:T(8,128)}, u32[]{:S(2)}) copy-start(f32[8,10,130]{2,0,1:T(8,128)} %get-tuple-element.174) | copy-start | bytes 124804
  121.8 4.0 %copy-start.10 = (f32[8,10,130]{2,0,1:T(8,128)S(1)}, f32[8,10,130]{2,0,1:T(8,128)}, u32[]{:S(2)}) copy-start(f32[8,10,130]{2,0,1:T(8,128)} %get-tuple-element.175) | copy-start | bytes 124804
  121.8 4.0 %copy-start.11 = (f32[8,10,130]{2,0,1:T(8,128)S(1)}, f32[8,10,130]{2,0,1:T(8,128)}, u32[]{:S(2)}) copy-start(f32[8,10,130]{2,0,1:T(8,128)} %get-tuple-element.176) | copy-start | bytes 124804
  125.8 1.4 copy-start.4
  125.8 1.5 copy-start.15
  125.8 1.6 copy-start.14
  126.2 1.6 copy-start.13
  126.2 1.6 copy-start.12
  126.2 1.6 copy-start.18
  128.4 1.2 copy-start
  185.5 1.4 copy-start.1
  187.0 0.7 copy-start.20
where the time goes:
time: 201 us; the launch traced here: 200 us
  blocking collectives  120 us (60%)
  local copies, waits for them, and re-layouts  37 us (18%)
  starting transfers between devices  16.8 us (8%)
  other arithmetic  16.6 us (8%)
  matrix products  5.37 us (3%)
  between operations  2.65 us (1%)
    psum x10, blocking collectives, by_axis(): return functools.reduce(lax.psum, axes, shard)  120 us
    scatter x10, local copies, waits for them, and re-layouts, stream_block(): arrived = arrived.at[planes - 1].set(top_inflow[incoming.index(index)])  11.3 us
    ppermute x2, starting transfers between devices, extended(): lax.ppermute(lax.slice_in_dim(block, 0, width, axis=dim), axis, backward)  11.3 us
    unnamed x78, local copies, waits for them, and re-layouts  8.84 us
    another operation x18, local copies, waits for them, and re-layouts, stream_block(): return jnp.where(solid[None] == 1, before, jnp.stack(results))  6.59 us
    ppermute x2, starting transfers between devices, extended(): lax.ppermute(lax.slice_in_dim(block, block.shape[dim] - width, None, axis...  5.5 us
    dot_general x2, matrix products, collide(): jnp.tensordot(jnp.asarray(collide_matrix()), current - base_state, axes=1...  5.37 us
  transfers between devices with their start and end apart: 4, of which 1 were waited for; matrix products, arithmetic and copies ran while one was open for 1% of the time, Pallas kernels for 0%

commit v1 on v0

v1 whole, which is shorter than its diff:
```python
import jax
import jax.numpy as jnp
from jax import lax
from jax.experimental import pallas as pl
from jax.experimental.pallas import tpu as pltpu
from jax.sharding import PartitionSpec as P

Q = 19
PLANES = 8
LATTICE = (
    (0, 0, 0),
    (1, 0, 0),
    (-1, 0, 0),
    (0, 1, 0),
    (0, -1, 0),
    (0, 0, 1),
    (0, 0, -1),
    (1, 1, 0),
    (-1, -1, 0),
    (1, -1, 0),
    (-1, 1, 0),
    (1, 0, 1),
    (-1, 0, -1),
    (1, 0, -1),
    (-1, 0, 1),
    (0, 1, 1),
    (0, -1, -1),
    (0, 1, -1),
    (0, -1, 1),
)
OPPOSITE = (0, 2, 1, 4, 3, 6, 5, 8, 7, 10, 9, 12, 11, 14, 13, 16, 15, 18, 17)
INCOMING = (4, 8, 9, 16, 18)
SECOND, THIRD, FOURTH = 1.8, 1.2, 1.1
BASE_DRIVE = 0.0001
DRIVE_GAIN = 1.0
TARGET_FLOW = 0.1

FLAG_SLOT = Q * PLANES
INFLOW_SLOT = FLAG_SLOT + 2
SLOTS = INFLOW_SLOT + len(INCOMING)
TILES = 5
ZROWS = SLOTS + TILES


def relax(f):
    along = []
    for p in (1, 3, 5):
        along.append((f[p] + f[p + 1], f[p] - f[p + 1]))
    diagonal = []
    for p in (7, 11, 15):
        a, b = f[p] + f[p + 1], f[p + 2] + f[p + 3]
        c, d = f[p] - f[p + 1], f[p + 2] - f[p + 3]
        diagonal.append((a + b, a - b, c + d, c - d))
    (xxyy, xy, xyy, xxy), (xxzz, xz, xzz, xxz), (yyzz, yz, yzz, yyz) = diagonal
    density = f[0] + (along[0][0] + along[1][0] + along[2][0]) + (xxyy + xxzz + yyzz)
    jx = along[0][1] + xyy + xzz
    jy = along[1][1] + xxy + yzz
    jz = along[2][1] + xxz + yyz
    inv = 1.0 / density
    ux, uy, uz = jx * inv, jy * inv, jz * inv
    exx, eyy, ezz = jx * ux, jy * uy, jz * uz
    third = density * (1.0 / 3.0)
    ninth = density * (1.0 / 9.0)
    xx = along[0][0] + xxyy + xxzz
    yy = along[1][0] + xxyy + yyzz
    zz = along[2][0] + xxzz + yyzz
    dxx = SECOND * (xx - third - exx)
    dyy = SECOND * (yy - third - eyy)
    dzz = SECOND * (zz - third - ezz)
    dxy = SECOND * (xy - jx * uy)
    dxz = SECOND * (xz - jx * uz)
    dyz = SECOND * (yz - jy * uz)
    x3, y3, z3 = jx * (1.0 / 3.0), jy * (1.0 / 3.0), jz * (1.0 / 3.0)
    dxyy, dxzz = THIRD * (xyy - x3), THIRD * (xzz - x3)
    dxxy, dyzz = THIRD * (xxy - y3), THIRD * (yzz - y3)
    dxxz, dyyz = THIRD * (xxz - z3), THIRD * (yyz - z3)
    half = 0.5 * (exx + eyy + ezz)
    dxxyy = FOURTH * (xxyy - ninth - (half - 0.5 * ezz) * (2.0 / 3.0) + ezz * (1.0 / 6.0))
    dxxzz = FOURTH * (xxzz - ninth - (half - 0.5 * eyy) * (2.0 / 3.0) + eyy * (1.0 / 6.0))
    dyyzz = FOURTH * (yyzz - ninth - (half - 0.5 * exx) * (2.0 / 3.0) + exx * (1.0 / 6.0))
    out = [None] * Q
    out[0] = f[0] + (dxx + dyy + dzz) - (dxxyy + dxxzz + dyyzz)
    for p, even, odd in (
        (1, dxx - dxxyy - dxxzz, dxyy + dxzz),
        (3, dyy - dxxyy - dyyzz, dxxy + dyzz),
        (5, dzz - dxxzz - dyyzz, dxxz + dyyz),
    ):
        out[p] = f[p] - 0.5 * (even - odd)
        out[p + 1] = f[p + 1] - 0.5 * (even + odd)
    for p, four, cross, first, second in (
        (7, dxxyy, dxy, dxyy, dxxy),
        (11, dxxzz, dxz, dxzz, dxxz),
        (15, dyyzz, dyz, dyzz, dyyz),
    ):
        same, other = 0.25 * (four + cross), 0.25 * (four - cross)
        total, rest = 0.25 * (first + second), 0.25 * (first - second)
        out[p] = f[p] - (same + total)
        out[p + 1] = f[p + 1] - (same - total)
        out[p + 2] = f[p + 2] - (other + rest)
        out[p + 3] = f[p + 3] - (other - rest)
    return out, (ux, uy, uz), inv


def weight(index):
    return 1.0 / 3.0 if index == 0 else (1.0 / 18.0 if index < 7 else 1.0 / 36.0)


def push_parts(index, velocity, inv):
    cx, cy, cz = LATTICE[index]
    along = 9.0 * velocity[0] - 3.0 * velocity[0] + 3.0 * cx
    if cy:
        along = along + (9.0 * cx * cy) * velocity[1]
    if cz:
        along = along + (9.0 * cx * cz) * velocity[2]
    return weight(index) * along, (3.0 * weight(index)) * inv


def driven(relaxed, velocity, inv, drive):
    ux, uy, uz = velocity
    square = drive * drive * inv
    still = -3.0 * drive * ux - 1.5 * square
    moved = still + 9.0 * drive * ux + 4.5 * square
    three = 3.0 * drive
    up, down = moved + three, moved - three
    hy, hz = 9.0 * drive * uy, 9.0 * drive * uz
    calm = still * (1.0 / 36.0)
    out = list(relaxed)
    out[0] = out[0] + still * (1.0 / 3.0)
    out[1] = out[1] + up * (1.0 / 18.0)
    out[2] = out[2] + down * (1.0 / 18.0)
    for index in (3, 4, 5, 6):
        out[index] = out[index] + (calm + calm)
    for p, side in ((7, hy), (11, hz)):
        out[p] = out[p] + (up + side) * (1.0 / 36.0)
        out[p + 1] = out[p + 1] + (down + side) * (1.0 / 36.0)
        out[p + 2] = out[p + 2] + (up - side) * (1.0 / 36.0)
        out[p + 3] = out[p + 3] + (down - side) * (1.0 / 36.0)
    for index in (15, 16, 17, 18):
        out[index] = out[index] + calm
    return out


def rolled(value, step_z, step_x):
    if step_z:
        value = pltpu.roll(value, step_z % value.shape[0], 0)
    if step_x:
        value = pltpu.roll(value, step_x % value.shape[1], 1)
    return value


def slot_values(pops, solid, inflow):
    values = [lambda q=q, y=y: pops[q, y] for q in range(Q) for y in range(PLANES)]
    values += [lambda y=y: solid[y].astype(jnp.float32) for y in range(2)]
    values += [lambda i=i: inflow[i] for i in range(len(INCOMING))]
    return values


def pack_columns(pops, solid, inflow, edges):
    lane = lax.broadcasted_iota(jnp.int32, (8, 128), 1)
    values = slot_values(pops, solid, inflow)
    for tile in range(TILES):
        first = jnp.zeros((8, 128), jnp.float32)
        for slot in range(32):
            if tile * 32 + slot < SLOTS:
                offset = 4 * slot
                moved = rolled(values[tile * 32 + slot](), 0, offset)
                place = ((lane + (128 - offset + 2)) & 127) < 4
                first = jnp.where(place, moved, first)
        edges[tile] = first


def pack_rows(pops, solid, inflow, left, right, below, above, sides):
    lane = lax.broadcasted_iota(jnp.int32, (8, 128), 1)
    for index, value in enumerate(slot_values(pops, solid, inflow)):
        tile = value()
        below[index] = tile[0:2]
        above[index] = tile[6:8]
    for tile in range(TILES):
        both = jnp.where((lane & 3) < 2, right[tile], left[tile])
        sides[tile] = both
        below[SLOTS + tile] = both[0:2]
        above[SLOTS + tile] = both[6:8]


def lay_sides(sides, below, above, ring):
    for tile in range(TILES):
        ring[tile, 0:8] = sides[tile]
        ring[tile, 8:10] = above[SLOTS + tile]
        ring[tile, 14:16] = below[SLOTS + tile]


def lay_out(target, main, slot, ring, below, above):
    target[0:8, 0:128] = main
    target[8:10, 0:128] = above[slot]
    target[14:16, 0:128] = below[slot]
    target[:, 128:256] = rolled(ring[slot // 32], 0, -4 * (slot % 32))


def tally(pops, solid, inflow, sides, below, above, out, ring, flags):
    lay_sides(sides, below, above, ring)
    for y in range(2):
        lay_out(flags.at[y], solid[y].astype(jnp.float32), FLAG_SLOT + y, ring, below, above)
    flow = jnp.zeros((8, 128), jnp.float32)
    count = jnp.full((8, 128), float(PLANES - 2), jnp.float32)
    fluid = [1.0 - flags[y, 0:8, 0:128] for y in range(2)]
    for y in range(PLANES):
        f = pops
        jx = (
            (f[1, y] - f[2, y])
            + (f[7, y] - f[8, y])
            + (f[9, y] - f[10, y])
            + (f[11, y] - f[12, y])
            + (f[13, y] - f[14, y])
        )
        flow = flow + (jx * fluid[y] if y < 2 else jx)
    count = count + fluid[0] + fluid[1]
    one = flow
    two = jnp.zeros((8, 128), jnp.float32)
    for y in (0, 1, 2, PLANES - 1):
        relaxed, velocity, inv = relax([pops[q, y] for q in range(Q)])
        for index in range(Q):
            cx, cy, cz = LATTICE[index]
            target = y + cy
            if not cx or 1 < target < PLANES:
                continue
            linear, square = push_parts(index, velocity, inv)
            if target >= PLANES:
                factor = -float(cx)
            elif target < 0:
                factor = (-2.0 * cx) * fluid[y]
            else:
                hit = rolled(flags[target], -cz, -cx)[0:8, 0:128]
                factor = (-2.0 * cx) * hit
                if y < 2:
                    factor = factor * fluid[y]
            one = one + factor * relaxed[index]
            count = count + factor * linear
            two = two + factor * square
    one = one + (inflow[INCOMING.index(9)] - inflow[INCOMING.index(8)])
    lane = lax.broadcasted_iota(jnp.int32, (1, 128), 1)
    packed = jnp.zeros((1, 128), jnp.float32)
    for place, part in enumerate((flow, one, count, two)):
        total = jnp.sum(jnp.sum(part, axis=0, keepdims=True), axis=1, keepdims=True)
        packed = jnp.where(lane == place, total, packed)
    out[...] = jnp.broadcast_to(packed[None], out.shape)


def advance(node_total, pops, solid, inflow, sides, below, above, sums, out, ring, flags, entry, hits, now, moved):
    total = jnp.sum(sums[...], axis=0)
    flow, one, count, two = (total[:, i : i + 1] for i in range(4))
    first = BASE_DRIVE + DRIVE_GAIN * (TARGET_FLOW - flow / node_total)
    later = (one + count * first + two * (first * first)) / node_total
    second = BASE_DRIVE + DRIVE_GAIN * (TARGET_FLOW - later)

    lay_sides(sides, below, above, ring)
    for y in range(2):
        lay_out(flags.at[y], solid[y].astype(jnp.float32), FLAG_SLOT + y, ring, below, above)
        for step_z in (-1, 0, 1):
            for step_x in (-1, 0, 1):
                hits[y, 3 * step_z + step_x + 4] = rolled(flags[y], step_z, step_x)
    for i in range(len(INCOMING)):
        lay_out(entry.at[i], inflow[i], INFLOW_SLOT + i, ring, below, above)
    for y in range(PLANES):
        for q in range(Q):
            lay_out(now.at[y, q], pops[q, y], q * PLANES + y, ring, below, above)

    for step in range(2):
        drive = jnp.broadcast_to(first if step == 0 else second, (8, 128))

        def collide(y, carry):
            for rows in (slice(0, 8), slice(8, 16)):
                for cols in (slice(0, 128), slice(128, 256)):
                    result = relax([now[y, q, rows, cols] for q in range(Q)])
                    for q, value in enumerate(driven(*result, drive)):
                        moved[y, q, rows, cols] = value
            return carry

        lax.fori_loop(0, PLANES, collide, 0)
        whole = (slice(0, 16), slice(0, 256))
        part = whole if step == 0 else (slice(0, 8), slice(0, 128))
        for y in range(PLANES):
            for q in range(Q):
                cx, cy, cz = LATTICE[q]
                source = y - cy
                if source < 0:
                    arrived = moved[(y, OPPOSITE[q]) + part]
                elif source >= PLANES:
                    arrived = entry[(INCOMING.index(q),) + part]
                else:
                    arrived = rolled(moved[source, q], cz, cx)[part]
                    if source < 2:
                        hit = hits[(source, 3 * cz + cx + 4) + part]
                        arrived = jnp.where(hit > 0.5, moved[(y, OPPOSITE[q]) + part], arrived)
                if y < 2:
                    arrived = jnp.where(flags[(y,) + part] > 0.5, now[(y, q) + part], arrived)
                if step == 0:
                    now[y, q] = arrived
                else:
                    out[q, y] = arrived


def kernel_call(body, shapes, scratch, *operands):
    vmem = pl.BlockSpec(memory_space=pltpu.VMEM)
    return pl.pallas_call(
        body,
        in_specs=[vmem] * len(operands),
        out_specs=[vmem] * len(shapes),
        out_shape=[jax.ShapeDtypeStruct(shape, jnp.float32) for shape in shapes],
        scratch_shapes=[pltpu.VMEM(shape, jnp.float32) for shape in scratch],
        compiler_params=pltpu.CompilerParams(vmem_limit_bytes=48 * 1024 * 1024),
    )(*operands)


def neighbours(axis, low, high):
    count = lax.axis_size(axis)
    up = [(i, (i + 1) % count) for i in range(count)]
    down = [(target, source) for source, target in up]
    return lax.ppermute(high, axis, up), lax.ppermute(low, axis, down)


def local(populations, solid, top_inflow):
    along_x, along_z = lax.axis_size("gx"), lax.axis_size("gz")
    node_total = float(PLANES * 8 * 128 * along_x * along_z)
    fields = (populations, solid, top_inflow)
    (edges,) = kernel_call(pack_columns, [(TILES, 8, 128)], [], *fields)
    left, right = neighbours("gx", edges, edges)
    below, above, sides = kernel_call(
        pack_rows, [(ZROWS, 2, 128)] * 2 + [(TILES, 8, 128)], [], *fields, left, right
    )
    below, above = neighbours("gz", below, above)
    ring = [(TILES, 16, 128), (2, 16, 256)]
    halo = (sides, below, above)
    (sums,) = kernel_call(tally, [(along_x, 1, 128)], ring, *fields, *halo)
    sums = lax.all_to_all(sums, "gx", 0, 0, tiled=True)
    sums = jnp.broadcast_to(jnp.sum(sums, axis=0, keepdims=True), (along_z, 1, 128))
    sums = lax.all_to_all(sums, "gz", 0, 0, tiled=True)
    state = [(PLANES, Q, 16, 256)] * 2
    (advanced,) = kernel_call(
        lambda *refs: advance(node_total, *refs),
        [(Q, PLANES, 8, 128)],
        ring + [(len(INCOMING), 16, 256), (2, 9, 16, 256)] + state,
        *fields,
        *halo,
        sums,
    )
    return advanced


def solution(mesh):
    placed = (P(None, None, "gz", "gx"), P(None, "gz", "gx"), P(None, "gz", "gx"))
    return jax.shard_map(
        local, mesh=mesh, in_specs=placed, out_specs=P(None, None, "gz", "gx"), check_vma=False
    )
```

time: 201 us -> 80.2 us (0.40)
  the two profiles are of different devices: /device:TPU:2 before, /device:TPU:1 now
where the time goes in v1:
time: 80.2 us; the launch traced here: 79.7 us
  blocking collectives  37.3 us (47%)
  starting transfers between devices  28.2 us (35%)
  waiting for transfers between devices  6.24 us (8%)
  Pallas kernels  5.29 us (7%)
  local copies, waits for them, and re-layouts  2.59 us (3%)
    ppermute x4, starting transfers between devices, neighbours(): return (lax.ppermute(high, axis, up), lax.ppermute(low, axis, down))  28.2 us
    all_to_all x1, blocking collectives, local(): sums = lax.all_to_all(sums, 'gz', 0, 0, tiled=True)  20.4 us
    all_to_all x1, blocking collectives, local(): sums = lax.all_to_all(sums, 'gx', 0, 0, tiled=True)  16.8 us
    ppermute x4, waiting for transfers between devices, neighbours(): return (lax.ppermute(high, axis, up), lax.ppermute(low, axis, down))  6.24 us
    pallas_call x4, Pallas kernels, kernel_call(): pl.pallas_call(body, in_specs=[vmem] * len(operands), out_specs=[vmem] *...  5.29 us
    unnamed x12, local copies, waits for them, and re-layouts  2.58 us
  transfers between devices with their start and end apart: 4, of which 3 were waited for; matrix products, arithmetic and copies ran while one was open for 0% of the time, Pallas kernels for 0%

profile of v1, /device:TPU:1, one launch (start us, length us, event | category | flops | bytes accessed | tf_op | source)
XLA Modules:
  0.0 79.7 jit_solution(7635923269224888054)
XLA Ops:
  0.0 0.0 copy-start
  0.0 1.1 %copy-done = f32[19,8,8,128]{3,2,1,0:T(8,128)S(1)} copy-done((f32[19,8,8,128]{3,2,1,0:T(8,128)S(1)}, f32[19,8,8,128]{3,2,1,0:T(8,128)}, u32[]{:S(2)}) %copy-start) | copy-done | bytes 622616
  1.1 0.0 copy-start.2
  1.1 0.8 copy-done.2
  1.8 0.0 copy-start.4
  1.8 0.7 copy-done.4
  2.6 0.2 shard_map.37
  2.8 16.0 %collective-permute-start.1 = (f32[5,8,128]{2,1,0:T(8,128)S(1)}, f32[5,8,128]{2,1,0:T(8,128)S(1)}, u32[]{:S(2)}, u32[]{:S(2)}) collective-permute-start(f32[5,8,128]{2,1,0:T(8,128)S(1)} %shard_map.37), channel_id=1, source_target_pairs={{32,0},{64,32},{96,64},{128,96},{160,128},{192,160},{224,192},{256... | collective-permute-start | bytes 61448 | tf_op jit(solution)/shard_map/ppermute | solution.py:318
  18.8 1.9 %collective-permute-start = (f32[5,8,128]{2,1,0:T(8,128)S(1)}, f32[5,8,128]{2,1,0:T(8,128)S(1)}, u32[]{:S(2)}, u32[]{:S(2)}) collective-permute-start(f32[5,8,128]{2,1,0:T(8,128)S(1)} %shard_map.37), channel_id=1, source_target_pairs={{0,32},{32,64},{64,96},{96,128},{128,160},{160,192},{192,224},{224... | collective-permute-start | bytes 61448 | tf_op jit(solution)/shard_map/ppermute | solution.py:318
  20.7 0.0 collective-permute-done.1.right
  20.8 3.8 %collective-permute-done.left = f32[5,8,128]{2,1,0:T(8,128)S(1)} collective-permute-done((f32[5,8,128]{2,1,0:T(8,128)S(1)}, f32[5,8,128]{2,1,0:T(8,128)S(1)}, u32[]{:S(2)}, u32[]{:S(2)}) %collective-permute-start) | collective-permute-done | bytes 20512 | tf_op jit(solution)/shard_map/ppermute | solution.py:318
  24.6 0.1 shard_map.38
  24.6 0.0 copy-start.1
  24.7 3.5 %collective-permute-start.2 = (f32[164,2,128]{2,1,0:T(2,128)S(1)}, f32[164,2,128]{2,1,0:T(2,128)S(1)}, u32[]{:S(2)}, u32[]{:S(2)}) collective-permute-start(f32[164,2,128]{2,1,0:T(2,128)S(1)} %get-tuple-element.9), channel_id=1, source_target_pairs={{0,1},{1,2},{2,3},{3,4},{4,5},{5,6},{6,7},{7,8},{8,9},{9,10},{10,1... | collective-permute-start | bytes 503816 | tf_op jit(solution)/shard_map/ppermute | solution.py:318
  28.1 6.8 %collective-permute-start.3 = (f32[164,2,128]{2,1,0:T(2,128)S(1)}, f32[164,2,128]{2,1,0:T(2,128)S(1)}, u32[]{:S(2)}, u32[]{:S(2)}) collective-permute-start(f32[164,2,128]{2,1,0:T(2,128)S(1)} %get-tuple-element.10), channel_id=1, source_target_pairs={{1,0},{2,1},{3,2},{4,3},{5,4},{6,5},{7,6},{8,7},{9,8},{10,9},{11,1... | collective-permute-start | bytes 503816 | tf_op jit(solution)/shard_map/ppermute | solution.py:318
  34.9 0.8 %collective-permute-done.2.below.refs_4_ = f32[164,2,128]{2,1,0:T(2,128)S(1)} collective-permute-done((f32[164,2,128]{2,1,0:T(2,128)S(1)}, f32[164,2,128]{2,1,0:T(2,128)S(1)}, u32[]{:S(2)}, u32[]{:S(2)}) %collective-permute-start.2) | collective-permute-done | bytes 167968 | tf_op jit(solution)/shard_map/ppermute | solution.py:318
  35.7 1.6 %collective-permute-done.3.above.refs_5_ = f32[164,2,128]{2,1,0:T(2,128)S(1)} collective-permute-done((f32[164,2,128]{2,1,0:T(2,128)S(1)}, f32[164,2,128]{2,1,0:T(2,128)S(1)}, u32[]{:S(2)}, u32[]{:S(2)}) %collective-permute-start.3) | collective-permute-done | bytes 167968 | tf_op jit(solution)/shard_map/ppermute | solution.py:318
  37.3 0.3 shard_map.39
  37.6 16.8 %all_to_all.10 = f32[32,1,128]{2,1,0:T(1,128)S(1)} all-to-all(f32[32,1,128]{2,1,0:T(1,128)S(1)} %shard_map.39), channel_id=1, replica_groups=mesh['gx'=32,'gz'=32] {'gx'}, dimensions={0} | all-to-all | bytes 32768 | tf_op jit(solution)/shard_map/all_to_all | solution.py:334
  54.4 0.0 copy-start.3
  54.4 0.1 reduce_sum.9
  54.5 0.0 copy-start.5
  54.5 20.4 %all_to_all.11.refs_6_ = f32[32,1,128]{2,1,0:T(1,128)S(1)} all-to-all(f32[32,1,128]{2,1,0:T(1,128)S(1)} %broadcast_in_dim.2), channel_id=1, replica_groups=mesh['gx'=32,'gz'=32] {'gz'}, dimensions={0} | all-to-all | bytes 32768 | tf_op jit(solution)/shard_map/all_to_all | solution.py:336
  75.0 0.0 copy-done.1
  75.0 0.0 copy-done.3
  75.0 0.0 copy-done.5
  75.0 4.7 %shard_map.40 = f32[19,8,8,128]{3,2,1,0:T(8,128)} custom-call(f32[19,8,8,128]{3,2,1,0:T(8,128)S(1)} %copy-done.1, s32[8,8,128]{2,1,0:T(8,128)S(1)} %copy-done.3, f32[5,8,128]{2,1,0:T(8,128)S(1)} %copy-done.5, f32[5,8,128]{2,1,0:T(8,128)S(1)} %get-tuple-element.8.sides.refs_3_, f32[164,2,128]{2,1,0:T(2,128)S(1)} %collective-permute-done.2.below.refs_4_, ...), custom_call_target="tpu_custom_call" | custom-call | tf_op jit(solution)/shard_map/pallas_call | solution.py:304
  (1 shorter events, 0.0 us)
Async XLA Ops:
  0.0 1.1 %copy-start = (f32[19,8,8,128]{3,2,1,0:T(8,128)S(1)}, f32[19,8,8,128]{3,2,1,0:T(8,128)}, u32[]{:S(2)}) copy-start(f32[19,8,8,128]{3,2,1,0:T(8,128)} %refs_0_.1) | copy-start | bytes 1867780
  1.1 0.8 copy-start.2
  1.8 0.7 copy-start.4
  2.8 18.0 %collective-permute-start.1 = (f32[5,8,128]{2,1,0:T(8,128)S(1)}, f32[5,8,128]{2,1,0:T(8,128)S(1)}, u32[]{:S(2)}, u32[]{:S(2)}) collective-permute-start(f32[5,8,128]{2,1,0:T(8,128)S(1)} %shard_map.37), channel_id=1, source_target_pairs={{32,0},{64,32},{96,64},{128,96},{160,128},{192,160},{224,192},{256... | collective-permute-start | bytes 61448 | tf_op jit(solution)/shard_map/ppermute | solution.py:318
  18.8 5.7 %collective-permute-start = (f32[5,8,128]{2,1,0:T(8,128)S(1)}, f32[5,8,128]{2,1,0:T(8,128)S(1)}, u32[]{:S(2)}, u32[]{:S(2)}) collective-permute-start(f32[5,8,128]{2,1,0:T(8,128)S(1)} %shard_map.37), channel_id=1, source_target_pairs={{0,32},{32,64},{64,96},{96,128},{128,160},{160,192},{192,224},{224... | collective-permute-start | bytes 61448 | tf_op jit(solution)/shard_map/ppermute | solution.py:318
  24.6 50.3 %copy-start.1 = (f32[19,8,8,128]{3,2,1,0:T(8,128)S(1)}, f32[19,8,8,128]{3,2,1,0:T(8,128)}, u32[]{:S(2)}) copy-start(f32[19,8,8,128]{3,2,1,0:T(8,128)} %refs_0_.1) | copy-start | bytes 1867780
  24.7 11.0 %collective-permute-start.2 = (f32[164,2,128]{2,1,0:T(2,128)S(1)}, f32[164,2,128]{2,1,0:T(2,128)S(1)}, u32[]{:S(2)}, u32[]{:S(2)}) collective-permute-start(f32[164,2,128]{2,1,0:T(2,128)S(1)} %get-tuple-element.9), channel_id=1, source_target_pairs={{0,1},{1,2},{2,3},{3,4},{4,5},{5,6},{6,7},{7,8},{8,9},{9,10},{10,1... | collective-permute-start | bytes 503816 | tf_op jit(solution)/shard_map/ppermute | solution.py:318
  28.1 9.2 %collective-permute-start.3 = (f32[164,2,128]{2,1,0:T(2,128)S(1)}, f32[164,2,128]{2,1,0:T(2,128)S(1)}, u32[]{:S(2)}, u32[]{:S(2)}) collective-permute-start(f32[164,2,128]{2,1,0:T(2,128)S(1)} %get-tuple-element.10), channel_id=1, source_target_pairs={{1,0},{2,1},{3,2},{4,3},{5,4},{6,5},{7,6},{8,7},{9,8},{10,9},{11,1... | collective-permute-start | bytes 503816 | tf_op jit(solution)/shard_map/ppermute | solution.py:318
  54.4 20.5 %copy-start.3 = (s32[8,8,128]{2,1,0:T(8,128)S(1)}, s32[8,8,128]{2,1,0:T(8,128)}, u32[]{:S(2)}) copy-start(s32[8,8,128]{2,1,0:T(8,128)} %refs_1_.1) | copy-start | bytes 98308
  54.5 20.5 %copy-start.5 = (f32[5,8,128]{2,1,0:T(8,128)S(1)}, f32[5,8,128]{2,1,0:T(8,128)}, u32[]{:S(2)}) copy-start(f32[5,8,128]{2,1,0:T(8,128)} %refs_2_.1) | copy-start | bytes 61444

commit v2 on v1

--- a/solution.py
+++ b/solution.py
@@ -39,7 +39,8 @@
 INFLOW_SLOT = FLAG_SLOT + 2
 SLOTS = INFLOW_SLOT + len(INCOMING)
 TILES = 5
-ZROWS = SLOTS + TILES
+GROUP = 24
+SUMS_LANE = 10 * GROUP
 
 
 def relax(f):
@@ -155,54 +156,49 @@
     return values
 
 
-def pack_columns(pops, solid, inflow, edges):
-    lane = lax.broadcasted_iota(jnp.int32, (8, 128), 1)
-    values = slot_values(pops, solid, inflow)
-    for tile in range(TILES):
-        first = jnp.zeros((8, 128), jnp.float32)
-        for slot in range(32):
-            if tile * 32 + slot < SLOTS:
-                offset = 4 * slot
-                moved = rolled(values[tile * 32 + slot](), 0, offset)
-                place = ((lane + (128 - offset + 2)) & 127) < 4
-                first = jnp.where(place, moved, first)
-        edges[tile] = first
-
-
-def pack_rows(pops, solid, inflow, left, right, below, above, sides):
-    lane = lax.broadcasted_iota(jnp.int32, (8, 128), 1)
+def pack_rows(pops_hbm, solid_hbm, inflow_hbm, below, above, pops, solid, inflow, done):
+    copies = [
+        pltpu.make_async_copy(source, target, done.at[i])
+        for i, (source, target) in enumerate(((pops_hbm, pops), (solid_hbm, solid), (inflow_hbm, inflow)))
+    ]
+    for copy in copies:
+        copy.start()
+    for copy in copies:
+        copy.wait()
     for index, value in enumerate(slot_values(pops, solid, inflow)):
         tile = value()
         below[index] = tile[0:2]
         above[index] = tile[6:8]
+
+
+def lay_rows(target, main, slot, below, above):
+    target[0:8] = main
+    target[8:10] = above[slot]
+    target[14:16] = below[slot]
+
+
+def pack_columns(pops, solid, inflow, below, above, edges, rows):
+    lane = lax.broadcasted_iota(jnp.int32, (16, 128), 1)
+    values = slot_values(pops, solid, inflow)
+    rows[8:16] = jnp.zeros((8, 128), jnp.float32)
     for tile in range(TILES):
-        both = jnp.where((lane & 3) < 2, right[tile], left[tile])
-        sides[tile] = both
-        below[SLOTS + tile] = both[0:2]
-        above[SLOTS + tile] = both[6:8]
-
-
-def lay_sides(sides, below, above, ring):
-    for tile in range(TILES):
-        ring[tile, 0:8] = sides[tile]
-        ring[tile, 8:10] = above[SLOTS + tile]
-        ring[tile, 14:16] = below[SLOTS + tile]
-
-
-def lay_out(target, main, slot, ring, below, above):
-    target[0:8, 0:128] = main
-    target[8:10, 0:128] = above[slot]
-    target[14:16, 0:128] = below[slot]
-    target[:, 128:256] = rolled(ring[slot // 32], 0, -4 * (slot % 32))
-
-
-def tally(pops, solid, inflow, sides, below, above, out, ring, flags):
-    lay_sides(sides, below, above, ring)
+        packed = jnp.zeros((16, 128), jnp.float32)
+        for slot in range(tile * 32, min(tile * 32 + 32, SLOTS)):
+            offset = 4 * (slot % 32)
+            lay_rows(rows, values[slot](), slot, below, above)
+            place = ((lane + (128 - offset + 2)) & 127) < 4
+            packed = jnp.where(place, rolled(rows[...], 0, offset), packed)
+        edges[tile] = packed
+
+
+def tally(pops, solid, inflow, below, above, out, flags, weights):
+    lane = lax.broadcasted_iota(jnp.int32, (8, 128), 1)
+    flags[...] = jnp.zeros(flags.shape, jnp.float32)
+    weights[...] = jnp.zeros(weights.shape, jnp.float32)
     for y in range(2):
-        lay_out(flags.at[y], solid[y].astype(jnp.float32), FLAG_SLOT + y, ring, below, above)
+        lay_rows(flags.at[y], solid[y].astype(jnp.float32), FLAG_SLOT + y, below, above)
+    fluid = [1.0 - flags[y, 0:8] for y in range(2)]
     flow = jnp.zeros((8, 128), jnp.float32)
-    count = jnp.full((8, 128), float(PLANES - 2), jnp.float32)
-    fluid = [1.0 - flags[y, 0:8, 0:128] for y in range(2)]
     for y in range(PLANES):
         f = pops
         jx = (
@@ -213,9 +209,10 @@
             + (f[13, y] - f[14, y])
         )
         flow = flow + (jx * fluid[y] if y < 2 else jx)
-    count = count + fluid[0] + fluid[1]
     one = flow
+    count = float(PLANES - 2) + fluid[0] + fluid[1]
     two = jnp.zeros((8, 128), jnp.float32)
+    nothing = jnp.zeros((8, 128), jnp.float32)
     for y in (0, 1, 2, PLANES - 1):
         relaxed, velocity, inv = relax([pops[q, y] for q in range(Q)])
         for index in range(Q):
@@ -224,60 +221,112 @@
             if not cx or 1 < target < PLANES:
                 continue
             linear, square = push_parts(index, velocity, inv)
-            if target >= PLANES:
-                factor = -float(cx)
-            elif target < 0:
-                factor = (-2.0 * cx) * fluid[y]
-            else:
-                hit = rolled(flags[target], -cz, -cx)[0:8, 0:128]
-                factor = (-2.0 * cx) * hit
-                if y < 2:
-                    factor = factor * fluid[y]
-            one = one + factor * relaxed[index]
-            count = count + factor * linear
-            two = two + factor * square
+            factor = -float(cx) if target >= PLANES else -2.0 * cx
+            parts = [relaxed[index] * factor, linear * factor, square * factor]
+            if y < 2:
+                parts = [part * fluid[y] for part in parts]
+            if 0 <= target < PLANES:
+                beyond = 0 if cx > 0 else 6
+                for i, part in enumerate(parts):
+                    wide = jnp.concatenate([part, nothing], axis=0)
+                    place = beyond + 3 * target + i
+                    weights[place] = weights[place] + rolled(wide, cz, 0)
+                hit = rolled(flags[target], -cz, -cx)[0:8]
+                hit = jnp.where(lane == (127 if cx > 0 else 0), 0.0, hit)
+                parts = [part * hit for part in parts]
+            one, count, two = one + parts[0], count + parts[1], two + parts[2]
     one = one + (inflow[INCOMING.index(9)] - inflow[INCOMING.index(8)])
+
+    lanes = lax.broadcasted_iota(jnp.int32, (16, 128), 1)
+    table = jnp.zeros((16, 128), jnp.float32)
+    for place in range(12):
+        source = 127 if place < 6 else 0
+        table = jnp.where(lanes == place, rolled(weights[place], 0, place - source), table)
+    for y in range(2):
+        for i in range(3):
+            place = 12 + 3 * y + i
+            table = jnp.where(lanes == place, rolled(flags[y], 0, place), table)
+            table = jnp.where(lanes == place + 6, rolled(flags[y], 0, place + 6 - 127), table)
+    table = jnp.concatenate([table, jnp.zeros((16, 128), jnp.float32)], axis=1)
+    packed = jnp.zeros((1, 256), jnp.float32)
+    for k in range(10):
+        row = k if k < 9 else 15
+        packed = packed + rolled(table, -row, GROUP * k)[0:1]
+    wide = lax.broadcasted_iota(jnp.int32, (1, 256), 1)
+    for i, part in enumerate((flow, one, count, two)):
+        total = jnp.sum(jnp.sum(part, axis=0, keepdims=True), axis=1, keepdims=True)
+        packed = jnp.where(wide == SUMS_LANE + i, total, packed)
+    out[...] = jnp.broadcast_to(packed[None], out.shape)
+
+
+def cross(messages, out):
+    table = messages[...]
+    count = table.shape[0]
+    place = lax.broadcasted_iota(jnp.int32, table.shape, 1)
+    within = lax.rem(place, GROUP)
+    following = jnp.where(within < 18, pltpu.roll(table, count - 1, 0), pltpu.roll(table, 1, 0))
+    matched = jnp.where((within < 12) & (place < SUMS_LANE), table * rolled(following, 0, -12), 0.0)
+    matched = jnp.sum(matched, axis=0, keepdims=True)
+    sums = jnp.sum(table, axis=0, keepdims=True)
+    place, within = place[0:1], within[0:1]
     lane = lax.broadcasted_iota(jnp.int32, (1, 128), 1)
     packed = jnp.zeros((1, 128), jnp.float32)
-    for place, part in enumerate((flow, one, count, two)):
-        total = jnp.sum(jnp.sum(part, axis=0, keepdims=True), axis=1, keepdims=True)
-        packed = jnp.where(lane == place, total, packed)
+    for i in range(4):
+        part = jnp.where(place == SUMS_LANE + i, sums, 0.0)
+        if i:
+            part = part + jnp.where(lax.rem(within, 3) == i - 1, matched, 0.0)
+        packed = jnp.where(lane == i, jnp.sum(part, axis=1, keepdims=True), packed)
     out[...] = jnp.broadcast_to(packed[None], out.shape)
 
 
-def advance(node_total, pops, solid, inflow, sides, below, above, sums, out, ring, flags, entry, hits, now, moved):
+QUARTERS = tuple(
+    (rows, cols)
+    for rows in (slice(0, 8), slice(8, 16))
+    for cols in (slice(0, 128), slice(128, 256))
+)
+MAIN = (slice(0, 8), slice(0, 128))
+
+
+def advance(
+    node_total, pops, solid, inflow, below, above, left, right, sums, out, flags, entry, hits, now, moved, edges
+):
     total = jnp.sum(sums[...], axis=0)
     flow, one, count, two = (total[:, i : i + 1] for i in range(4))
     first = BASE_DRIVE + DRIVE_GAIN * (TARGET_FLOW - flow / node_total)
     later = (one + count * first + two * (first * first)) / node_total
     second = BASE_DRIVE + DRIVE_GAIN * (TARGET_FLOW - later)
 
-    lay_sides(sides, below, above, ring)
+    lane = lax.broadcasted_iota(jnp.int32, (16, 128), 1)
+    for tile in range(TILES):
+        edges[tile] = jnp.where((lane & 3) < 2, right[tile], left[tile])
+
+    def lay_out(target, main, slot):
+        lay_rows(target.at[:, 0:128], main, slot, below, above)
+        target[:, 128:256] = rolled(edges[slot // 32], 0, -4 * (slot % 32))
+
     for y in range(2):
-        lay_out(flags.at[y], solid[y].astype(jnp.float32), FLAG_SLOT + y, ring, below, above)
+        lay_out(flags.at[y], solid[y].astype(jnp.float32), FLAG_SLOT + y)
         for step_z in (-1, 0, 1):
             for step_x in (-1, 0, 1):
                 hits[y, 3 * step_z + step_x + 4] = rolled(flags[y], step_z, step_x)
     for i in range(len(INCOMING)):
-        lay_out(entry.at[i], inflow[i], INFLOW_SLOT + i, ring, below, above)
+        lay_out(entry.at[i], inflow[i], INFLOW_SLOT + i)
     for y in range(PLANES):
         for q in range(Q):
-            lay_out(now.at[y, q], pops[q, y], q * PLANES + y, ring, below, above)
+            lay_out(now.at[y, q], pops[q, y], q * PLANES + y)
 
     for step in range(2):
         drive = jnp.broadcast_to(first if step == 0 else second, (8, 128))
 
         def collide(y, carry):
-            for rows in (slice(0, 8), slice(8, 16)):
-                for cols in (slice(0, 128), slice(128, 256)):
-                    result = relax([now[y, q, rows, cols] for q in range(Q)])
-                    for q, value in enumerate(driven(*result, drive)):
-                        moved[y, q, rows, cols] = value
+            for rows, cols in QUARTERS:
+                result = relax([now[y, q, rows, cols] for q in range(Q)])
+                for q, value in enumerate(driven(*result, drive)):
+                    moved[y, q, rows, cols] = value
             return carry
 
         lax.fori_loop(0, PLANES, collide, 0)
-        whole = (slice(0, 16), slice(0, 256))
-        part = whole if step == 0 else (slice(0, 8), slice(0, 128))
+        part = (slice(0, 16), slice(0, 256)) if step == 0 else MAIN
         for y in range(PLANES):
             for q in range(Q):
                 cx, cy, cz = LATTICE[q]
@@ -299,15 +348,17 @@
                     out[q, y] = arrived
 
 
-def kernel_call(body, shapes, scratch, *operands):
+def kernel_call(body, shapes, scratch, *operands, memory=pltpu.VMEM):
     vmem = pl.BlockSpec(memory_space=pltpu.VMEM)
     return pl.pallas_call(
         body,
-        in_specs=[vmem] * len(operands),
+        in_specs=[pl.BlockSpec(memory_space=memory)] * len(operands),
         out_specs=[vmem] * len(shapes),
-        out_shape=[jax.ShapeDtypeStruct(shape, jnp.float32) for shape in shapes],
-        scratch_shapes=[pltpu.VMEM(shape, jnp.float32) for shape in scratch],
-        compiler_params=pltpu.CompilerParams(vmem_limit_bytes=48 * 1024 * 1024),
+        out_shape=[pltpu.VMEM(item, jnp.float32) if isinstance(item, tuple) else item for item in shapes],
+        scratch_shapes=[
+            pltpu.VMEM(item, jnp.float32) if isinstance(item, tuple) else item for item in scratch
+        ],
+        compiler_params=pltpu.CompilerParams(vmem_limit_bytes=20 * 1024 * 1024),
     )(*operands)
 
 
@@ -322,25 +373,36 @@
     along_x, along_z = lax.axis_size("gx"), lax.axis_size("gz")
     node_total = float(PLANES * 8 * 128 * along_x * along_z)
     fields = (populations, solid, top_inflow)
-    (edges,) = kernel_call(pack_columns, [(TILES, 8, 128)], [], *fields)
+    below, above, *fields = kernel_call(
+        pack_rows,
+        [(SLOTS, 2, 128)] * 2 + [pltpu.VMEM(field.shape, field.dtype) for field in fields],
+        [pltpu.SemaphoreType.DMA((3,))],
+        *(pltpu.with_memory_space_constraint(field, pltpu.HBM) for field in fields),
+        memory=pltpu.HBM,
+    )
+    halo = neighbours("gz", below, above)
+    (sums,) = kernel_call(tally, [(along_x, 1, 256)], [(2, 16, 128), (12, 16, 128)], *fields, *halo)
+    sums = lax.all_to_all(sums, "gx", 0, 0, tiled=True)
+    (edges,) = kernel_call(pack_columns, [(TILES, 16, 128)], [(16, 128)], *fields, *halo)
     left, right = neighbours("gx", edges, edges)
-    below, above, sides = kernel_call(
-        pack_rows, [(ZROWS, 2, 128)] * 2 + [(TILES, 8, 128)], [], *fields, left, right
-    )
-    below, above = neighbours("gz", below, above)
-    ring = [(TILES, 16, 128), (2, 16, 256)]
-    halo = (sides, below, above)
-    (sums,) = kernel_call(tally, [(along_x, 1, 128)], ring, *fields, *halo)
-    sums = lax.all_to_all(sums, "gx", 0, 0, tiled=True)
-    sums = jnp.broadcast_to(jnp.sum(sums, axis=0, keepdims=True), (along_z, 1, 128))
+    (sums,) = kernel_call(cross, [(along_z, 1, 128)], [], sums.reshape(along_x, 256))
     sums = lax.all_to_all(sums, "gz", 0, 0, tiled=True)
-    state = [(PLANES, Q, 16, 256)] * 2
+    lattice = (PLANES, Q, 16, 256)
     (advanced,) = kernel_call(
         lambda *refs: advance(node_total, *refs),
-        [(Q, PLANES, 8, 128)],
-        ring + [(len(INCOMING), 16, 256), (2, 9, 16, 256)] + state,
+        [jax.ShapeDtypeStruct((Q, PLANES, 8, 128), jnp.float32)],
+        [
+            (2, 16, 256),
+            (len(INCOMING), 16, 256),
+            (2, 9, 16, 256),
+            lattice,
+            lattice,
+            (TILES, 16, 128),
+        ],
         *fields,
         *halo,
+        left,
+        right,
         sums,
     )
     return advanced

time: 80.2 us -> 72.2 us (0.900)
  blocking collectives: 37.3 us -> 0 us
  starting transfers between devices: 28.2 us -> 45 us
  waiting for transfers between devices: 6.24 us -> 18.3 us
  Pallas kernels: 5.29 us -> 8.56 us
  local copies, waits for them, and re-layouts: 2.59 us -> 0.01 us
    all_to_all x2 -> x0, blocking collectives: 37.3 us -> none  [the longest x1 20.4 us: local(): sums = lax.all_to_all(sums, 'gz', 0, 0, tiled=True)]
    all_to_all x0 -> x2, starting transfers between devices: none -> 27.6 us  [the longest x1 19 us: local(): sums = lax.all_to_all(sums, 'gx', 0, 0, tiled=True)]
    all_to_all x0 -> x2, waiting for transfers between devices: none -> 12.5 us  [the longest x1 11 us: local(): sums = lax.all_to_all(sums, 'gz', 0, 0, tiled=True)]
    ppermute x4, starting transfers between devices: 28.2 us -> 17.4 us  [neighbours(): return (lax.ppermute(high, axis, up), lax.ppermute(low, axis, down))]
    pallas_call x4 -> x5, Pallas kernels: 5.29 us -> 8.56 us  [kernel_call(): pl.pallas_call(body, in_specs=[pl.BlockSpec(memory_space=memory)] * len(o...]
    unnamed x12 -> x1, local copies, waits for them, and re-layouts: 2.58 us -> 0.01 us
  transfers between devices with their start and end apart: 4 -> 6, of which waited for: 3 -> 4; matrix products, arithmetic and copies ran while one was open for 0% -> 0% of each run, Pallas kernels for 0% -> 2%
where the time goes in v2:
time: 72.2 us; the launch traced here: 71.8 us
  starting transfers between devices  45 us (62%)
  waiting for transfers between devices  18.3 us (25%)
  Pallas kernels  8.56 us (12%)
    all_to_all x1, starting transfers between devices, local(): sums = lax.all_to_all(sums, 'gx', 0, 0, tiled=True)  19 us
    ppermute x4, starting transfers between devices, neighbours(): return (lax.ppermute(high, axis, up), lax.ppermute(low, axis, down))  17.4 us
    all_to_all x1, waiting for transfers between devices, local(): sums = lax.all_to_all(sums, 'gz', 0, 0, tiled=True)  11 us
    all_to_all x1, starting transfers between devices, local(): sums = lax.all_to_all(sums, 'gz', 0, 0, tiled=True)  8.62 us
    pallas_call x5, Pallas kernels, kernel_call(): pl.pallas_call(body, in_specs=[pl.BlockSpec(memory_space=memory)] * len(o...  8.56 us
    ppermute x4, waiting for transfers between devices, neighbours(): return (lax.ppermute(high, axis, up), lax.ppermute(low, axis, down))  5.72 us
    all_to_all x1, waiting for transfers between devices, local(): sums = lax.all_to_all(sums, 'gx', 0, 0, tiled=True)  1.56 us
  transfers between devices with their start and end apart: 6, of which 4 were waited for; matrix products, arithmetic and copies ran while one was open for 0% of the time, Pallas kernels for 2%

profile of v2, /device:TPU:1, one launch (start us, length us, event | category | flops | bytes accessed | tf_op | source)
XLA Modules:
  0.0 71.8 jit_solution(6798494870490062228)
XLA Ops:
  0.0 1.2 %shard_map.37 = (f32[159,2,128]{2,1,0:T(2,128)S(1)}, f32[159,2,128]{2,1,0:T(2,128)S(1)}, f32[19,8,8,128]{3,2,1,0:T(8,128)S(1)}, s32[8,8,128]{2,1,0:T(8,128)S(1)}, f32[5,8,128]{2,1,0:T(8,128)S(1)}) custom-call(f32[19,8,8,128]{3,2,1,0:T(8,128)} %pops_hbm.1, s32[8,8,128]{2,1,0:T(8,128)} %solid_hbm.1, f32[5,8,128]{2,1,0:T(8,128)} %inflow_hbm.1), custom_call_target="tpu_custom_call" | custom-call | tf_op jit(solution)/shard_map/pallas_call | solution.py:353
  1.2 4.1 %collective-permute-start = (f32[159,2,128]{2,1,0:T(2,128)S(1)}, f32[159,2,128]{2,1,0:T(2,128)S(1)}, u32[]{:S(2)}, u32[]{:S(2)}) collective-permute-start(f32[159,2,128]{2,1,0:T(2,128)S(1)} %get-tuple-element.13), channel_id=1, source_target_pairs={{0,1},{1,2},{2,3},{3,4},{4,5},{5,6},{6,7},{7,8},{8,9},{9,10},{10,1... | collective-permute-start | bytes 488456 | tf_op jit(solution)/shard_map/ppermute | solution.py:369
  5.3 7.7 %collective-permute-start.1 = (f32[159,2,128]{2,1,0:T(2,128)S(1)}, f32[159,2,128]{2,1,0:T(2,128)S(1)}, u32[]{:S(2)}, u32[]{:S(2)}) collective-permute-start(f32[159,2,128]{2,1,0:T(2,128)S(1)} %get-tuple-element.14), channel_id=1, source_target_pairs={{1,0},{2,1},{3,2},{4,3},{5,4},{6,5},{7,6},{8,7},{9,8},{10,9},{11,1... | collective-permute-start | bytes 488456 | tf_op jit(solution)/shard_map/ppermute | solution.py:369
  13.0 1.7 %collective-permute-done.below.refs_3_ = f32[159,2,128]{2,1,0:T(2,128)S(1)} collective-permute-done((f32[159,2,128]{2,1,0:T(2,128)S(1)}, f32[159,2,128]{2,1,0:T(2,128)S(1)}, u32[]{:S(2)}, u32[]{:S(2)}) %collective-permute-start) | collective-permute-done | bytes 162848 | tf_op jit(solution)/shard_map/ppermute | solution.py:369
  14.7 4.0 %collective-permute-done.1.above.refs_4_ = f32[159,2,128]{2,1,0:T(2,128)S(1)} collective-permute-done((f32[159,2,128]{2,1,0:T(2,128)S(1)}, f32[159,2,128]{2,1,0:T(2,128)S(1)}, u32[]{:S(2)}, u32[]{:S(2)}) %collective-permute-start.1) | collective-permute-done | bytes 162848 | tf_op jit(solution)/shard_map/ppermute | solution.py:369
  18.7 0.9 %shard_map.39 = f32[32,1,256]{2,1,0:T(1,128)} custom-call(f32[19,8,8,128]{3,2,1,0:T(8,128)S(1)} %get-tuple-element.10.pops.refs_0_, s32[8,8,128]{2,1,0:T(8,128)S(1)} %get-tuple-element.11.solid.refs_1_, f32[5,8,128]{2,1,0:T(8,128)S(1)} %get-tuple-element.12.inflow.refs_2_, f32[159,2,128]{2,1,0:T(2,128)S(1)} %collective-permute-done.below.refs_3_, ...), custom_call_target="tpu_custom_call" | custom-call | tf_op jit(solution)/shard_map/pallas_call | solution.py:353
  19.7 19.0 %all-to-all-start = ((f32[32,1,256]{2,1,0:T(1,128)}), f32[32,1,256]{2,1,0:T(1,128)S(1)}, u32[]{:S(2)}, u32[]{:S(2)}) async-start(f32[32,1,256]{2,1,0:T(1,128)} %shard_map.39), calls=%async_computation | async-start | bytes 65536 | tf_op jit(solution)/shard_map/all_to_all | solution.py:385
  38.7 1.0 %shard_map.38 = f32[5,16,128]{2,1,0:T(8,128)S(1)} custom-call(f32[19,8,8,128]{3,2,1,0:T(8,128)S(1)} %get-tuple-element.10.pops.refs_0_, s32[8,8,128]{2,1,0:T(8,128)S(1)} %get-tuple-element.11.solid.refs_1_, f32[5,8,128]{2,1,0:T(8,128)S(1)} %get-tuple-element.12.inflow.refs_2_, f32[159,2,128]{2,1,0:T(2,128)S(1)} %collective-permute-done.below.refs_3_, ...), custom_call_target="tpu_custom_call" | custom-call | tf_op jit(solution)/shard_map/pallas_call | solution.py:353
  39.7 2.1 %collective-permute-start.3 = (f32[5,16,128]{2,1,0:T(8,128)S(1)}, f32[5,16,128]{2,1,0:T(8,128)S(1)}, u32[]{:S(2)}, u32[]{:S(2)}) collective-permute-start(f32[5,16,128]{2,1,0:T(8,128)S(1)} %shard_map.38), channel_id=1, source_target_pairs={{32,0},{64,32},{96,64},{128,96},{160,128},{192,160},{224,192},{256... | collective-permute-start | bytes 122888 | tf_op jit(solution)/shard_map/ppermute | solution.py:369
  41.8 3.4 %collective-permute-start.2 = (f32[5,16,128]{2,1,0:T(8,128)S(1)}, f32[5,16,128]{2,1,0:T(8,128)S(1)}, u32[]{:S(2)}, u32[]{:S(2)}) collective-permute-start(f32[5,16,128]{2,1,0:T(8,128)S(1)} %shard_map.38), channel_id=1, source_target_pairs={{0,32},{32,64},{64,96},{96,128},{128,160},{160,192},{192,224},{224... | collective-permute-start | bytes 122888 | tf_op jit(solution)/shard_map/ppermute | solution.py:369
  45.2 1.6 %all-to-all-done = f32[32,1,256]{2,1,0:T(1,128)S(1)} async-done(((f32[32,1,256]{2,1,0:T(1,128)}), f32[32,1,256]{2,1,0:T(1,128)S(1)}, u32[]{:S(2)}, u32[]{:S(2)}) %all-to-all-start) | async-done | bytes 32800 | tf_op jit(solution)/shard_map/all_to_all | solution.py:385
  46.8 0.8 %shard_map.40 = f32[32,1,128]{2,1,0:T(1,128)} custom-call(f32[32,256]{1,0:T(8,128)S(1)} %bitcast.3), custom_call_target="tpu_custom_call" | custom-call | tf_op jit(solution)/shard_map/pallas_call | solution.py:353
  47.6 8.6 %all-to-all-start.1 = ((f32[32,1,128]{2,1,0:T(1,128)}), f32[32,1,128]{2,1,0:T(1,128)S(1)}, u32[]{:S(2)}, u32[]{:S(2)}) async-start(f32[32,1,128]{2,1,0:T(1,128)} %shard_map.40), calls=%async_computation.1 | async-start | bytes 32768 | tf_op jit(solution)/shard_map/all_to_all | solution.py:389
  56.2 0.0 collective-permute-done.3.refs_6_
  56.2 0.0 collective-permute-done.2.refs_5_
  56.2 11.0 %all-to-all-done.1.refs_7_ = f32[32,1,128]{2,1,0:T(1,128)S(1)} async-done(((f32[32,1,128]{2,1,0:T(1,128)}), f32[32,1,128]{2,1,0:T(1,128)S(1)}, u32[]{:S(2)}, u32[]{:S(2)}) %all-to-all-start.1) | async-done | bytes 16416 | tf_op jit(solution)/shard_map/all_to_all | solution.py:389
  67.2 4.7 %shard_map.41 = f32[19,8,8,128]{3,2,1,0:T(8,128)} custom-call(f32[19,8,8,128]{3,2,1,0:T(8,128)S(1)} %get-tuple-element.10.pops.refs_0_, s32[8,8,128]{2,1,0:T(8,128)S(1)} %get-tuple-element.11.solid.refs_1_, f32[5,8,128]{2,1,0:T(8,128)S(1)} %get-tuple-element.12.inflow.refs_2_, f32[159,2,128]{2,1,0:T(2,128)S(1)} %collective-permute-done.below.refs_3_, ...), custom_call_target="tpu_custom_call" | custom-call | tf_op jit(solution)/shard_map/pallas_call | solution.py:353
  (1 shorter events, 0.0 us)
Async XLA Ops:
  1.2 13.6 %collective-permute-start = (f32[159,2,128]{2,1,0:T(2,128)S(1)}, f32[159,2,128]{2,1,0:T(2,128)S(1)}, u32[]{:S(2)}, u32[]{:S(2)}) collective-permute-start(f32[159,2,128]{2,1,0:T(2,128)S(1)} %get-tuple-element.13), channel_id=1, source_target_pairs={{0,1},{1,2},{2,3},{3,4},{4,5},{5,6},{6,7},{7,8},{8,9},{9,10},{10,1... | collective-permute-start | bytes 488456 | tf_op jit(solution)/shard_map/ppermute | solution.py:369
  5.3 13.4 %collective-permute-start.1 = (f32[159,2,128]{2,1,0:T(2,128)S(1)}, f32[159,2,128]{2,1,0:T(2,128)S(1)}, u32[]{:S(2)}, u32[]{:S(2)}) collective-permute-start(f32[159,2,128]{2,1,0:T(2,128)S(1)} %get-tuple-element.14), channel_id=1, source_target_pairs={{1,0},{2,1},{3,2},{4,3},{5,4},{6,5},{7,6},{8,7},{9,8},{10,9},{11,1... | collective-permute-start | bytes 488456 | tf_op jit(solution)/shard_map/ppermute | solution.py:369
  19.7 27.1 %all-to-all-start = ((f32[32,1,256]{2,1,0:T(1,128)}), f32[32,1,256]{2,1,0:T(1,128)S(1)}, u32[]{:S(2)}, u32[]{:S(2)}) async-start(f32[32,1,256]{2,1,0:T(1,128)} %shard_map.39), calls=%async_computation | async-start | bytes 65536 | tf_op jit(solution)/shard_map/all_to_all | solution.py:385
  39.7 16.5 %collective-permute-start.3 = (f32[5,16,128]{2,1,0:T(8,128)S(1)}, f32[5,16,128]{2,1,0:T(8,128)S(1)}, u32[]{:S(2)}, u32[]{:S(2)}) collective-permute-start(f32[5,16,128]{2,1,0:T(8,128)S(1)} %shard_map.38), channel_id=1, source_target_pairs={{32,0},{64,32},{96,64},{128,96},{160,128},{192,160},{224,192},{256... | collective-permute-start | bytes 122888 | tf_op jit(solution)/shard_map/ppermute | solution.py:369
  41.8 14.4 %collective-permute-start.2 = (f32[5,16,128]{2,1,0:T(8,128)S(1)}, f32[5,16,128]{2,1,0:T(8,128)S(1)}, u32[]{:S(2)}, u32[]{:S(2)}) collective-permute-start(f32[5,16,128]{2,1,0:T(8,128)S(1)} %shard_map.38), channel_id=1, source_target_pairs={{0,32},{32,64},{64,96},{96,128},{128,160},{160,192},{192,224},{224... | collective-permute-start | bytes 122888 | tf_op jit(solution)/shard_map/ppermute | solution.py:369
  47.6 19.6 %all-to-all-start.1 = ((f32[32,1,128]{2,1,0:T(1,128)}), f32[32,1,128]{2,1,0:T(1,128)S(1)}, u32[]{:S(2)}, u32[]{:S(2)}) async-start(f32[32,1,128]{2,1,0:T(1,128)} %shard_map.40), calls=%async_computation.1 | async-start | bytes 32768 | tf_op jit(solution)/shard_map/all_to_all | solution.py:389

commit v3 on v2

v3 whole, which is shorter than its diff:
```python
import jax
import jax.numpy as jnp
from jax import lax
from jax.experimental import pallas as pl
from jax.experimental.pallas import tpu as pltpu
from jax.sharding import PartitionSpec as P

Q = 19
PLANES = 8
LATTICE = (
    (0, 0, 0),
    (1, 0, 0),
    (-1, 0, 0),
    (0, 1, 0),
    (0, -1, 0),
    (0, 0, 1),
    (0, 0, -1),
    (1, 1, 0),
    (-1, -1, 0),
    (1, -1, 0),
    (-1, 1, 0),
    (1, 0, 1),
    (-1, 0, -1),
    (1, 0, -1),
    (-1, 0, 1),
    (0, 1, 1),
    (0, -1, -1),
    (0, 1, -1),
    (0, -1, 1),
)
OPPOSITE = (0, 2, 1, 4, 3, 6, 5, 8, 7, 10, 9, 12, 11, 14, 13, 16, 15, 18, 17)
INCOMING = (4, 8, 9, 16, 18)
SECOND, THIRD, FOURTH = 1.8, 1.2, 1.1
BASE_DRIVE = 0.0001
DRIVE_GAIN = 1.0
TARGET_FLOW = 0.1

FLAG_SLOT = Q * PLANES
INFLOW_SLOT = FLAG_SLOT + 2
SLOTS = INFLOW_SLOT + len(INCOMING)
TILES = 5
ROW_TILES = 40
GROUP = 24
SUMS_LANE = 10 * GROUP


def relax(f):
    along = []
    for p in (1, 3, 5):
        along.append((f[p] + f[p + 1], f[p] - f[p + 1]))
    diagonal = []
    for p in (7, 11, 15):
        a, b = f[p] + f[p + 1], f[p + 2] + f[p + 3]
        c, d = f[p] - f[p + 1], f[p + 2] - f[p + 3]
        diagonal.append((a + b, a - b, c + d, c - d))
    (xxyy, xy, xyy, xxy), (xxzz, xz, xzz, xxz), (yyzz, yz, yzz, yyz) = diagonal
    density = f[0] + (along[0][0] + along[1][0] + along[2][0]) + (xxyy + xxzz + yyzz)
    jx = along[0][1] + xyy + xzz
    jy = along[1][1] + xxy + yzz
    jz = along[2][1] + xxz + yyz
    inv = 1.0 / density
    ux, uy, uz = jx * inv, jy * inv, jz * inv
    exx, eyy, ezz = jx * ux, jy * uy, jz * uz
    third = density * (1.0 / 3.0)
    ninth = density * (1.0 / 9.0)
    xx = along[0][0] + xxyy + xxzz
    yy = along[1][0] + xxyy + yyzz
    zz = along[2][0] + xxzz + yyzz
    dxx = SECOND * (xx - third - exx)
    dyy = SECOND * (yy - third - eyy)
    dzz = SECOND * (zz - third - ezz)
    dxy = SECOND * (xy - jx * uy)
    dxz = SECOND * (xz - jx * uz)
    dyz = SECOND * (yz - jy * uz)
    x3, y3, z3 = jx * (1.0 / 3.0), jy * (1.0 / 3.0), jz * (1.0 / 3.0)
    dxyy, dxzz = THIRD * (xyy - x3), THIRD * (xzz - x3)
    dxxy, dyzz = THIRD * (xxy - y3), THIRD * (yzz - y3)
    dxxz, dyyz = THIRD * (xxz - z3), THIRD * (yyz - z3)
    half = 0.5 * (exx + eyy + ezz)
    dxxyy = FOURTH * (xxyy - ninth - (half - 0.5 * ezz) * (2.0 / 3.0) + ezz * (1.0 / 6.0))
    dxxzz = FOURTH * (xxzz - ninth - (half - 0.5 * eyy) * (2.0 / 3.0) + eyy * (1.0 / 6.0))
    dyyzz = FOURTH * (yyzz - ninth - (half - 0.5 * exx) * (2.0 / 3.0) + exx * (1.0 / 6.0))
    out = [None] * Q
    out[0] = f[0] + (dxx + dyy + dzz) - (dxxyy + dxxzz + dyyzz)
    for p, even, odd in (
        (1, dxx - dxxyy - dxxzz, dxyy + dxzz),
        (3, dyy - dxxyy - dyyzz, dxxy + dyzz),
        (5, dzz - dxxzz - dyyzz, dxxz + dyyz),
    ):
        out[p] = f[p] - 0.5 * (even - odd)
        out[p + 1] = f[p + 1] - 0.5 * (even + odd)
    for p, four, cross, first, second in (
        (7, dxxyy, dxy, dxyy, dxxy),
        (11, dxxzz, dxz, dxzz, dxxz),
        (15, dyyzz, dyz, dyzz, dyyz),
    ):
        same, other = 0.25 * (four + cross), 0.25 * (four - cross)
        total, rest = 0.25 * (first + second), 0.25 * (first - second)
        out[p] = f[p] - (same + total)
        out[p + 1] = f[p + 1] - (same - total)
        out[p + 2] = f[p + 2] - (other + rest)
        out[p + 3] = f[p + 3] - (other - rest)
    return out, (ux, uy, uz), inv


def weight(index):
    return 1.0 / 3.0 if index == 0 else (1.0 / 18.0 if index < 7 else 1.0 / 36.0)


def push_parts(index, velocity, inv):
    cx, cy, cz = LATTICE[index]
    along = 9.0 * velocity[0] - 3.0 * velocity[0] + 3.0 * cx
    if cy:
        along = along + (9.0 * cx * cy) * velocity[1]
    if cz:
        along = along + (9.0 * cx * cz) * velocity[2]
    return weight(index) * along, (3.0 * weight(index)) * inv


def driven(relaxed, velocity, inv, drive):
    ux, uy, uz = velocity
    square = drive * drive * inv
    still = -3.0 * drive * ux - 1.5 * square
    moved = still + 9.0 * drive * ux + 4.5 * square
    three = 3.0 * drive
    up, down = moved + three, moved - three
    hy, hz = 9.0 * drive * uy, 9.0 * drive * uz
    calm = still * (1.0 / 36.0)
    out = list(relaxed)
    out[0] = out[0] + still * (1.0 / 3.0)
    out[1] = out[1] + up * (1.0 / 18.0)
    out[2] = out[2] + down * (1.0 / 18.0)
    for index in (3, 4, 5, 6):
        out[index] = out[index] + (calm + calm)
    for p, side in ((7, hy), (11, hz)):
        out[p] = out[p] + (up + side) * (1.0 / 36.0)
        out[p + 1] = out[p + 1] + (down + side) * (1.0 / 36.0)
        out[p + 2] = out[p + 2] + (up - side) * (1.0 / 36.0)
        out[p + 3] = out[p + 3] + (down - side) * (1.0 / 36.0)
    for index in (15, 16, 17, 18):
        out[index] = out[index] + calm
    return out


def rolled(value, step_z, step_x):
    if step_z:
        value = pltpu.roll(value, step_z % value.shape[0], 0)
    if step_x:
        value = pltpu.roll(value, step_x % value.shape[1], 1)
    return value


def slot_values(pops, solid, inflow):
    values = [lambda q=q, y=y: pops[q, y] for q in range(Q) for y in range(PLANES)]
    values += [lambda y=y: solid[y].astype(jnp.float32) for y in range(2)]
    values += [lambda i=i: inflow[i] for i in range(len(INCOMING))]
    return values


def is_odd(axis):
    return lax.axis_index(axis) % 2 == 1


def pack_rows(pops_hbm, solid_hbm, inflow_hbm, first, second, pops, solid, inflow, done):
    copies = [
        pltpu.make_async_copy(source, target, done.at[i])
        for i, (source, target) in enumerate(((pops_hbm, pops), (solid_hbm, solid), (inflow_hbm, inflow)))
    ]
    for copy in copies:
        copy.start()
    for copy in copies:
        copy.wait()
    odd = is_odd("gz")
    for slot, value in enumerate(slot_values(pops, solid, inflow)):
        tile = value()
        low, high = tile[0:2], tile[6:8]
        place = (slot // 4, slice(2 * (slot % 4), 2 * (slot % 4) + 2))
        first[place] = jnp.where(odd, low, high)
        second[place] = jnp.where(odd, high, low)


def lay_rows(target, main, slot, odd, first, second):
    place = (slot // 4, slice(2 * (slot % 4), 2 * (slot % 4) + 2))
    one, two = first[place], second[place]
    target[0:8] = main
    target[8:10] = jnp.where(odd, two, one)
    target[14:16] = jnp.where(odd, one, two)


def tally(pops, solid, inflow, first, second, out, flags):
    lane = lax.broadcasted_iota(jnp.int32, (8, 128), 1)
    odd = is_odd("gz")
    flags[...] = jnp.zeros(flags.shape, jnp.float32)
    for y in range(2):
        lay_rows(flags.at[y], solid[y].astype(jnp.float32), FLAG_SLOT + y, odd, first, second)
    fluid = [1.0 - flags[y, 0:8] for y in range(2)]
    flow = jnp.zeros((8, 128), jnp.float32)
    for y in range(PLANES):
        f = pops
        jx = (
            (f[1, y] - f[2, y])
            + (f[7, y] - f[8, y])
            + (f[9, y] - f[10, y])
            + (f[11, y] - f[12, y])
            + (f[13, y] - f[14, y])
        )
        flow = flow + (jx * fluid[y] if y < 2 else jx)
    one = flow
    count = float(PLANES - 2) + fluid[0] + fluid[1]
    two = jnp.zeros((8, 128), jnp.float32)
    weights = {}
    for y in (0, 1, 2, PLANES - 1):
        relaxed, velocity, inv = relax([pops[q, y] for q in range(Q)])
        for index in range(Q):
            cx, cy, cz = LATTICE[index]
            target = y + cy
            if not cx or 1 < target < PLANES:
                continue
            linear, square = push_parts(index, velocity, inv)
            factor = -float(cx) if target >= PLANES else -2.0 * cx
            parts = [relaxed[index] * factor, linear * factor, square * factor]
            if y < 2:
                parts = [part * fluid[y] for part in parts]
            if 0 <= target < PLANES:
                for i, part in enumerate(parts):
                    key = ((0 if cx > 0 else 6) + 3 * target + i, cz)
                    weights[key] = weights[key] + part if key in weights else part
                hit = rolled(flags[target], -cz, -cx)[0:8]
                hit = jnp.where(lane == (127 if cx > 0 else 0), 0.0, hit)
                parts = [part * hit for part in parts]
            one, count, two = one + parts[0], count + parts[1], two + parts[2]
    one = one + (inflow[INCOMING.index(9)] - inflow[INCOMING.index(8)])

    nothing = jnp.zeros((8, 128), jnp.float32)
    by_row = {-1: nothing, 0: nothing, 1: nothing}
    for (place, cz), part in weights.items():
        by_row[cz] = jnp.where(lane == place, rolled(part, 0, place - (127 if place < 6 else 0)), by_row[cz])
    table = jnp.zeros((16, 128), jnp.float32)
    for cz, part in by_row.items():
        table = table + rolled(jnp.concatenate([part, nothing], axis=0), cz, 0)
    lanes = lax.broadcasted_iota(jnp.int32, (16, 128), 1)
    for y in range(2):
        for i in range(3):
            place = 12 + 3 * y + i
            table = jnp.where(lanes == place, rolled(flags[y], 0, place), table)
            table = jnp.where(lanes == place + 6, rolled(flags[y], 0, place + 6 - 127), table)
    halves = [nothing, nothing]
    for k in range(10):
        row = k if k < 9 else 15
        spread = rolled(jnp.broadcast_to(table[row : row + 1], (8, 128)), 0, (GROUP * k) % 128)
        for half in range(2):
            start = GROUP * k - 128 * half
            if -GROUP < start < 128:
                halves[half] = jnp.where((lane >= start) & (lane < start + GROUP), spread, halves[half])
    for i, part in enumerate((flow, one, count, two)):
        total = jnp.sum(jnp.sum(part, axis=0, keepdims=True), axis=1, keepdims=True)
        halves[1] = jnp.where(lane == SUMS_LANE - 128 + i, total, halves[1])
    packed = jnp.concatenate([halves[0][0:1], halves[1][0:1]], axis=1)
    out[...] = jnp.broadcast_to(packed[None], out.shape)


def cross(messages, edges, out, edges_out):
    table = messages[...]
    count = table.shape[0]
    place = lax.broadcasted_iota(jnp.int32, table.shape, 1)
    within = lax.rem(place, GROUP)
    following = jnp.where(within < 18, pltpu.roll(table, count - 1, 0), pltpu.roll(table, 1, 0))
    matched = jnp.where(within < 12, table * rolled(following, 0, -12), 0.0)
    packed = jnp.sum(jnp.where(place < SUMS_LANE, matched, table), axis=0, keepdims=True)
    out[...] = jnp.broadcast_to(packed[None], out.shape)
    edges_out[...] = edges[...]


def drives(sums, node_total):
    packed = jnp.sum(sums, axis=0)
    place = lax.broadcasted_iota(jnp.int32, packed.shape, 1)
    within = lax.rem(place, GROUP)
    totals = []
    for i in range(4):
        keep = place == SUMS_LANE + i
        if i:
            keep = keep | ((place < SUMS_LANE) & (within < 12) & (lax.rem(within, 3) == i - 1))
        totals.append(jnp.sum(jnp.where(keep, packed, 0.0), axis=1, keepdims=True))
    flow, one, count, two = totals
    first = BASE_DRIVE + DRIVE_GAIN * (TARGET_FLOW - flow / node_total)
    later = (one + count * first + two * (first * first)) / node_total
    second = BASE_DRIVE + DRIVE_GAIN * (TARGET_FLOW - later)
    return jnp.broadcast_to(first, (8, 128)), jnp.broadcast_to(second, (8, 128))


HALVES = (slice(0, 8), slice(8, 16))


def prepare(pops, solid, inflow, first, second, edges, kept, relaxed, state, flags, entry, rows):
    odd = is_odd("gz")
    lane = lax.broadcasted_iota(jnp.int32, (8, 128), 1)
    row = lax.broadcasted_iota(jnp.int32, (8, 128), 0)
    values = slot_values(pops, solid, inflow)
    for tile in range(TILES):
        packed = [jnp.zeros((8, 128), jnp.float32)] * 2
        for slot in range(tile * 32, min(tile * 32 + 32, SLOTS)):
            offset = 4 * (slot % 32)
            one, two = first[slot // 4], second[slot // 4]
            above, below = jnp.where(odd, two, one), jnp.where(odd, one, two)
            start = 2 * (slot % 4)
            outer = jnp.where(row < 4, rolled(above, -start, 0), rolled(below, 6 - start, 0))
            place = ((lane + (128 - offset + 2)) & 127) < 4
            for half, value in enumerate((values[slot](), outer)):
                packed[half] = jnp.where(place, rolled(value, 0, offset), packed[half])
        edges[tile, 0:8] = packed[0]
        edges[tile, 8:16] = packed[1]
    for y in range(2):
        lay_rows(flags.at[y], solid[y].astype(jnp.float32), FLAG_SLOT + y, odd, first, second)
    for i in range(len(INCOMING)):
        lay_rows(entry.at[i], inflow[i], INFLOW_SLOT + i, odd, first, second)
    for y in range(PLANES):
        for q in range(Q):
            lay_rows(rows.at[y, q], pops[q, y], q * PLANES + y, odd, first, second)
    kept[...] = rows[0:2]

    def collide(y, carry):
        for half in HALVES:
            result, velocity, inv = relax([rows[y, q, half] for q in range(Q)])
            for q in range(Q):
                relaxed[y, q, half] = result[q]
            for i, value in enumerate(velocity + (inv,)):
                state[y, i, half] = value
        return carry

    lax.fori_loop(0, PLANES, collide, 0)


def advance(
    node_total, kept, relaxed, state, flags, entry, near, far, sums,
    out_hbm, out, moved, now, moved_side, now_side, hits, hits_side, done,
):
    drive, drive_later = drives(sums[...], node_total)
    odd = is_odd("gx")
    lane = lax.broadcasted_iota(jnp.int32, (16, 128), 1)
    edges = []
    for tile in range(TILES):
        one, two = near[tile], far[tile]
        low, high = jnp.where(odd, one, two), jnp.where(odd, two, one)
        edges.append(jnp.where((lane & 3) < 2, high, low))
    for q in range(Q):
        now_side[q] = rolled(edges[q // 4], 0, -32 * (q % 4))
    wall = ((lane + 2) & 127) < 8
    flags_side = jnp.where(wall, rolled(edges[4], 0, -96), 0.0)
    stay_side = flags_side > 0.5

    def sideways(value, q, source):
        cx, _, cz = LATTICE[q]
        lane_to = 0 if cx > 0 else 127
        return lane == lane_to, rolled(value, cz, lane_to - (4 * source - (1 if cx > 0 else 0)))

    def inward(q, source):
        cx, cy, cz = LATTICE[q]
        lane_to = 4 * (source + cy) - (0 if cx > 0 else 1)
        return lane == lane_to % 128, lane_to - (127 if cx > 0 else 0)

    for q in range(Q):
        cx, cy, cz = LATTICE[q]
        for source in range(2):
            hit = rolled(flags[source], cz, cx)
            if cx:
                edge, value = sideways(flags_side, q, source)
                hit = jnp.where(edge, value, hit)
            hits[source, q] = hit
        hit = rolled(flags_side, cz, 4 * cy + cx)
        for source in range(2):
            if cx and 0 <= source + cy:
                edge, shift = inward(q, source)
                hit = jnp.where(edge, rolled(flags[source], cz, shift), hit)
        if cy > 0:
            hit = jnp.where(((lane + 2) & 127) < 4, 1.0, hit)
        hits_side[q] = hit

    def push(y, carry):
        for half in HALVES:
            velocity = tuple(state[y, i, half] for i in range(3))
            result = driven([relaxed[y, q, half] for q in range(Q)], velocity, state[y, 3, half], drive)
            for q in range(Q):
                moved[y, q, half] = result[q]
        return carry

    def collide(y, carry):
        for half in HALVES:
            result = driven(*relax([now[y, q, half] for q in range(Q)]), drive_later)
            for q in range(Q):
                moved[y, q, half] = result[q]
        return carry

    def collide_side(applied):
        for half in HALVES:
            result = driven(*relax([now_side[q, half] for q in range(Q)]), applied)
            for q in range(Q):
                moved_side[q, half] = result[q]

    def arrive(y, q, part):
        cx, cy, cz = LATTICE[q]
        source = y - cy
        if source < 0:
            arrived = moved[y, OPPOSITE[q], part]
        elif source >= PLANES:
            arrived = entry[INCOMING.index(q), part]
        else:
            arrived = rolled(moved[source, q], cz, cx)
            if cx:
                edge, value = sideways(moved_side[q], q, source)
                arrived = jnp.where(edge, value, arrived)
            arrived = arrived[part]
            if source < 2:
                arrived = jnp.where(hits[source, q, part] > 0.5, moved[y, OPPOSITE[q], part], arrived)
        if y < 2:
            before = kept if part == slice(0, 16) else now
            arrived = jnp.where(flags[y, part] > 0.5, before[y, q, part], arrived)
        return arrived

    def arrive_side(q):
        cx, cy, cz = LATTICE[q]
        arrived = rolled(moved_side[q], cz, 4 * cy + cx)
        if cx:
            for source in range(PLANES):
                if 0 <= source + cy < PLANES:
                    edge, shift = inward(q, source)
                    arrived = jnp.where(edge, rolled(moved[source, q], cz, shift), arrived)
        arrived = jnp.where(hits_side[q] > 0.5, moved_side[OPPOSITE[q]], arrived)
        if cy < 0:
            slot = (INFLOW_SLOT + INCOMING.index(q)) % 32
            value = rolled(edges[INFLOW_SLOT // 32], 0, 4 * (PLANES - 1) - 4 * slot)
            arrived = jnp.where(((lane - 26) & 127) < 4, value, arrived)
        return jnp.where(stay_side, now_side[q], arrived)

    lax.fori_loop(0, PLANES, push, 0)
    collide_side(drive)
    for y in range(PLANES):
        for q in range(Q):
            now[y, q] = arrive(y, q, slice(0, 16))
    for q in range(Q):
        now_side[q] = arrive_side(q)
    lax.fori_loop(0, PLANES, collide, 0)
    collide_side(drive_later)
    copies = []
    for y in range(PLANES):
        for q in range(Q):
            out[y, q] = arrive(y, q, slice(0, 8))
        copies.append(pltpu.make_async_copy(out.at[y], out_hbm.at[:, y], done.at[y]))
        copies[-1].start()
    for copy in copies:
        copy.wait()


def kernel_call(body, shapes, scratch, *operands, memory=pltpu.VMEM):
    return pl.pallas_call(
        body,
        in_specs=[pl.BlockSpec(memory_space=memory)] * len(operands),
        out_specs=[pl.BlockSpec(memory_space=pltpu.VMEM)] * len(shapes),
        out_shape=[pltpu.VMEM(item, jnp.float32) if isinstance(item, tuple) else item for item in shapes],
        scratch_shapes=[
            pltpu.VMEM(item, jnp.float32) if isinstance(item, tuple) else item for item in scratch
        ],
        compiler_params=pltpu.CompilerParams(vmem_limit_bytes=20 * 1024 * 1024),
    )(*operands)


def swapped(axis, first, second):
    count = lax.axis_size(axis)
    pairs = [(i, i ^ 1) for i in range(count)]
    others = [(i, (i + 1 if i % 2 else i - 1) % count) for i in range(count)]
    return lax.ppermute(first, axis, pairs), lax.ppermute(second, axis, others)


def local(populations, solid, top_inflow):
    along_x, along_z = lax.axis_size("gx"), lax.axis_size("gz")
    node_total = float(PLANES * 8 * 128 * along_x * along_z)
    fields = (populations, solid, top_inflow)
    first, second, *fields = kernel_call(
        pack_rows,
        [(ROW_TILES, 8, 128)] * 2 + [pltpu.VMEM(field.shape, field.dtype) for field in fields],
        [pltpu.SemaphoreType.DMA((3,))],
        *(pltpu.with_memory_space_constraint(field, pltpu.HBM) for field in fields),
        memory=pltpu.HBM,
    )
    halo = swapped("gz", first, second)
    (sums,) = kernel_call(tally, [(along_x, 1, 256)], [(2, 16, 128)], *fields, *halo)
    sums = lax.all_to_all(sums, "gx", 0, 0, tiled=True)
    edges, *prepared = kernel_call(
        prepare,
        [
            (TILES, 16, 128),
            (2, Q, 16, 128),
            (PLANES, Q, 16, 128),
            (PLANES, 4, 16, 128),
            (2, 16, 128),
            (len(INCOMING), 16, 128),
        ],
        [(PLANES, Q, 16, 128)],
        *fields,
        *halo,
    )
    sums, edges = kernel_call(
        cross,
        [(along_z, 1, 256), (TILES, 16, 128)],
        [],
        sums.reshape(along_x, 256),
        edges,
    )
    sums = lax.all_to_all(sums, "gz", 0, 0, tiled=True)
    near, far = swapped("gx", edges, edges)
    (advanced,) = pl.pallas_call(
        lambda *refs: advance(node_total, *refs),
        in_specs=[pl.BlockSpec(memory_space=pltpu.VMEM)] * 8,
        out_specs=[pl.BlockSpec(memory_space=pltpu.HBM)],
        out_shape=[jax.ShapeDtypeStruct((Q, PLANES, 8, 128), jnp.float32)],
        scratch_shapes=[
            pltpu.VMEM((PLANES, Q, 8, 128), jnp.float32),
            pltpu.VMEM((PLANES, Q, 16, 128), jnp.float32),
            pltpu.VMEM((PLANES, Q, 16, 128), jnp.float32),
            pltpu.VMEM((Q, 16, 128), jnp.float32),
            pltpu.VMEM((Q, 16, 128), jnp.float32),
            pltpu.VMEM((2, Q, 16, 128), jnp.float32),
            pltpu.VMEM((Q, 16, 128), jnp.float32),
            pltpu.SemaphoreType.DMA((PLANES,)),
        ],
        compiler_params=pltpu.CompilerParams(vmem_limit_bytes=20 * 1024 * 1024),
    )(*prepared, near, far, sums)
    return advanced


def solution(mesh):
    placed = (P(None, None, "gz", "gx"), P(None, "gz", "gx"), P(None, "gz", "gx"))
    return jax.shard_map(
        local, mesh=mesh, in_specs=placed, out_specs=P(None, None, "gz", "gx"), check_vma=False
    )
```

time: 72.2 us -> 71.4 us (0.989)
  Pallas kernels: 8.56 us -> 6.67 us
    all_to_all x1, waiting for transfers between devices: 11 us -> 4.93 us  [local(): sums = lax.all_to_all(sums, 'gz', 0, 0, tiled=True)]
    all_to_all x1, waiting for transfers between devices: 1.56 us -> 7.12 us  [local(): sums = lax.all_to_all(sums, 'gx', 0, 0, tiled=True)]
    pallas_call x5 -> x4, Pallas kernels: 8.56 us -> 3.89 us  [kernel_call(): pl.pallas_call(body, in_specs=[pl.BlockSpec(memory_space=memory)] * len(o...]
    pallas_call x0 -> x1, Pallas kernels: none -> 2.78 us  [local(): pl.pallas_call(lambda *refs: advance(node_total, *refs), in_specs=[pl.Blo...]
    ppermute x4, waiting for transfers between devices: 5.72 us -> 6.62 us  [the longest x2 6.38 us: swapped(): lax.ppermute(second, axis, others)]
  transfers between devices with their start and end apart: 6 -> 6, of which waited for: 4 -> 5; matrix products, arithmetic and copies ran while one was open for 0% -> 0% of each run, Pallas kernels for 2% -> 1%
where the time goes in v3:
time: 71.4 us; the launch traced here: 71.1 us
  starting transfers between devices  45.6 us (64%)
  waiting for transfers between devices  18.7 us (26%)
  Pallas kernels  6.67 us (9%)
    all_to_all x1, starting transfers between devices, local(): sums = lax.all_to_all(sums, 'gx', 0, 0, tiled=True)  19.4 us
    ppermute x2, starting transfers between devices, swapped(): lax.ppermute(second, axis, others)  11.7 us
    all_to_all x1, starting transfers between devices, local(): sums = lax.all_to_all(sums, 'gz', 0, 0, tiled=True)  8.51 us
    all_to_all x1, waiting for transfers between devices, local(): sums = lax.all_to_all(sums, 'gx', 0, 0, tiled=True)  7.12 us
    ppermute x2, waiting for transfers between devices, swapped(): lax.ppermute(second, axis, others)  6.38 us
    ppermute x2, starting transfers between devices, swapped(): lax.ppermute(first, axis, pairs)  6.06 us
    all_to_all x1, waiting for transfers between devices, local(): sums = lax.all_to_all(sums, 'gz', 0, 0, tiled=True)  4.93 us
    pallas_call x4, Pallas kernels, kernel_call(): pl.pallas_call(body, in_specs=[pl.BlockSpec(memory_space=memory)] * len(o...  3.89 us
  transfers between devices with their start and end apart: 6, of which 5 were waited for; matrix products, arithmetic and copies ran while one was open for 0% of the time, Pallas kernels for 1%

profile of v3, /device:TPU:1, one launch (start us, length us, event | category | flops | bytes accessed | tf_op | source)
XLA Modules:
  0.0 71.1 jit_solution(12321001644268398902)
XLA Ops:
  0.0 1.2 %shard_map.37 = (f32[40,8,128]{2,1,0:T(8,128)S(1)}, f32[40,8,128]{2,1,0:T(8,128)S(1)}, f32[19,8,8,128]{3,2,1,0:T(8,128)S(1)}, s32[8,8,128]{2,1,0:T(8,128)S(1)}, f32[5,8,128]{2,1,0:T(8,128)S(1)}) custom-call(f32[19,8,8,128]{3,2,1,0:T(8,128)} %pops_hbm.1, s32[8,8,128]{2,1,0:T(8,128)} %solid_hbm.1, f32[5,8,128]{2,1,0:T(8,128)} %inflow_hbm.1), custom_call_target="tpu_custom_call" | custom-call | tf_op jit(solution)/shard_map/pallas_call | solution.py:454
  1.2 4.1 %collective-permute-start = (f32[40,8,128]{2,1,0:T(8,128)S(1)}, f32[40,8,128]{2,1,0:T(8,128)S(1)}, u32[]{:S(2)}, u32[]{:S(2)}) collective-permute-start(f32[40,8,128]{2,1,0:T(8,128)S(1)} %get-tuple-element.21), channel_id=1, source_target_pairs={{0,1},{1,0},{2,3},{3,2},{4,5},{5,4},{6,7},{7,6},{8,9},{9,8},{10,11... | collective-permute-start | bytes 491528 | tf_op jit(solution)/shard_map/ppermute | solution.py:470
  5.4 8.6 %collective-permute-start.1 = (f32[40,8,128]{2,1,0:T(8,128)S(1)}, f32[40,8,128]{2,1,0:T(8,128)S(1)}, u32[]{:S(2)}, u32[]{:S(2)}) collective-permute-start(f32[40,8,128]{2,1,0:T(8,128)S(1)} %get-tuple-element.22), channel_id=1, source_target_pairs={{0,31},{1,2},{2,1},{3,4},{4,3},{5,6},{6,5},{7,8},{8,7},{9,10},{10,... | collective-permute-start | bytes 491528 | tf_op jit(solution)/shard_map/ppermute | solution.py:470
  14.0 0.0 collective-permute-done.first
  14.0 5.4 %collective-permute-done.1.second = f32[40,8,128]{2,1,0:T(8,128)S(1)} collective-permute-done((f32[40,8,128]{2,1,0:T(8,128)S(1)}, f32[40,8,128]{2,1,0:T(8,128)S(1)}, u32[]{:S(2)}, u32[]{:S(2)}) %collective-permute-start.1) | collective-permute-done | bytes 163872 | tf_op jit(solution)/shard_map/ppermute | solution.py:470
  19.4 1.0 %shard_map.39 = f32[32,1,256]{2,1,0:T(1,128)} custom-call(f32[19,8,8,128]{3,2,1,0:T(8,128)S(1)} %get-tuple-element.18.pops, s32[8,8,128]{2,1,0:T(8,128)S(1)} %get-tuple-element.19.solid, f32[5,8,128]{2,1,0:T(8,128)S(1)} %get-tuple-element.20.inflow, f32[40,8,128]{2,1,0:T(8,128)S(1)} %collective-permute-done.first, ...), custom_call_target="tpu_custom_call" | custom-call | tf_op jit(solution)/shard_map/pallas_call | solution.py:454
  20.4 19.4 %all-to-all-start = ((f32[32,1,256]{2,1,0:T(1,128)}), f32[32,1,256]{2,1,0:T(1,128)S(1)}, u32[]{:S(2)}, u32[]{:S(2)}) async-start(f32[32,1,256]{2,1,0:T(1,128)} %shard_map.39), calls=%async_computation | async-start | bytes 65536 | tf_op jit(solution)/shard_map/all_to_all | solution.py:486
  39.8 1.0 %shard_map.38 = (f32[5,16,128]{2,1,0:T(8,128)S(1)}, f32[2,19,16,128]{3,2,1,0:T(8,128)S(1)}, f32[8,19,16,128]{3,2,1,0:T(8,128)S(1)}, f32[8,4,16,128]{3,2,1,0:T(8,...) custom-call(f32[19,8,8,128]{3,2,1,0:T(8,128)S(1)} %get-tuple-element.18.pops, ...), custom_call_target="tpu_custom_call" | custom-call | tf_op jit(solution)/shard_map/pallas_call | solution.py:454
  40.8 7.1 %all-to-all-done = f32[32,1,256]{2,1,0:T(1,128)S(1)} async-done(((f32[32,1,256]{2,1,0:T(1,128)}), f32[32,1,256]{2,1,0:T(1,128)S(1)}, u32[]{:S(2)}, u32[]{:S(2)}) %all-to-all-start) | async-done | bytes 32800 | tf_op jit(solution)/shard_map/all_to_all | solution.py:486
  47.9 0.7 %shard_map.40 = (f32[32,1,256]{2,1,0:T(1,128)}, f32[5,16,128]{2,1,0:T(8,128)S(1)}) custom-call(f32[32,256]{1,0:T(8,128)S(1)} %bitcast.3, f32[5,16,128]{2,1,0:T(8,128)S(1)} %get-tuple-element.28.edges), custom_call_target="tpu_custom_call" | custom-call | tf_op jit(solution)/shard_map/pallas_call | solution.py:454
  48.6 8.5 %all-to-all-start.1 = ((f32[32,1,256]{2,1,0:T(1,128)}), f32[32,1,256]{2,1,0:T(1,128)S(1)}, u32[]{:S(2)}, u32[]{:S(2)}) async-start(f32[32,1,256]{2,1,0:T(1,128)} %get-tuple-element.30), calls=%async_computation.1 | async-start | bytes 65536 | tf_op jit(solution)/shard_map/all_to_all | solution.py:508
  57.2 3.1 %collective-permute-start.3 = (f32[5,16,128]{2,1,0:T(8,128)S(1)}, f32[5,16,128]{2,1,0:T(8,128)S(1)}, u32[]{:S(2)}, u32[]{:S(2)}) collective-permute-start(f32[5,16,128]{2,1,0:T(8,128)S(1)} %get-tuple-element.29), channel_id=1, source_target_pairs={{0,992},{32,64},{64,32},{96,128},{128,96},{160,192},{192,160},{224... | collective-permute-start | bytes 122888 | tf_op jit(solution)/shard_map/ppermute | solution.py:470
  60.2 1.9 %collective-permute-start.2 = (f32[5,16,128]{2,1,0:T(8,128)S(1)}, f32[5,16,128]{2,1,0:T(8,128)S(1)}, u32[]{:S(2)}, u32[]{:S(2)}) collective-permute-start(f32[5,16,128]{2,1,0:T(8,128)S(1)} %get-tuple-element.29), channel_id=1, source_target_pairs={{0,32},{32,0},{64,96},{96,64},{128,160},{160,128},{192,224},{224,1... | collective-permute-start | bytes 122888 | tf_op jit(solution)/shard_map/ppermute | solution.py:470
  62.2 1.0 %collective-permute-done.3.refs_6_ = f32[5,16,128]{2,1,0:T(8,128)S(1)} collective-permute-done((f32[5,16,128]{2,1,0:T(8,128)S(1)}, f32[5,16,128]{2,1,0:T(8,128)S(1)}, u32[]{:S(2)}, u32[]{:S(2)}) %collective-permute-start.3) | collective-permute-done | bytes 40992 | tf_op jit(solution)/shard_map/ppermute | solution.py:470
  63.1 0.2 collective-permute-done.2.refs_5_
  63.3 4.9 %all-to-all-done.1.refs_7_ = f32[32,1,256]{2,1,0:T(1,128)S(1)} async-done(((f32[32,1,256]{2,1,0:T(1,128)}), f32[32,1,256]{2,1,0:T(1,128)S(1)}, u32[]{:S(2)}, u32[]{:S(2)}) %all-to-all-start.1) | async-done | bytes 32800 | tf_op jit(solution)/shard_map/all_to_all | solution.py:508
  68.3 2.8 %shard_map.41 = f32[19,8,8,128]{3,2,1,0:T(8,128)} custom-call(f32[2,19,16,128]{3,2,1,0:T(8,128)S(1)} %get-tuple-element.23.refs_0_, f32[8,19,16,128]{3,2,1,0:T(8,128)S(1)} %get-tuple-element.24.refs_1_, f32[8,4,16,128]{3,2,1,0:T(8,128)S(1)} %get-tuple-element.25.refs_2_, f32[2,16,128]{2,1,0:T(8,128)S(1)} %get-tuple-element.26.refs_3_, ...), custom_call_target="tpu_custom_call" | custom-call | tf_op jit(solution)/shard_map/pallas_call | solution.py:510
  (1 shorter events, 0.0 us)
Async XLA Ops:
  1.2 12.8 %collective-permute-start = (f32[40,8,128]{2,1,0:T(8,128)S(1)}, f32[40,8,128]{2,1,0:T(8,128)S(1)}, u32[]{:S(2)}, u32[]{:S(2)}) collective-permute-start(f32[40,8,128]{2,1,0:T(8,128)S(1)} %get-tuple-element.21), channel_id=1, source_target_pairs={{0,1},{1,0},{2,3},{3,2},{4,5},{5,4},{6,7},{7,6},{8,9},{9,8},{10,11... | collective-permute-start | bytes 491528 | tf_op jit(solution)/shard_map/ppermute | solution.py:470
  5.4 14.1 %collective-permute-start.1 = (f32[40,8,128]{2,1,0:T(8,128)S(1)}, f32[40,8,128]{2,1,0:T(8,128)S(1)}, u32[]{:S(2)}, u32[]{:S(2)}) collective-permute-start(f32[40,8,128]{2,1,0:T(8,128)S(1)} %get-tuple-element.22), channel_id=1, source_target_pairs={{0,31},{1,2},{2,1},{3,4},{4,3},{5,6},{6,5},{7,8},{8,7},{9,10},{10,... | collective-permute-start | bytes 491528 | tf_op jit(solution)/shard_map/ppermute | solution.py:470
  20.4 27.5 %all-to-all-start = ((f32[32,1,256]{2,1,0:T(1,128)}), f32[32,1,256]{2,1,0:T(1,128)S(1)}, u32[]{:S(2)}, u32[]{:S(2)}) async-start(f32[32,1,256]{2,1,0:T(1,128)} %shard_map.39), calls=%async_computation | async-start | bytes 65536 | tf_op jit(solution)/shard_map/all_to_all | solution.py:486
  48.6 19.6 %all-to-all-start.1 = ((f32[32,1,256]{2,1,0:T(1,128)}), f32[32,1,256]{2,1,0:T(1,128)S(1)}, u32[]{:S(2)}, u32[]{:S(2)}) async-start(f32[32,1,256]{2,1,0:T(1,128)} %get-tuple-element.30), calls=%async_computation.1 | async-start | bytes 65536 | tf_op jit(solution)/shard_map/all_to_all | solution.py:508
  57.2 5.9 %collective-permute-start.3 = (f32[5,16,128]{2,1,0:T(8,128)S(1)}, f32[5,16,128]{2,1,0:T(8,128)S(1)}, u32[]{:S(2)}, u32[]{:S(2)}) collective-permute-start(f32[5,16,128]{2,1,0:T(8,128)S(1)} %get-tuple-element.29), channel_id=1, source_target_pairs={{0,992},{32,64},{64,32},{96,128},{128,96},{160,192},{192,160},{224... | collective-permute-start | bytes 122888 | tf_op jit(solution)/shard_map/ppermute | solution.py:470
  60.2 3.1 %collective-permute-start.2 = (f32[5,16,128]{2,1,0:T(8,128)S(1)}, f32[5,16,128]{2,1,0:T(8,128)S(1)}, u32[]{:S(2)}, u32[]{:S(2)}) collective-permute-start(f32[5,16,128]{2,1,0:T(8,128)S(1)} %get-tuple-element.29), channel_id=1, source_target_pairs={{0,32},{32,0},{64,96},{96,64},{128,160},{160,128},{192,224},{224,1... | collective-permute-start | bytes 122888 | tf_op jit(solution)/shard_map/ppermute | solution.py:470

commit v4 on v3

--- a/solution.py
+++ b/solution.py
@@ -4,6 +4,7 @@
 from jax.experimental import pallas as pl
 from jax.experimental.pallas import tpu as pltpu
 from jax.sharding import PartitionSpec as P
+
 
 Q = 19
 PLANES = 8
@@ -40,6 +41,7 @@
 SLOTS = INFLOW_SLOT + len(INCOMING)
 TILES = 5
 ROW_TILES = 40
+PIECES = ((0, 5), (5, 10), (10, 15), (15, 19))
 GROUP = 24
 SUMS_LANE = 10 * GROUP
 
@@ -161,40 +163,55 @@
     return lax.axis_index(axis) % 2 == 1
 
 
-def pack_rows(pops_hbm, solid_hbm, inflow_hbm, first, second, pops, solid, inflow, done):
-    copies = [
-        pltpu.make_async_copy(source, target, done.at[i])
-        for i, (source, target) in enumerate(((pops_hbm, pops), (solid_hbm, solid), (inflow_hbm, inflow)))
-    ]
+def load(pops_hbm, solid_hbm, inflow_hbm, first, second, pops, solid, inflow, done):
+    copies = [(solid_hbm, solid), (inflow_hbm, inflow)]
+    copies += [(pops_hbm.at[a:b], pops.at[a:b]) for a, b in PIECES]
+    copies = [pltpu.make_async_copy(source, target, done.at[i]) for i, (source, target) in enumerate(copies)]
     for copy in copies:
         copy.start()
-    for copy in copies:
+    copies[0].wait()
+    odd = is_odd("gz")
+    first[...] = jnp.zeros(first.shape, jnp.float32)
+    second[...] = jnp.zeros(second.shape, jnp.float32)
+    for y in range(2):
+        tile = solid[y].astype(jnp.float32)
+        low, high = tile[0:2], tile[6:8]
+        first[2 * y : 2 * y + 2] = jnp.where(odd, low, high)
+        second[2 * y : 2 * y + 2] = jnp.where(odd, high, low)
+    for copy in copies[1:]:
         copy.wait()
+
+
+def pack_rows(pops, inflow, after, first, second):
     odd = is_odd("gz")
-    for slot, value in enumerate(slot_values(pops, solid, inflow)):
-        tile = value()
+    values = [(q * PLANES + y, pops[q, y]) for q in range(Q) for y in range(PLANES)]
+    values += [(INFLOW_SLOT + i, inflow[i]) for i in range(len(INCOMING))]
+    for slot, tile in values:
         low, high = tile[0:2], tile[6:8]
         place = (slot // 4, slice(2 * (slot % 4), 2 * (slot % 4) + 2))
         first[place] = jnp.where(odd, low, high)
         second[place] = jnp.where(odd, high, low)
 
 
-def lay_rows(target, main, slot, odd, first, second):
-    place = (slot // 4, slice(2 * (slot % 4), 2 * (slot % 4) + 2))
-    one, two = first[place], second[place]
+def lay_rows(target, main, odd, one, two):
     target[0:8] = main
     target[8:10] = jnp.where(odd, two, one)
     target[14:16] = jnp.where(odd, one, two)
 
 
-def tally(pops, solid, inflow, first, second, out, flags):
+def halo_rows(slot, first, second):
+    place = (slot // 4, slice(2 * (slot % 4), 2 * (slot % 4) + 2))
+    return first[place], second[place]
+
+
+def tally(pops, solid, inflow, acc, low_rows, high_rows, half_one, half_two):
     lane = lax.broadcasted_iota(jnp.int32, (8, 128), 1)
-    odd = is_odd("gz")
-    flags[...] = jnp.zeros(flags.shape, jnp.float32)
-    for y in range(2):
-        lay_rows(flags.at[y], solid[y].astype(jnp.float32), FLAG_SLOT + y, odd, first, second)
-    fluid = [1.0 - flags[y, 0:8] for y in range(2)]
-    flow = jnp.zeros((8, 128), jnp.float32)
+    row = lax.broadcasted_iota(jnp.int32, (8, 128), 0)
+    nothing = jnp.zeros((8, 128), jnp.float32)
+    blocked = [solid[y].astype(jnp.float32) for y in range(2)]
+    flags = [jnp.concatenate([part, nothing], axis=0) for part in blocked]
+    fluid = [1.0 - part for part in blocked]
+    flow = nothing
     for y in range(PLANES):
         f = pops
         jx = (
@@ -205,10 +222,11 @@
             + (f[13, y] - f[14, y])
         )
         flow = flow + (jx * fluid[y] if y < 2 else jx)
-    one = flow
+    one = flow + (inflow[INCOMING.index(9)] - inflow[INCOMING.index(8)])
     count = float(PLANES - 2) + fluid[0] + fluid[1]
-    two = jnp.zeros((8, 128), jnp.float32)
+    two = nothing
     weights = {}
+    outer = {-1: nothing, 1: nothing}
     for y in (0, 1, 2, PLANES - 1):
         relaxed, velocity, inv = relax([pops[q, y] for q in range(Q)])
         for index in range(Q):
@@ -225,13 +243,22 @@
                 for i, part in enumerate(parts):
                     key = ((0 if cx > 0 else 6) + 3 * target + i, cz)
                     weights[key] = weights[key] + part if key in weights else part
+                    if cz:
+                        place = 3 * target + i
+                        moved = rolled(part, place - (7 if cz > 0 else 0), cx)
+                        keep = (row == place) & (lane != (0 if cx > 0 else 127))
+                        outer[cz] = outer[cz] + jnp.where(keep, moved, 0.0)
                 hit = rolled(flags[target], -cz, -cx)[0:8]
                 hit = jnp.where(lane == (127 if cx > 0 else 0), 0.0, hit)
                 parts = [part * hit for part in parts]
             one, count, two = one + parts[0], count + parts[1], two + parts[2]
-    one = one + (inflow[INCOMING.index(9)] - inflow[INCOMING.index(8)])
-
-    nothing = jnp.zeros((8, 128), jnp.float32)
+    low_rows[...] = outer[-1]
+    high_rows[...] = outer[1]
+    totals = nothing
+    for i, part in enumerate((flow, one, count, two)):
+        totals = jnp.where(row == i, jnp.sum(part, axis=0, keepdims=True), totals)
+    acc[...] = totals
+
     by_row = {-1: nothing, 0: nothing, 1: nothing}
     for (place, cz), part in weights.items():
         by_row[cz] = jnp.where(lane == place, rolled(part, 0, place - (127 if place < 6 else 0)), by_row[cz])
@@ -246,40 +273,66 @@
             table = jnp.where(lanes == place + 6, rolled(flags[y], 0, place + 6 - 127), table)
     halves = [nothing, nothing]
     for k in range(10):
-        row = k if k < 9 else 15
-        spread = rolled(jnp.broadcast_to(table[row : row + 1], (8, 128)), 0, (GROUP * k) % 128)
+        source = k if k < 9 else 15
+        spread = rolled(jnp.broadcast_to(table[source : source + 1], (8, 128)), 0, (GROUP * k) % 128)
         for half in range(2):
             start = GROUP * k - 128 * half
             if -GROUP < start < 128:
                 halves[half] = jnp.where((lane >= start) & (lane < start + GROUP), spread, halves[half])
-    for i, part in enumerate((flow, one, count, two)):
-        total = jnp.sum(jnp.sum(part, axis=0, keepdims=True), axis=1, keepdims=True)
-        halves[1] = jnp.where(lane == SUMS_LANE - 128 + i, total, halves[1])
-    packed = jnp.concatenate([halves[0][0:1], halves[1][0:1]], axis=1)
+    half_one[...] = halves[0]
+    half_two[...] = halves[1]
+
+
+def announce(first, second, acc, low_rows, high_rows, half_one, half_two, out):
+    lane = lax.broadcasted_iota(jnp.int32, (8, 128), 1)
+    row = lax.broadcasted_iota(jnp.int32, (8, 128), 0)
+    odd = is_odd("gz")
+    one, two = first[...], second[...]
+    below, above = jnp.where(odd, one, two), jnp.where(odd, two, one)
+    tail = half_two[...]
+    edge = []
+    for flags, offset, k in ((below, 1, 9), (above, 0, 8)):
+        planes = [jnp.broadcast_to(flags[2 * y + offset : 2 * y + offset + 1], (8, 128)) for y in range(2)]
+        edge.append(jnp.where(row < 3, planes[0], jnp.where(row < 6, planes[1], 0.0)))
+        for y in range(2):
+            start = GROUP * k - 128 + 12 + 3 * y
+            for begin, column in ((start, 0), (start + 6, 127)):
+                value = jnp.broadcast_to(planes[y][:, column : column + 1], (8, 128))
+                tail = jnp.where((lane >= begin) & (lane < begin + 3), value, tail)
+    more = low_rows[...] * edge[0] + high_rows[...] * edge[1]
+    inside = (row >= 1) & (row < 4)
+    total = acc[...] + jnp.where(inside, rolled(more, 1, 0) + rolled(more, -2, 0), 0.0)
+    total = jnp.broadcast_to(jnp.sum(total, axis=1, keepdims=True), (8, 128))
+    total = jnp.sum(jnp.where(lane == SUMS_LANE - 128 + row, total, 0.0), axis=0, keepdims=True)
+    tail = jnp.where((lane >= SUMS_LANE - 128) & (lane < SUMS_LANE - 124), total, tail)
+    packed = jnp.concatenate([half_one[0:1], tail[0:1]], axis=1)
     out[...] = jnp.broadcast_to(packed[None], out.shape)
 
 
-def cross(messages, edges, out, edges_out):
+def within_group(place):
+    return place - GROUP * lax.shift_right_logical(place * 2731, 16)
+
+
+def cross(messages, out):
     table = messages[...]
     count = table.shape[0]
     place = lax.broadcasted_iota(jnp.int32, table.shape, 1)
-    within = lax.rem(place, GROUP)
+    within = within_group(place)
     following = jnp.where(within < 18, pltpu.roll(table, count - 1, 0), pltpu.roll(table, 1, 0))
     matched = jnp.where(within < 12, table * rolled(following, 0, -12), 0.0)
     packed = jnp.sum(jnp.where(place < SUMS_LANE, matched, table), axis=0, keepdims=True)
     out[...] = jnp.broadcast_to(packed[None], out.shape)
-    edges_out[...] = edges[...]
 
 
 def drives(sums, node_total):
     packed = jnp.sum(sums, axis=0)
     place = lax.broadcasted_iota(jnp.int32, packed.shape, 1)
-    within = lax.rem(place, GROUP)
+    within = within_group(place)
     totals = []
     for i in range(4):
         keep = place == SUMS_LANE + i
-        if i:
-            keep = keep | ((place < SUMS_LANE) & (within < 12) & (lax.rem(within, 3) == i - 1))
+        for start in range(i - 1, 12 if i else 0, 3):
+            keep = keep | ((place < SUMS_LANE) & (within == start))
         totals.append(jnp.sum(jnp.where(keep, packed, 0.0), axis=1, keepdims=True))
     flow, one, count, two = totals
     first = BASE_DRIVE + DRIVE_GAIN * (TARGET_FLOW - flow / node_total)
@@ -291,7 +344,7 @@
 HALVES = (slice(0, 8), slice(8, 16))
 
 
-def prepare(pops, solid, inflow, first, second, edges, kept, relaxed, state, flags, entry, rows):
+def pack_columns(pops, solid, inflow, first, second, first_flags, second_flags, after, edges):
     odd = is_odd("gz")
     lane = lax.broadcasted_iota(jnp.int32, (8, 128), 1)
     row = lax.broadcasted_iota(jnp.int32, (8, 128), 0)
@@ -300,22 +353,33 @@
         packed = [jnp.zeros((8, 128), jnp.float32)] * 2
         for slot in range(tile * 32, min(tile * 32 + 32, SLOTS)):
             offset = 4 * (slot % 32)
-            one, two = first[slot // 4], second[slot // 4]
+            start = 2 * (slot % 4)
+            if slot in (FLAG_SLOT, FLAG_SLOT + 1):
+                one, two = first_flags[...], second_flags[...]
+                start = 2 * (slot - FLAG_SLOT)
+            else:
+                one, two = first[slot // 4], second[slot // 4]
             above, below = jnp.where(odd, two, one), jnp.where(odd, one, two)
-            start = 2 * (slot % 4)
             outer = jnp.where(row < 4, rolled(above, -start, 0), rolled(below, 6 - start, 0))
             place = ((lane + (128 - offset + 2)) & 127) < 4
             for half, value in enumerate((values[slot](), outer)):
                 packed[half] = jnp.where(place, rolled(value, 0, offset), packed[half])
         edges[tile, 0:8] = packed[0]
         edges[tile, 8:16] = packed[1]
+
+
+def prepare(
+    pops, solid, inflow, first, second, first_flags, second_flags, after, kept, relaxed, state, flags, entry, rows
+):
+    odd = is_odd("gz")
     for y in range(2):
-        lay_rows(flags.at[y], solid[y].astype(jnp.float32), FLAG_SLOT + y, odd, first, second)
+        pair = slice(2 * y, 2 * y + 2)
+        lay_rows(flags.at[y], solid[y].astype(jnp.float32), odd, first_flags[pair], second_flags[pair])
     for i in range(len(INCOMING)):
-        lay_rows(entry.at[i], inflow[i], INFLOW_SLOT + i, odd, first, second)
+        lay_rows(entry.at[i], inflow[i], odd, *halo_rows(INFLOW_SLOT + i, first, second))
     for y in range(PLANES):
         for q in range(Q):
-            lay_rows(rows.at[y, q], pops[q, y], q * PLANES + y, odd, first, second)
+            lay_rows(rows.at[y, q], pops[q, y], odd, *halo_rows(q * PLANES + y, first, second))
     kept[...] = rows[0:2]
 
     def collide(y, carry):
@@ -354,7 +418,7 @@
         return lane == lane_to, rolled(value, cz, lane_to - (4 * source - (1 if cx > 0 else 0)))
 
     def inward(q, source):
-        cx, cy, cz = LATTICE[q]
+        cx, cy, _ = LATTICE[q]
         lane_to = 4 * (source + cy) - (0 if cx > 0 else 1)
         return lane == lane_to % 128, lane_to - (127 if cx > 0 else 0)
 
@@ -474,20 +538,27 @@
     along_x, along_z = lax.axis_size("gx"), lax.axis_size("gz")
     node_total = float(PLANES * 8 * 128 * along_x * along_z)
     fields = (populations, solid, top_inflow)
-    first, second, *fields = kernel_call(
-        pack_rows,
-        [(ROW_TILES, 8, 128)] * 2 + [pltpu.VMEM(field.shape, field.dtype) for field in fields],
-        [pltpu.SemaphoreType.DMA((3,))],
+    *flags, pops, solid, top_inflow = kernel_call(
+        load,
+        [(8, 128)] * 2 + [pltpu.VMEM(field.shape, field.dtype) for field in fields],
+        [pltpu.SemaphoreType.DMA((2 + len(PIECES),))],
         *(pltpu.with_memory_space_constraint(field, pltpu.HBM) for field in fields),
         memory=pltpu.HBM,
     )
-    halo = swapped("gz", first, second)
-    (sums,) = kernel_call(tally, [(along_x, 1, 256)], [(2, 16, 128)], *fields, *halo)
+    flags = swapped("gz", *flags)
+    own = kernel_call(tally, [(8, 128)] * 5, [], pops, solid, top_inflow)
+    (sums,) = kernel_call(announce, [(along_x, 1, 256)], [], *flags, *own)
+    rows = kernel_call(pack_rows, [(ROW_TILES, 8, 128)] * 2, [], pops, top_inflow, sums)
     sums = lax.all_to_all(sums, "gx", 0, 0, tiled=True)
-    edges, *prepared = kernel_call(
+    halo = swapped("gz", *rows)
+    (sums,) = kernel_call(cross, [(along_z, 1, 256)], [], sums.reshape(along_x, 256))
+    block = (pops, solid, top_inflow, *halo, *flags)
+    (edges,) = kernel_call(pack_columns, [(TILES, 16, 128)], [], *block, sums)
+    sums = lax.all_to_all(sums, "gz", 0, 0, tiled=True)
+    near, far = swapped("gx", edges, edges)
+    prepared = kernel_call(
         prepare,
         [
-            (TILES, 16, 128),
             (2, Q, 16, 128),
             (PLANES, Q, 16, 128),
             (PLANES, 4, 16, 128),
@@ -495,18 +566,9 @@
             (len(INCOMING), 16, 128),
         ],
         [(PLANES, Q, 16, 128)],
-        *fields,
-        *halo,
-    )
-    sums, edges = kernel_call(
-        cross,
-        [(along_z, 1, 256), (TILES, 16, 128)],
-        [],
-        sums.reshape(along_x, 256),
+        *block,
         edges,
     )
-    sums = lax.all_to_all(sums, "gz", 0, 0, tiled=True)
-    near, far = swapped("gx", edges, edges)
     (advanced,) = pl.pallas_call(
         lambda *refs: advance(node_total, *refs),
         in_specs=[pl.BlockSpec(memory_space=pltpu.VMEM)] * 8,

time: 71.4 us -> 71.9 us (level)
  blocking collectives: 0 us -> 27.2 us
  waiting for transfers between devices: 18.7 us -> 4.93 us
  starting transfers between devices: 45.6 us -> 32.1 us
    all_to_all x0 -> x1, blocking collectives: none -> 27.2 us  [local(): sums = lax.all_to_all(sums, 'gx', 0, 0, tiled=True)]
    all_to_all x1 -> x0, starting transfers between devices: 19.4 us -> none  [local(): sums = lax.all_to_all(sums, 'gx', 0, 0, tiled=True)]
    all_to_all x1 -> x0, waiting for transfers between devices: 7.12 us -> none  [local(): sums = lax.all_to_all(sums, 'gx', 0, 0, tiled=True)]
    ppermute x2 -> x3, starting transfers between devices: 11.7 us -> 18.6 us  [swapped(): lax.ppermute(second, axis, others)]
    ppermute x2 -> x3, waiting for transfers between devices: 6.38 us -> 0.7 us  [swapped(): lax.ppermute(second, axis, others)]
    all_to_all x1, starting transfers between devices: 8.51 us -> 4.83 us  [local(): sums = lax.all_to_all(sums, 'gz', 0, 0, tiled=True)]
    ppermute x2 -> x3, starting transfers between devices: 6.06 us -> 8.66 us  [swapped(): lax.ppermute(first, axis, pairs)]
    pallas_call x4 -> x7, Pallas kernels: 3.89 us -> 4.32 us  [kernel_call(): pl.pallas_call(body, in_specs=[pl.BlockSpec(memory_space=memory)] * len(o...]
  transfers between devices with their start and end apart: 6 -> 7, of which waited for: 5 -> 2; matrix products, arithmetic and copies ran while one was open for 0% -> 0% of each run, Pallas kernels for 1% -> 4%
where the time goes in v4:
time: 71.9 us; the launch traced here: 71.4 us
  starting transfers between devices  32.1 us (45%)
  blocking collectives  27.2 us (38%)
  Pallas kernels  7.12 us (10%)
  waiting for transfers between devices  4.93 us (7%)
    all_to_all x1, blocking collectives, local(): sums = lax.all_to_all(sums, 'gx', 0, 0, tiled=True)  27.2 us
    ppermute x3, starting transfers between devices, swapped(): lax.ppermute(second, axis, others)  18.6 us
    ppermute x3, starting transfers between devices, swapped(): lax.ppermute(first, axis, pairs)  8.66 us
    all_to_all x1, starting transfers between devices, local(): sums = lax.all_to_all(sums, 'gz', 0, 0, tiled=True)  4.83 us
    pallas_call x7, Pallas kernels, kernel_call(): pl.pallas_call(body, in_specs=[pl.BlockSpec(memory_space=memory)] * len(o...  4.32 us
    all_to_all x1, waiting for transfers between devices, local(): sums = lax.all_to_all(sums, 'gz', 0, 0, tiled=True)  4.22 us
    pallas_call x1, Pallas kernels, local(): pl.pallas_call(lambda *refs: advance(node_total, *refs), in_specs=[pl.Blo...  2.8 us
  transfers between devices with their start and end apart: 7, of which 2 were waited for; matrix products, arithmetic and copies ran while one was open for 0% of the time, Pallas kernels for 4%

profile of v4, /device:TPU:1, one launch (start us, length us, event | category | flops | bytes accessed | tf_op | source)
XLA Modules:
  0.0 71.4 jit_solution(2881265564805220864)
XLA Ops:
  0.0 1.2 %shard_map.37 = (f32[8,128]{1,0:T(8,128)S(1)}, f32[8,128]{1,0:T(8,128)S(1)}, f32[19,8,8,128]{3,2,1,0:T(8,128)S(1)}, s32[8,8,128]{2,1,0:T(8,128)S(1)}, f32[5,8,128]{2,1,0:T(8,128)S(1)}) custom-call(f32[19,8,8,128]{3,2,1,0:T(8,128)} %pops_hbm.1, s32[8,8,128]{2,1,0:T(8,128)} %solid_hbm.1, f32[5,8,128]{2,1,0:T(8,128)} %inflow_hbm.1), custom_call_target="tpu_custom_call" | custom-call | tf_op jit(solution)/shard_map/pallas_call | solution.py:518
  1.2 4.1 %collective-permute-start = (f32[8,128]{1,0:T(8,128)S(1)}, f32[8,128]{1,0:T(8,128)S(1)}, u32[]{:S(2)}, u32[]{:S(2)}) collective-permute-start(f32[8,128]{1,0:T(8,128)S(1)} %get-tuple-element.25), channel_id=1, source_target_pairs={{0,1},{1,0},{2,3},{3,2},{4,5},{5,4},{6,7},{7,6},{8,9},{9,8},{10,11... | collective-permute-start | bytes 12296 | tf_op jit(solution)/shard_map/ppermute | solution.py:534
  5.4 8.6 %collective-permute-start.1 = (f32[8,128]{1,0:T(8,128)S(1)}, f32[8,128]{1,0:T(8,128)S(1)}, u32[]{:S(2)}, u32[]{:S(2)}) collective-permute-start(f32[8,128]{1,0:T(8,128)S(1)} %get-tuple-element.26), channel_id=1, source_target_pairs={{0,31},{1,2},{2,1},{3,4},{4,3},{5,6},{6,5},{7,8},{8,7},{9,10},{10,... | collective-permute-start | bytes 12296 | tf_op jit(solution)/shard_map/ppermute | solution.py:534
  14.0 0.3 shard_map.38
  14.3 0.0 collective-permute-done.first.first_flags
  14.3 0.7 collective-permute-done.1.second.second_flags
  15.0 0.1 shard_map.39.after
  15.1 0.1 shard_map.40
  15.2 1.9 %collective-permute-start.2 = (f32[40,8,128]{2,1,0:T(8,128)S(1)}, f32[40,8,128]{2,1,0:T(8,128)S(1)}, u32[]{:S(2)}, u32[]{:S(2)}) collective-permute-start(f32[40,8,128]{2,1,0:T(8,128)S(1)} %get-tuple-element.32), channel_id=1, source_target_pairs={{0,1},{1,0},{2,3},{3,2},{4,5},{5,4},{6,7},{7,6},{8,9},{9,8},{10,11... | collective-permute-start | bytes 491528 | tf_op jit(solution)/shard_map/ppermute | solution.py:534
  17.2 7.6 %collective-permute-start.3 = (f32[40,8,128]{2,1,0:T(8,128)S(1)}, f32[40,8,128]{2,1,0:T(8,128)S(1)}, u32[]{:S(2)}, u32[]{:S(2)}) collective-permute-start(f32[40,8,128]{2,1,0:T(8,128)S(1)} %get-tuple-element.33), channel_id=1, source_target_pairs={{0,31},{1,2},{2,1},{3,4},{4,3},{5,6},{6,5},{7,8},{8,7},{9,10},{10,... | collective-permute-start | bytes 491528 | tf_op jit(solution)/shard_map/ppermute | solution.py:534
  24.8 27.2 %all_to_all.10 = f32[32,1,256]{2,1,0:T(1,128)S(1)} all-to-all(f32[32,1,256]{2,1,0:T(1,128)S(1)} %shard_map.39.after), channel_id=1, replica_groups=mesh['gx'=32,'gz'=32] {'gx'}, dimensions={0} | all-to-all | bytes 65536 | tf_op jit(solution)/shard_map/all_to_all | solution.py:552
  51.9 0.7 %shard_map.41.after = f32[32,1,256]{2,1,0:T(1,128)} custom-call(f32[32,256]{1,0:T(8,128)S(1)} %bitcast.3), custom_call_target="tpu_custom_call" | custom-call | tf_op jit(solution)/shard_map/pallas_call | solution.py:518
  52.7 4.8 %all-to-all-start.1 = ((f32[32,1,256]{2,1,0:T(1,128)}), f32[32,1,256]{2,1,0:T(1,128)S(1)}, u32[]{:S(2)}, u32[]{:S(2)}) async-start(f32[32,1,256]{2,1,0:T(1,128)} %shard_map.41.after), calls=%async_computation.1 | async-start | bytes 65536 | tf_op jit(solution)/shard_map/all_to_all | solution.py:557
  57.5 0.0 collective-permute-done.2.first
  57.5 0.0 collective-permute-done.3.second
  57.5 1.2 %shard_map.42.after = f32[5,16,128]{2,1,0:T(8,128)S(1)} custom-call(f32[19,8,8,128]{3,2,1,0:T(8,128)S(1)} %get-tuple-element.22.pops, s32[8,8,128]{2,1,0:T(8,128)S(1)} %get-tuple-element.23.solid, f32[5,8,128]{2,1,0:T(8,128)S(1)} %get-tuple-element.24.inflow, f32[40,8,128]{2,1,0:T(8,128)S(1)} %collective-permute-done.2.first, ...), custom_call_target="tpu_custom_call" | custom-call | tf_op jit(solution)/shard_map/pallas_call | solution.py:518
  58.7 2.6 %collective-permute-start.4 = (f32[5,16,128]{2,1,0:T(8,128)S(1)}, f32[5,16,128]{2,1,0:T(8,128)S(1)}, u32[]{:S(2)}, u32[]{:S(2)}) collective-permute-start(f32[5,16,128]{2,1,0:T(8,128)S(1)} %shard_map.42.after), channel_id=1, source_target_pairs={{0,32},{32,0},{64,96},{96,64},{128,160},{160,128},{192,224},{224,1... | collective-permute-start | bytes 122888 | tf_op jit(solution)/shard_map/ppermute | solution.py:534
  61.3 2.4 %collective-permute-start.5 = (f32[5,16,128]{2,1,0:T(8,128)S(1)}, f32[5,16,128]{2,1,0:T(8,128)S(1)}, u32[]{:S(2)}, u32[]{:S(2)}) collective-permute-start(f32[5,16,128]{2,1,0:T(8,128)S(1)} %shard_map.42.after), channel_id=1, source_target_pairs={{0,992},{32,64},{64,32},{96,128},{128,96},{160,192},{192,160},{224... | collective-permute-start | bytes 122888 | tf_op jit(solution)/shard_map/ppermute | solution.py:534
  63.7 0.7 shard_map.43
  64.4 4.2 %all-to-all-done.1.refs_7_ = f32[32,1,256]{2,1,0:T(1,128)S(1)} async-done(((f32[32,1,256]{2,1,0:T(1,128)}), f32[32,1,256]{2,1,0:T(1,128)S(1)}, u32[]{:S(2)}, u32[]{:S(2)}) %all-to-all-start.1) | async-done | bytes 32800 | tf_op jit(solution)/shard_map/all_to_all | solution.py:557
  68.6 0.0 collective-permute-done.4.refs_5_
  68.6 0.0 collective-permute-done.5.refs_6_
  68.6 2.8 %shard_map.44 = f32[19,8,8,128]{3,2,1,0:T(8,128)} custom-call(f32[2,19,16,128]{3,2,1,0:T(8,128)S(1)} %get-tuple-element.34.refs_0_, f32[8,19,16,128]{3,2,1,0:T(8,128)S(1)} %get-tuple-element.35.refs_1_, f32[8,4,16,128]{3,2,1,0:T(8,128)S(1)} %get-tuple-element.36.refs_2_, f32[2,16,128]{2,1,0:T(8,128)S(1)} %get-tuple-element.37.refs_3_, ...), custom_call_target="tpu_custom_call" | custom-call | tf_op jit(solution)/shard_map/pallas_call | solution.py:572
  (1 shorter events, 0.0 us)
Async XLA Ops:
  1.2 13.0 %collective-permute-start = (f32[8,128]{1,0:T(8,128)S(1)}, f32[8,128]{1,0:T(8,128)S(1)}, u32[]{:S(2)}, u32[]{:S(2)}) collective-permute-start(f32[8,128]{1,0:T(8,128)S(1)} %get-tuple-element.25), channel_id=1, source_target_pairs={{0,1},{1,0},{2,3},{3,2},{4,5},{5,4},{6,7},{7,6},{8,9},{9,8},{10,11... | collective-permute-start | bytes 12296 | tf_op jit(solution)/shard_map/ppermute | solution.py:534
  5.4 9.6 %collective-permute-start.1 = (f32[8,128]{1,0:T(8,128)S(1)}, f32[8,128]{1,0:T(8,128)S(1)}, u32[]{:S(2)}, u32[]{:S(2)}) collective-permute-start(f32[8,128]{1,0:T(8,128)S(1)} %get-tuple-element.26), channel_id=1, source_target_pairs={{0,31},{1,2},{2,1},{3,4},{4,3},{5,6},{6,5},{7,8},{8,7},{9,10},{10,... | collective-permute-start | bytes 12296 | tf_op jit(solution)/shard_map/ppermute | solution.py:534
  15.2 42.3 %collective-permute-start.2 = (f32[40,8,128]{2,1,0:T(8,128)S(1)}, f32[40,8,128]{2,1,0:T(8,128)S(1)}, u32[]{:S(2)}, u32[]{:S(2)}) collective-permute-start(f32[40,8,128]{2,1,0:T(8,128)S(1)} %get-tuple-element.32), channel_id=1, source_target_pairs={{0,1},{1,0},{2,3},{3,2},{4,5},{5,4},{6,7},{7,6},{8,9},{9,8},{10,11... | collective-permute-start | bytes 491528 | tf_op jit(solution)/shard_map/ppermute | solution.py:534
  17.2 40.4 %collective-permute-start.3 = (f32[40,8,128]{2,1,0:T(8,128)S(1)}, f32[40,8,128]{2,1,0:T(8,128)S(1)}, u32[]{:S(2)}, u32[]{:S(2)}) collective-permute-start(f32[40,8,128]{2,1,0:T(8,128)S(1)} %get-tuple-element.33), channel_id=1, source_target_pairs={{0,31},{1,2},{2,1},{3,4},{4,3},{5,6},{6,5},{7,8},{8,7},{9,10},{10,... | collective-permute-start | bytes 491528 | tf_op jit(solution)/shard_map/ppermute | solution.py:534
  52.7 15.9 %all-to-all-start.1 = ((f32[32,1,256]{2,1,0:T(1,128)}), f32[32,1,256]{2,1,0:T(1,128)S(1)}, u32[]{:S(2)}, u32[]{:S(2)}) async-start(f32[32,1,256]{2,1,0:T(1,128)} %shard_map.41.after), calls=%async_computation.1 | async-start | bytes 65536 | tf_op jit(solution)/shard_map/all_to_all | solution.py:557
  58.7 9.9 %collective-permute-start.4 = (f32[5,16,128]{2,1,0:T(8,128)S(1)}, f32[5,16,128]{2,1,0:T(8,128)S(1)}, u32[]{:S(2)}, u32[]{:S(2)}) collective-permute-start(f32[5,16,128]{2,1,0:T(8,128)S(1)} %shard_map.42.after), channel_id=1, source_target_pairs={{0,32},{32,0},{64,96},{96,64},{128,160},{160,128},{192,224},{224,1... | collective-permute-start | bytes 122888 | tf_op jit(solution)/shard_map/ppermute | solution.py:534
  61.3 7.3 %collective-permute-start.5 = (f32[5,16,128]{2,1,0:T(8,128)S(1)}, f32[5,16,128]{2,1,0:T(8,128)S(1)}, u32[]{:S(2)}, u32[]{:S(2)}) collective-permute-start(f32[5,16,128]{2,1,0:T(8,128)S(1)} %shard_map.42.after), channel_id=1, source_target_pairs={{0,992},{32,64},{64,32},{96,128},{128,96},{160,192},{192,160},{224... | collective-permute-start | bytes 122888 | tf_op jit(solution)/shard_map/ppermute | solution.py:534

commit v5 on v4

--- a/solution.py
+++ b/solution.py
@@ -182,15 +182,25 @@
         copy.wait()
 
 
-def pack_rows(pops, inflow, after, first, second):
+def pack(pops, solid, inflow, first, second, columns):
     odd = is_odd("gz")
-    values = [(q * PLANES + y, pops[q, y]) for q in range(Q) for y in range(PLANES)]
-    values += [(INFLOW_SLOT + i, inflow[i]) for i in range(len(INCOMING))]
-    for slot, tile in values:
-        low, high = tile[0:2], tile[6:8]
-        place = (slot // 4, slice(2 * (slot % 4), 2 * (slot % 4) + 2))
-        first[place] = jnp.where(odd, low, high)
-        second[place] = jnp.where(odd, high, low)
+    lane = lax.broadcasted_iota(jnp.int32, (8, 128), 1)
+    values = slot_values(pops, solid, inflow)
+    for tile in range(TILES):
+        packed = jnp.zeros((8, 128), jnp.float32)
+        for slot in range(tile * 32, min(tile * 32 + 32, SLOTS)):
+            value = values[slot]()
+            if slot not in (FLAG_SLOT, FLAG_SLOT + 1):
+                low, high = value[0:2], value[6:8]
+                place = (slot // 4, slice(2 * (slot % 4), 2 * (slot % 4) + 2))
+                first[place] = jnp.where(odd, low, high)
+                second[place] = jnp.where(odd, high, low)
+            packed = jnp.where(in_slot(lane, slot), rolled(value, 0, 4 * (slot % 32)), packed)
+        columns[tile] = packed
+
+
+def in_slot(lane, slot):
+    return ((lane + (128 - 4 * (slot % 32) + 2)) & 127) < 4
 
 
 def lay_rows(target, main, odd, one, two):
@@ -344,34 +354,9 @@
 HALVES = (slice(0, 8), slice(8, 16))
 
 
-def pack_columns(pops, solid, inflow, first, second, first_flags, second_flags, after, edges):
+def lay_out(pops, solid, inflow, first, second, first_flags, second_flags, columns, after, rows, flags, entry, edges):
     odd = is_odd("gz")
     lane = lax.broadcasted_iota(jnp.int32, (8, 128), 1)
-    row = lax.broadcasted_iota(jnp.int32, (8, 128), 0)
-    values = slot_values(pops, solid, inflow)
-    for tile in range(TILES):
-        packed = [jnp.zeros((8, 128), jnp.float32)] * 2
-        for slot in range(tile * 32, min(tile * 32 + 32, SLOTS)):
-            offset = 4 * (slot % 32)
-            start = 2 * (slot % 4)
-            if slot in (FLAG_SLOT, FLAG_SLOT + 1):
-                one, two = first_flags[...], second_flags[...]
-                start = 2 * (slot - FLAG_SLOT)
-            else:
-                one, two = first[slot // 4], second[slot // 4]
-            above, below = jnp.where(odd, two, one), jnp.where(odd, one, two)
-            outer = jnp.where(row < 4, rolled(above, -start, 0), rolled(below, 6 - start, 0))
-            place = ((lane + (128 - offset + 2)) & 127) < 4
-            for half, value in enumerate((values[slot](), outer)):
-                packed[half] = jnp.where(place, rolled(value, 0, offset), packed[half])
-        edges[tile, 0:8] = packed[0]
-        edges[tile, 8:16] = packed[1]
-
-
-def prepare(
-    pops, solid, inflow, first, second, first_flags, second_flags, after, kept, relaxed, state, flags, entry, rows
-):
-    odd = is_odd("gz")
     for y in range(2):
         pair = slice(2 * y, 2 * y + 2)
         lay_rows(flags.at[y], solid[y].astype(jnp.float32), odd, first_flags[pair], second_flags[pair])
@@ -380,6 +365,19 @@
     for y in range(PLANES):
         for q in range(Q):
             lay_rows(rows.at[y, q], pops[q, y], odd, *halo_rows(q * PLANES + y, first, second))
+    outer = slice(8, 16)
+    values = [lambda q=q, y=y: rows[y, q, outer] for q in range(Q) for y in range(PLANES)]
+    values += [lambda y=y: flags[y, outer] for y in range(2)]
+    values += [lambda i=i: entry[i, outer] for i in range(len(INCOMING))]
+    for tile in range(TILES):
+        packed = jnp.zeros((8, 128), jnp.float32)
+        for slot in range(tile * 32, min(tile * 32 + 32, SLOTS)):
+            packed = jnp.where(in_slot(lane, slot), rolled(values[slot](), 0, 4 * (slot % 32)), packed)
+        edges[tile, 0:8] = columns[tile]
+        edges[tile, outer] = packed
+
+
+def prepare(rows, after, kept, relaxed, state):
     kept[...] = rows[0:2]
 
     def collide(y, carry):
@@ -514,17 +512,17 @@
         copy.wait()
 
 
-def kernel_call(body, shapes, scratch, *operands, memory=pltpu.VMEM):
+def kernel_call(body, shapes, scratch, *operands, memory=pltpu.VMEM, after=()):
     return pl.pallas_call(
         body,
-        in_specs=[pl.BlockSpec(memory_space=memory)] * len(operands),
+        in_specs=[pl.BlockSpec(memory_space=memory)] * len(operands) + [pl.BlockSpec(memory_space=pl.ANY)] * len(after),
         out_specs=[pl.BlockSpec(memory_space=pltpu.VMEM)] * len(shapes),
         out_shape=[pltpu.VMEM(item, jnp.float32) if isinstance(item, tuple) else item for item in shapes],
         scratch_shapes=[
             pltpu.VMEM(item, jnp.float32) if isinstance(item, tuple) else item for item in scratch
         ],
         compiler_params=pltpu.CompilerParams(vmem_limit_bytes=20 * 1024 * 1024),
-    )(*operands)
+    )(*operands, *after)
 
 
 def swapped(axis, first, second):
@@ -545,30 +543,34 @@
         *(pltpu.with_memory_space_constraint(field, pltpu.HBM) for field in fields),
         memory=pltpu.HBM,
     )
+    block = (pops, solid, top_inflow)
     flags = swapped("gz", *flags)
-    own = kernel_call(tally, [(8, 128)] * 5, [], pops, solid, top_inflow)
+    *rows, columns = kernel_call(pack, [(ROW_TILES, 8, 128)] * 2 + [(TILES, 8, 128)], [], *block)
+    own = kernel_call(tally, [(8, 128)] * 5, [], *block)
     (sums,) = kernel_call(announce, [(along_x, 1, 256)], [], *flags, *own)
-    rows = kernel_call(pack_rows, [(ROW_TILES, 8, 128)] * 2, [], pops, top_inflow, sums)
     sums = lax.all_to_all(sums, "gx", 0, 0, tiled=True)
     halo = swapped("gz", *rows)
     (sums,) = kernel_call(cross, [(along_z, 1, 256)], [], sums.reshape(along_x, 256))
-    block = (pops, solid, top_inflow, *halo, *flags)
-    (edges,) = kernel_call(pack_columns, [(TILES, 16, 128)], [], *block, sums)
+    laid, flags, entry, edges = kernel_call(
+        lay_out,
+        [(PLANES, Q, 16, 128), (2, 16, 128), (len(INCOMING), 16, 128), (TILES, 16, 128)],
+        [],
+        *block,
+        *halo,
+        *flags,
+        columns,
+        after=(sums,),
+    )
     sums = lax.all_to_all(sums, "gz", 0, 0, tiled=True)
     near, far = swapped("gx", edges, edges)
     prepared = kernel_call(
         prepare,
-        [
-            (2, Q, 16, 128),
-            (PLANES, Q, 16, 128),
-            (PLANES, 4, 16, 128),
-            (2, 16, 128),
-            (len(INCOMING), 16, 128),
-        ],
-        [(PLANES, Q, 16, 128)],
-        *block,
-        edges,
+        [(2, Q, 16, 128), (PLANES, Q, 16, 128), (PLANES, 4, 16, 128)],
+        [],
+        laid,
+        after=(edges,),
     )
+    prepared = (*prepared, flags, entry)
     (advanced,) = pl.pallas_call(
         lambda *refs: advance(node_total, *refs),
         in_specs=[pl.BlockSpec(memory_space=pltpu.VMEM)] * 8,

time: 71.9 us -> 71.8 us (level)
  waiting for transfers between devices: 4.93 us -> 9.73 us
  starting transfers between devices: 32.1 us -> 28.2 us
  Pallas kernels: 7.12 us -> 6.22 us
    ppermute x3, starting transfers between devices: 18.6 us -> 14.8 us  [swapped(): lax.ppermute(second, axis, others)]
    ppermute x3, waiting for transfers between devices: 0.7 us -> 4.48 us  [swapped(): lax.ppermute(second, axis, others)]
    all_to_all x1, waiting for transfers between devices: 4.22 us -> 5.25 us  [local(): sums = lax.all_to_all(sums, 'gz', 0, 0, tiled=True)]
    pallas_call x7, Pallas kernels: 4.32 us -> 3.43 us  [kernel_call(): pl.pallas_call(body, in_specs=[pl.BlockSpec(memory_space=memory)] * len(o...]
  transfers between devices with their start and end apart: 7 -> 7, of which waited for: 2 -> 2; matrix products, arithmetic and copies ran while one was open for 0% -> 0% of each run, Pallas kernels for 4% -> 3%
where the time goes in v5:
time: 71.8 us; the launch traced here: 71.4 us
  starting transfers between devices  28.2 us (39%)
  blocking collectives  27.2 us (38%)
  waiting for transfers between devices  9.73 us (14%)
  Pallas kernels  6.22 us (9%)
    all_to_all x1, blocking collectives, local(): sums = lax.all_to_all(sums, 'gx', 0, 0, tiled=True)  27.2 us
    ppermute x3, starting transfers between devices, swapped(): lax.ppermute(second, axis, others)  14.8 us
    ppermute x3, starting transfers between devices, swapped(): lax.ppermute(first, axis, pairs)  8.66 us
    all_to_all x1, waiting for transfers between devices, local(): sums = lax.all_to_all(sums, 'gz', 0, 0, tiled=True)  5.25 us
    all_to_all x1, starting transfers between devices, local(): sums = lax.all_to_all(sums, 'gz', 0, 0, tiled=True)  4.72 us
    ppermute x3, waiting for transfers between devices, swapped(): lax.ppermute(second, axis, others)  4.48 us
    pallas_call x7, Pallas kernels, kernel_call(): pl.pallas_call(body, in_specs=[pl.BlockSpec(memory_space=memory)] * len(o...  3.43 us
    pallas_call x1, Pallas kernels, local(): pl.pallas_call(lambda *refs: advance(node_total, *refs), in_specs=[pl.Blo...  2.79 us
  transfers between devices with their start and end apart: 7, of which 2 were waited for; matrix products, arithmetic and copies ran while one was open for 0% of the time, Pallas kernels for 3%

profile of v5, /device:TPU:1, one launch (start us, length us, event | category | flops | bytes accessed | tf_op | source)
XLA Modules:
  0.0 71.4 jit_solution(18297155775338382694)
XLA Ops:
  0.0 1.2 %shard_map.37 = (f32[8,128]{1,0:T(8,128)S(1)}, f32[8,128]{1,0:T(8,128)S(1)}, f32[19,8,8,128]{3,2,1,0:T(8,128)S(1)}, s32[8,8,128]{2,1,0:T(8,128)S(1)}, f32[5,8,128]{2,1,0:T(8,128)S(1)}) custom-call(f32[19,8,8,128]{3,2,1,0:T(8,128)} %pops_hbm.1, s32[8,8,128]{2,1,0:T(8,128)} %solid_hbm.1, f32[5,8,128]{2,1,0:T(8,128)} %inflow_hbm.1), custom_call_target="tpu_custom_call" | custom-call | tf_op jit(solution)/shard_map/pallas_call | solution.py:516
  1.2 0.3 shard_map.38
  1.5 4.1 %collective-permute-start = (f32[40,8,128]{2,1,0:T(8,128)S(1)}, f32[40,8,128]{2,1,0:T(8,128)S(1)}, u32[]{:S(2)}, u32[]{:S(2)}) collective-permute-start(f32[40,8,128]{2,1,0:T(8,128)S(1)} %get-tuple-element.28), channel_id=1, source_target_pairs={{0,1},{1,0},{2,3},{3,2},{4,5},{5,4},{6,7},{7,6},{8,9},{9,8},{10,11... | collective-permute-start | bytes 491528 | tf_op jit(solution)/shard_map/ppermute | solution.py:532
  5.6 8.6 %collective-permute-start.1 = (f32[40,8,128]{2,1,0:T(8,128)S(1)}, f32[40,8,128]{2,1,0:T(8,128)S(1)}, u32[]{:S(2)}, u32[]{:S(2)}) collective-permute-start(f32[40,8,128]{2,1,0:T(8,128)S(1)} %get-tuple-element.29), channel_id=1, source_target_pairs={{0,31},{1,2},{2,1},{3,4},{4,3},{5,6},{6,5},{7,8},{8,7},{9,10},{10,... | collective-permute-start | bytes 491528 | tf_op jit(solution)/shard_map/ppermute | solution.py:532
  14.3 1.9 %collective-permute-start.2 = (f32[8,128]{1,0:T(8,128)S(1)}, f32[8,128]{1,0:T(8,128)S(1)}, u32[]{:S(2)}, u32[]{:S(2)}) collective-permute-start(f32[8,128]{1,0:T(8,128)S(1)} %get-tuple-element.30), channel_id=1, source_target_pairs={{0,1},{1,0},{2,3},{3,2},{4,5},{5,4},{6,7},{7,6},{8,9},{9,8},{10,11... | collective-permute-start | bytes 12296 | tf_op jit(solution)/shard_map/ppermute | solution.py:532
  16.2 3.8 %collective-permute-start.3 = (f32[8,128]{1,0:T(8,128)S(1)}, f32[8,128]{1,0:T(8,128)S(1)}, u32[]{:S(2)}, u32[]{:S(2)}) collective-permute-start(f32[8,128]{1,0:T(8,128)S(1)} %get-tuple-element.31), channel_id=1, source_target_pairs={{0,31},{1,2},{2,1},{3,4},{4,3},{5,6},{6,5},{7,8},{8,7},{9,10},{10,... | collective-permute-start | bytes 12296 | tf_op jit(solution)/shard_map/ppermute | solution.py:532
  20.0 0.3 shard_map.39
  20.3 0.0 collective-permute-done.2.first.first_flags
  20.3 4.5 %collective-permute-done.3.second.second_flags = f32[8,128]{1,0:T(8,128)S(1)} collective-permute-done((f32[8,128]{1,0:T(8,128)S(1)}, f32[8,128]{1,0:T(8,128)S(1)}, u32[]{:S(2)}, u32[]{:S(2)}) %collective-permute-start.3) | collective-permute-done | bytes 4128 | tf_op jit(solution)/shard_map/ppermute | solution.py:532
  24.8 0.1 shard_map.40
  24.9 27.2 %all_to_all.10 = f32[32,1,256]{2,1,0:T(1,128)S(1)} all-to-all(f32[32,1,256]{2,1,0:T(1,128)S(1)} %shard_map.40), channel_id=1, replica_groups=mesh['gx'=32,'gz'=32] {'gx'}, dimensions={0} | all-to-all | bytes 65536 | tf_op jit(solution)/shard_map/all_to_all | solution.py:551
  52.1 0.7 %shard_map.41.after = f32[32,1,256]{2,1,0:T(1,128)} custom-call(f32[32,256]{1,0:T(8,128)S(1)} %bitcast.3), custom_call_target="tpu_custom_call" | custom-call | tf_op jit(solution)/shard_map/pallas_call | solution.py:516
  52.8 4.7 %all-to-all-start.1 = ((f32[32,1,256]{2,1,0:T(1,128)}), f32[32,1,256]{2,1,0:T(1,128)S(1)}, u32[]{:S(2)}, u32[]{:S(2)}) async-start(f32[32,1,256]{2,1,0:T(1,128)} %shard_map.41.after), calls=%async_computation.1 | async-start | bytes 65536 | tf_op jit(solution)/shard_map/all_to_all | solution.py:564
  57.5 0.0 collective-permute-done.first
  57.5 0.0 collective-permute-done.1.second
  57.5 0.3 shard_map.42
  57.9 2.6 %collective-permute-start.4 = (f32[5,16,128]{2,1,0:T(8,128)S(1)}, f32[5,16,128]{2,1,0:T(8,128)S(1)}, u32[]{:S(2)}, u32[]{:S(2)}) collective-permute-start(f32[5,16,128]{2,1,0:T(8,128)S(1)} %get-tuple-element.39.after), channel_id=1, source_target_pairs={{0,32},{32,0},{64,96},{96,64},{128,160},{160,128},{192,224},{224,1... | collective-permute-start | bytes 122888 | tf_op jit(solution)/shard_map/ppermute | solution.py:532
  60.5 2.4 %collective-permute-start.5 = (f32[5,16,128]{2,1,0:T(8,128)S(1)}, f32[5,16,128]{2,1,0:T(8,128)S(1)}, u32[]{:S(2)}, u32[]{:S(2)}) collective-permute-start(f32[5,16,128]{2,1,0:T(8,128)S(1)} %get-tuple-element.39.after), channel_id=1, source_target_pairs={{0,992},{32,64},{64,32},{96,128},{128,96},{160,192},{192,160},{224... | collective-permute-start | bytes 122888 | tf_op jit(solution)/shard_map/ppermute | solution.py:532
  62.8 0.5 shard_map.43
  63.4 5.2 %all-to-all-done.1.refs_7_ = f32[32,1,256]{2,1,0:T(1,128)S(1)} async-done(((f32[32,1,256]{2,1,0:T(1,128)}), f32[32,1,256]{2,1,0:T(1,128)S(1)}, u32[]{:S(2)}, u32[]{:S(2)}) %all-to-all-start.1) | async-done | bytes 32800 | tf_op jit(solution)/shard_map/all_to_all | solution.py:564
  68.6 0.0 collective-permute-done.4.refs_5_
  68.6 0.0 collective-permute-done.5.refs_6_
  68.6 2.8 %shard_map.44 = f32[19,8,8,128]{3,2,1,0:T(8,128)} custom-call(f32[2,19,16,128]{3,2,1,0:T(8,128)S(1)} %get-tuple-element.40.refs_0_, f32[8,19,16,128]{3,2,1,0:T(8,128)S(1)} %get-tuple-element.41.refs_1_, f32[8,4,16,128]{3,2,1,0:T(8,128)S(1)} %get-tuple-element.42.refs_2_, f32[2,16,128]{2,1,0:T(8,128)S(1)} %get-tuple-element.43.refs_3_, ...), custom_call_target="tpu_custom_call" | custom-call | tf_op jit(solution)/shard_map/pallas_call | solution.py:574
  (1 shorter events, 0.0 us)
Async XLA Ops:
  1.5 56.0 %collective-permute-start = (f32[40,8,128]{2,1,0:T(8,128)S(1)}, f32[40,8,128]{2,1,0:T(8,128)S(1)}, u32[]{:S(2)}, u32[]{:S(2)}) collective-permute-start(f32[40,8,128]{2,1,0:T(8,128)S(1)} %get-tuple-element.28), channel_id=1, source_target_pairs={{0,1},{1,0},{2,3},{3,2},{4,5},{5,4},{6,7},{7,6},{8,9},{9,8},{10,11... | collective-permute-start | bytes 491528 | tf_op jit(solution)/shard_map/ppermute | solution.py:532
  5.6 51.9 %collective-permute-start.1 = (f32[40,8,128]{2,1,0:T(8,128)S(1)}, f32[40,8,128]{2,1,0:T(8,128)S(1)}, u32[]{:S(2)}, u32[]{:S(2)}) collective-permute-start(f32[40,8,128]{2,1,0:T(8,128)S(1)} %get-tuple-element.29), channel_id=1, source_target_pairs={{0,31},{1,2},{2,1},{3,4},{4,3},{5,6},{6,5},{7,8},{8,7},{9,10},{10,... | collective-permute-start | bytes 491528 | tf_op jit(solution)/shard_map/ppermute | solution.py:532
  14.3 6.0 %collective-permute-start.2 = (f32[8,128]{1,0:T(8,128)S(1)}, f32[8,128]{1,0:T(8,128)S(1)}, u32[]{:S(2)}, u32[]{:S(2)}) collective-permute-start(f32[8,128]{1,0:T(8,128)S(1)} %get-tuple-element.30), channel_id=1, source_target_pairs={{0,1},{1,0},{2,3},{3,2},{4,5},{5,4},{6,7},{7,6},{8,9},{9,8},{10,11... | collective-permute-start | bytes 12296 | tf_op jit(solution)/shard_map/ppermute | solution.py:532
  16.2 8.6 %collective-permute-start.3 = (f32[8,128]{1,0:T(8,128)S(1)}, f32[8,128]{1,0:T(8,128)S(1)}, u32[]{:S(2)}, u32[]{:S(2)}) collective-permute-start(f32[8,128]{1,0:T(8,128)S(1)} %get-tuple-element.31), channel_id=1, source_target_pairs={{0,31},{1,2},{2,1},{3,4},{4,3},{5,6},{6,5},{7,8},{8,7},{9,10},{10,... | collective-permute-start | bytes 12296 | tf_op jit(solution)/shard_map/ppermute | solution.py:532
  52.8 15.8 %all-to-all-start.1 = ((f32[32,1,256]{2,1,0:T(1,128)}), f32[32,1,256]{2,1,0:T(1,128)S(1)}, u32[]{:S(2)}, u32[]{:S(2)}) async-start(f32[32,1,256]{2,1,0:T(1,128)} %shard_map.41.after), calls=%async_computation.1 | async-start | bytes 65536 | tf_op jit(solution)/shard_map/all_to_all | solution.py:564
  57.9 10.8 %collective-permute-start.4 = (f32[5,16,128]{2,1,0:T(8,128)S(1)}, f32[5,16,128]{2,1,0:T(8,128)S(1)}, u32[]{:S(2)}, u32[]{:S(2)}) collective-permute-start(f32[5,16,128]{2,1,0:T(8,128)S(1)} %get-tuple-element.39.after), channel_id=1, source_target_pairs={{0,32},{32,0},{64,96},{96,64},{128,160},{160,128},{192,224},{224,1... | collective-permute-start | bytes 122888 | tf_op jit(solution)/shard_map/ppermute | solution.py:532
  60.5 8.2 %collective-permute-start.5 = (f32[5,16,128]{2,1,0:T(8,128)S(1)}, f32[5,16,128]{2,1,0:T(8,128)S(1)}, u32[]{:S(2)}, u32[]{:S(2)}) collective-permute-start(f32[5,16,128]{2,1,0:T(8,128)S(1)} %get-tuple-element.39.after), channel_id=1, source_target_pairs={{0,992},{32,64},{64,32},{96,128},{128,96},{160,192},{192,160},{224... | collective-permute-start | bytes 122888 | tf_op jit(solution)/shard_map/ppermute | solution.py:532

commit v6 on v5

--- a/solution.py
+++ b/solution.py
@@ -392,11 +392,21 @@
     lax.fori_loop(0, PLANES, collide, 0)
 
 
-def advance(
-    node_total, kept, relaxed, state, flags, entry, near, far, sums,
-    out_hbm, out, moved, now, moved_side, now_side, hits, hits_side, done,
-):
-    drive, drive_later = drives(sums[...], node_total)
+def sideways(value, q, source):
+    cx, _, cz = LATTICE[q]
+    lane = lax.broadcasted_iota(jnp.int32, (16, 128), 1)
+    lane_to = 0 if cx > 0 else 127
+    return lane == lane_to, rolled(value, cz, lane_to - (4 * source - (1 if cx > 0 else 0)))
+
+
+def inward(q, source):
+    cx, cy, _ = LATTICE[q]
+    lane = lax.broadcasted_iota(jnp.int32, (16, 128), 1)
+    lane_to = 4 * (source + cy) - (0 if cx > 0 else 1)
+    return lane == lane_to % 128, lane_to - (127 if cx > 0 else 0)
+
+
+def lay_side(flags, near, far, hits, hits_side, flags_side_out, now_side, entry_side, relaxed_side, state_side):
     odd = is_odd("gx")
     lane = lax.broadcasted_iota(jnp.int32, (16, 128), 1)
     edges = []
@@ -406,20 +416,11 @@
         edges.append(jnp.where((lane & 3) < 2, high, low))
     for q in range(Q):
         now_side[q] = rolled(edges[q // 4], 0, -32 * (q % 4))
-    wall = ((lane + 2) & 127) < 8
-    flags_side = jnp.where(wall, rolled(edges[4], 0, -96), 0.0)
-    stay_side = flags_side > 0.5
-
-    def sideways(value, q, source):
-        cx, _, cz = LATTICE[q]
-        lane_to = 0 if cx > 0 else 127
-        return lane == lane_to, rolled(value, cz, lane_to - (4 * source - (1 if cx > 0 else 0)))
-
-    def inward(q, source):
-        cx, cy, _ = LATTICE[q]
-        lane_to = 4 * (source + cy) - (0 if cx > 0 else 1)
-        return lane == lane_to % 128, lane_to - (127 if cx > 0 else 0)
-
+    for i in range(len(INCOMING)):
+        slot = (INFLOW_SLOT + i) % 32
+        entry_side[i] = rolled(edges[INFLOW_SLOT // 32], 0, 4 * (PLANES - 1) - 4 * slot)
+    flags_side = jnp.where(((lane + 2) & 127) < 8, rolled(edges[4], 0, -96), 0.0)
+    flags_side_out[...] = flags_side
     for q in range(Q):
         cx, cy, cz = LATTICE[q]
         for source in range(2):
@@ -436,6 +437,20 @@
         if cy > 0:
             hit = jnp.where(((lane + 2) & 127) < 4, 1.0, hit)
         hits_side[q] = hit
+    for half in HALVES:
+        result, velocity, inv = relax([now_side[q, half] for q in range(Q)])
+        for q in range(Q):
+            relaxed_side[q, half] = result[q]
+        for i, value in enumerate(velocity + (inv,)):
+            state_side[i, half] = value
+
+
+def advance(
+    node_total, kept, relaxed, state, flags, entry, hits, hits_side, flags_side, first_side, entry_side,
+    relaxed_side, state_side, sums, out_hbm, out, moved, now, moved_side, now_side, done,
+):
+    drive, drive_later = drives(sums[...], node_total)
+    lane = lax.broadcasted_iota(jnp.int32, (16, 128), 1)
 
     def push(y, carry):
         for half in HALVES:
@@ -452,9 +467,16 @@
                 moved[y, q, half] = result[q]
         return carry
 
-    def collide_side(applied):
+    def push_side():
         for half in HALVES:
-            result = driven(*relax([now_side[q, half] for q in range(Q)]), applied)
+            velocity = tuple(state_side[i, half] for i in range(3))
+            result = driven([relaxed_side[q, half] for q in range(Q)], velocity, state_side[3, half], drive)
+            for q in range(Q):
+                moved_side[q, half] = result[q]
+
+    def collide_side():
+        for half in HALVES:
+            result = driven(*relax([now_side[q, half] for q in range(Q)]), drive_later)
             for q in range(Q):
                 moved_side[q, half] = result[q]
 
@@ -488,20 +510,18 @@
                     arrived = jnp.where(edge, rolled(moved[source, q], cz, shift), arrived)
         arrived = jnp.where(hits_side[q] > 0.5, moved_side[OPPOSITE[q]], arrived)
         if cy < 0:
-            slot = (INFLOW_SLOT + INCOMING.index(q)) % 32
-            value = rolled(edges[INFLOW_SLOT // 32], 0, 4 * (PLANES - 1) - 4 * slot)
-            arrived = jnp.where(((lane - 26) & 127) < 4, value, arrived)
-        return jnp.where(stay_side, now_side[q], arrived)
+            arrived = jnp.where(((lane - 26) & 127) < 4, entry_side[INCOMING.index(q)], arrived)
+        return jnp.where(flags_side[...] > 0.5, first_side[q], arrived)
 
     lax.fori_loop(0, PLANES, push, 0)
-    collide_side(drive)
+    push_side()
     for y in range(PLANES):
         for q in range(Q):
             now[y, q] = arrive(y, q, slice(0, 16))
     for q in range(Q):
         now_side[q] = arrive_side(q)
     lax.fori_loop(0, PLANES, collide, 0)
-    collide_side(drive_later)
+    collide_side()
     copies = []
     for y in range(PLANES):
         for q in range(Q):
@@ -570,24 +590,31 @@
         laid,
         after=(edges,),
     )
-    prepared = (*prepared, flags, entry)
+    tile = (16, 128)
+    side = kernel_call(
+        lay_side,
+        [(2, Q) + tile, (Q,) + tile, tile, (Q,) + tile, (len(INCOMING),) + tile, (Q,) + tile, (4,) + tile],
+        [],
+        flags,
+        near,
+        far,
+    )
+    operands = (*prepared, flags, entry, *side, sums)
     (advanced,) = pl.pallas_call(
         lambda *refs: advance(node_total, *refs),
-        in_specs=[pl.BlockSpec(memory_space=pltpu.VMEM)] * 8,
+        in_specs=[pl.BlockSpec(memory_space=pltpu.VMEM)] * len(operands),
         out_specs=[pl.BlockSpec(memory_space=pltpu.HBM)],
         out_shape=[jax.ShapeDtypeStruct((Q, PLANES, 8, 128), jnp.float32)],
         scratch_shapes=[
             pltpu.VMEM((PLANES, Q, 8, 128), jnp.float32),
-            pltpu.VMEM((PLANES, Q, 16, 128), jnp.float32),
-            pltpu.VMEM((PLANES, Q, 16, 128), jnp.float32),
-            pltpu.VMEM((Q, 16, 128), jnp.float32),
-            pltpu.VMEM((Q, 16, 128), jnp.float32),
-            pltpu.VMEM((2, Q, 16, 128), jnp.float32),
-            pltpu.VMEM((Q, 16, 128), jnp.float32),
+            pltpu.VMEM((PLANES, Q) + tile, jnp.float32),
+            pltpu.VMEM((PLANES, Q) + tile, jnp.float32),
+            pltpu.VMEM((Q,) + tile, jnp.float32),
+            pltpu.VMEM((Q,) + tile, jnp.float32),
             pltpu.SemaphoreType.DMA((PLANES,)),
         ],
         compiler_params=pltpu.CompilerParams(vmem_limit_bytes=20 * 1024 * 1024),
-    )(*prepared, near, far, sums)
+    )(*operands)
     return advanced
 
 

time: 71.8 us -> 71.6 us (level)
    all_to_all x1, waiting for transfers between devices: 5.25 us -> 4.29 us  [local(): sums = lax.all_to_all(sums, 'gz', 0, 0, tiled=True)]
    pallas_call x7 -> x8, Pallas kernels: 3.43 us -> 3.73 us  [kernel_call(): pl.pallas_call(body, in_specs=[pl.BlockSpec(memory_space=memory)] * len(o...]
  transfers between devices with their start and end apart: 7 -> 7, of which waited for: 2 -> 4; matrix products, arithmetic and copies ran while one was open for 0% -> 0% of each run, Pallas kernels for 3% -> 3%
where the time goes in v6:
time: 71.6 us; the launch traced here: 71.2 us
  starting transfers between devices  28.2 us (39%)
  blocking collectives  27.2 us (38%)
  waiting for transfers between devices  9.42 us (13%)
  Pallas kernels  6.32 us (9%)
    all_to_all x1, blocking collectives, local(): sums = lax.all_to_all(sums, 'gx', 0, 0, tiled=True)  27.2 us
    ppermute x3, starting transfers between devices, swapped(): lax.ppermute(second, axis, others)  15.5 us
    ppermute x3, starting transfers between devices, swapped(): lax.ppermute(first, axis, pairs)  7.97 us
    ppermute x3, waiting for transfers between devices, swapped(): lax.ppermute(second, axis, others)  4.89 us
    all_to_all x1, starting transfers between devices, local(): sums = lax.all_to_all(sums, 'gz', 0, 0, tiled=True)  4.72 us
    all_to_all x1, waiting for transfers between devices, local(): sums = lax.all_to_all(sums, 'gz', 0, 0, tiled=True)  4.29 us
    pallas_call x8, Pallas kernels, kernel_call(): pl.pallas_call(body, in_specs=[pl.BlockSpec(memory_space=memory)] * len(o...  3.73 us
    pallas_call x1, Pallas kernels, local(): pl.pallas_call(lambda *refs: advance(node_total, *refs), in_specs=[pl.Blo...  2.58 us
  transfers between devices with their start and end apart: 7, of which 4 were waited for; matrix products, arithmetic and copies ran while one was open for 0% of the time, Pallas kernels for 3%

profile of v6, /device:TPU:1, one launch (start us, length us, event | category | flops | bytes accessed | tf_op | source)
XLA Modules:
  0.0 71.2 jit_solution(11915790644405450186)
XLA Ops:
  0.0 1.2 %shard_map.37 = (f32[8,128]{1,0:T(8,128)S(1)}, f32[8,128]{1,0:T(8,128)S(1)}, f32[19,8,8,128]{3,2,1,0:T(8,128)S(1)}, s32[8,8,128]{2,1,0:T(8,128)S(1)}, f32[5,8,128]{2,1,0:T(8,128)S(1)}) custom-call(f32[19,8,8,128]{3,2,1,0:T(8,128)} %pops_hbm.1, s32[8,8,128]{2,1,0:T(8,128)} %solid_hbm.1, f32[5,8,128]{2,1,0:T(8,128)} %inflow_hbm.1), custom_call_target="tpu_custom_call" | custom-call | tf_op jit(solution)/shard_map/pallas_call | solution.py:536
  1.2 0.3 shard_map.38
  1.5 4.1 %collective-permute-start = (f32[40,8,128]{2,1,0:T(8,128)S(1)}, f32[40,8,128]{2,1,0:T(8,128)S(1)}, u32[]{:S(2)}, u32[]{:S(2)}) collective-permute-start(f32[40,8,128]{2,1,0:T(8,128)S(1)} %get-tuple-element.35), channel_id=1, source_target_pairs={{0,1},{1,0},{2,3},{3,2},{4,5},{5,4},{6,7},{7,6},{8,9},{9,8},{10,11... | collective-permute-start | bytes 491528 | tf_op jit(solution)/shard_map/ppermute | solution.py:552
  5.6 8.6 %collective-permute-start.1 = (f32[40,8,128]{2,1,0:T(8,128)S(1)}, f32[40,8,128]{2,1,0:T(8,128)S(1)}, u32[]{:S(2)}, u32[]{:S(2)}) collective-permute-start(f32[40,8,128]{2,1,0:T(8,128)S(1)} %get-tuple-element.36), channel_id=1, source_target_pairs={{0,31},{1,2},{2,1},{3,4},{4,3},{5,6},{6,5},{7,8},{8,7},{9,10},{10,... | collective-permute-start | bytes 491528 | tf_op jit(solution)/shard_map/ppermute | solution.py:552
  14.3 1.9 %collective-permute-start.2 = (f32[8,128]{1,0:T(8,128)S(1)}, f32[8,128]{1,0:T(8,128)S(1)}, u32[]{:S(2)}, u32[]{:S(2)}) collective-permute-start(f32[8,128]{1,0:T(8,128)S(1)} %get-tuple-element.37), channel_id=1, source_target_pairs={{0,1},{1,0},{2,3},{3,2},{4,5},{5,4},{6,7},{7,6},{8,9},{9,8},{10,11... | collective-permute-start | bytes 12296 | tf_op jit(solution)/shard_map/ppermute | solution.py:552
  16.2 3.8 %collective-permute-start.3 = (f32[8,128]{1,0:T(8,128)S(1)}, f32[8,128]{1,0:T(8,128)S(1)}, u32[]{:S(2)}, u32[]{:S(2)}) collective-permute-start(f32[8,128]{1,0:T(8,128)S(1)} %get-tuple-element.38), channel_id=1, source_target_pairs={{0,31},{1,2},{2,1},{3,4},{4,3},{5,6},{6,5},{7,8},{8,7},{9,10},{10,... | collective-permute-start | bytes 12296 | tf_op jit(solution)/shard_map/ppermute | solution.py:552
  20.0 0.3 shard_map.39
  20.3 0.0 collective-permute-done.2.first.first_flags
  20.3 4.5 %collective-permute-done.3.second.second_flags = f32[8,128]{1,0:T(8,128)S(1)} collective-permute-done((f32[8,128]{1,0:T(8,128)S(1)}, f32[8,128]{1,0:T(8,128)S(1)}, u32[]{:S(2)}, u32[]{:S(2)}) %collective-permute-start.3) | collective-permute-done | bytes 4128 | tf_op jit(solution)/shard_map/ppermute | solution.py:552
  24.8 0.1 shard_map.40
  24.9 27.2 %all_to_all.10 = f32[32,1,256]{2,1,0:T(1,128)S(1)} all-to-all(f32[32,1,256]{2,1,0:T(1,128)S(1)} %shard_map.40), channel_id=1, replica_groups=mesh['gx'=32,'gz'=32] {'gx'}, dimensions={0} | all-to-all | bytes 65536 | tf_op jit(solution)/shard_map/all_to_all | solution.py:571
  52.1 0.7 %shard_map.41.after = f32[32,1,256]{2,1,0:T(1,128)} custom-call(f32[32,256]{1,0:T(8,128)S(1)} %bitcast.3), custom_call_target="tpu_custom_call" | custom-call | tf_op jit(solution)/shard_map/pallas_call | solution.py:536
  52.8 4.7 %all-to-all-start.1 = ((f32[32,1,256]{2,1,0:T(1,128)}), f32[32,1,256]{2,1,0:T(1,128)S(1)}, u32[]{:S(2)}, u32[]{:S(2)}) async-start(f32[32,1,256]{2,1,0:T(1,128)} %shard_map.41.after), calls=%async_computation.1 | async-start | bytes 65536 | tf_op jit(solution)/shard_map/all_to_all | solution.py:584
  57.5 0.0 collective-permute-done.first
  57.5 0.0 collective-permute-done.1.second
  57.5 0.3 shard_map.42
  57.9 3.1 %collective-permute-start.5 = (f32[5,16,128]{2,1,0:T(8,128)S(1)}, f32[5,16,128]{2,1,0:T(8,128)S(1)}, u32[]{:S(2)}, u32[]{:S(2)}) collective-permute-start(f32[5,16,128]{2,1,0:T(8,128)S(1)} %get-tuple-element.46.after), channel_id=1, source_target_pairs={{0,992},{32,64},{64,32},{96,128},{128,96},{160,192},{192,160},{224... | collective-permute-start | bytes 122888 | tf_op jit(solution)/shard_map/ppermute | solution.py:552
  60.9 1.9 %collective-permute-start.4 = (f32[5,16,128]{2,1,0:T(8,128)S(1)}, f32[5,16,128]{2,1,0:T(8,128)S(1)}, u32[]{:S(2)}, u32[]{:S(2)}) collective-permute-start(f32[5,16,128]{2,1,0:T(8,128)S(1)} %get-tuple-element.46.after), channel_id=1, source_target_pairs={{0,32},{32,0},{64,96},{96,64},{128,160},{160,128},{192,224},{224,1... | collective-permute-start | bytes 122888 | tf_op jit(solution)/shard_map/ppermute | solution.py:552
  62.8 0.5 shard_map.43
  63.4 0.4 collective-permute-done.5.far
  63.8 0.2 collective-permute-done.4.near
  64.0 0.3 shard_map.44
  64.3 4.3 %all-to-all-done.1.refs_12_ = f32[32,1,256]{2,1,0:T(1,128)S(1)} async-done(((f32[32,1,256]{2,1,0:T(1,128)}), f32[32,1,256]{2,1,0:T(1,128)S(1)}, u32[]{:S(2)}, u32[]{:S(2)}) %all-to-all-start.1) | async-done | bytes 32800 | tf_op jit(solution)/shard_map/all_to_all | solution.py:584
  68.6 2.6 %shard_map.45 = f32[19,8,8,128]{3,2,1,0:T(8,128)} custom-call(f32[2,19,16,128]{3,2,1,0:T(8,128)S(1)} %get-tuple-element.47.refs_0_, f32[8,19,16,128]{3,2,1,0:T(8,128)S(1)} %get-tuple-element.48.refs_1_, f32[8,4,16,128]{3,2,1,0:T(8,128)S(1)} %get-tuple-element.49.refs_2_, f32[2,16,128]{2,1,0:T(8,128)S(1)} %get-tuple-element.50.flags.refs_3_, ...), custom_call_target="tpu_custom_call" | custom-call | tf_op jit(solution)/shard_map/pallas_call | solution.py:603
  (1 shorter events, 0.0 us)
Async XLA Ops:
  1.5 56.0 %collective-permute-start = (f32[40,8,128]{2,1,0:T(8,128)S(1)}, f32[40,8,128]{2,1,0:T(8,128)S(1)}, u32[]{:S(2)}, u32[]{:S(2)}) collective-permute-start(f32[40,8,128]{2,1,0:T(8,128)S(1)} %get-tuple-element.35), channel_id=1, source_target_pairs={{0,1},{1,0},{2,3},{3,2},{4,5},{5,4},{6,7},{7,6},{8,9},{9,8},{10,11... | collective-permute-start | bytes 491528 | tf_op jit(solution)/shard_map/ppermute | solution.py:552
  5.6 51.9 %collective-permute-start.1 = (f32[40,8,128]{2,1,0:T(8,128)S(1)}, f32[40,8,128]{2,1,0:T(8,128)S(1)}, u32[]{:S(2)}, u32[]{:S(2)}) collective-permute-start(f32[40,8,128]{2,1,0:T(8,128)S(1)} %get-tuple-element.36), channel_id=1, source_target_pairs={{0,31},{1,2},{2,1},{3,4},{4,3},{5,6},{6,5},{7,8},{8,7},{9,10},{10,... | collective-permute-start | bytes 491528 | tf_op jit(solution)/shard_map/ppermute | solution.py:552
  14.3 6.0 %collective-permute-start.2 = (f32[8,128]{1,0:T(8,128)S(1)}, f32[8,128]{1,0:T(8,128)S(1)}, u32[]{:S(2)}, u32[]{:S(2)}) collective-permute-start(f32[8,128]{1,0:T(8,128)S(1)} %get-tuple-element.37), channel_id=1, source_target_pairs={{0,1},{1,0},{2,3},{3,2},{4,5},{5,4},{6,7},{7,6},{8,9},{9,8},{10,11... | collective-permute-start | bytes 12296 | tf_op jit(solution)/shard_map/ppermute | solution.py:552
  16.2 8.6 %collective-permute-start.3 = (f32[8,128]{1,0:T(8,128)S(1)}, f32[8,128]{1,0:T(8,128)S(1)}, u32[]{:S(2)}, u32[]{:S(2)}) collective-permute-start(f32[8,128]{1,0:T(8,128)S(1)} %get-tuple-element.38), channel_id=1, source_target_pairs={{0,31},{1,2},{2,1},{3,4},{4,3},{5,6},{6,5},{7,8},{8,7},{9,10},{10,... | collective-permute-start | bytes 12296 | tf_op jit(solution)/shard_map/ppermute | solution.py:552
  52.8 15.8 %all-to-all-start.1 = ((f32[32,1,256]{2,1,0:T(1,128)}), f32[32,1,256]{2,1,0:T(1,128)S(1)}, u32[]{:S(2)}, u32[]{:S(2)}) async-start(f32[32,1,256]{2,1,0:T(1,128)} %shard_map.41.after), calls=%async_computation.1 | async-start | bytes 65536 | tf_op jit(solution)/shard_map/all_to_all | solution.py:584
  57.9 5.9 %collective-permute-start.5 = (f32[5,16,128]{2,1,0:T(8,128)S(1)}, f32[5,16,128]{2,1,0:T(8,128)S(1)}, u32[]{:S(2)}, u32[]{:S(2)}) collective-permute-start(f32[5,16,128]{2,1,0:T(8,128)S(1)} %get-tuple-element.46.after), channel_id=1, source_target_pairs={{0,992},{32,64},{64,32},{96,128},{128,96},{160,192},{192,160},{224... | collective-permute-start | bytes 122888 | tf_op jit(solution)/shard_map/ppermute | solution.py:552
  60.9 3.1 %collective-permute-start.4 = (f32[5,16,128]{2,1,0:T(8,128)S(1)}, f32[5,16,128]{2,1,0:T(8,128)S(1)}, u32[]{:S(2)}, u32[]{:S(2)}) collective-permute-start(f32[5,16,128]{2,1,0:T(8,128)S(1)} %get-tuple-element.46.after), channel_id=1, source_target_pairs={{0,32},{32,0},{64,96},{96,64},{128,160},{160,128},{192,224},{224,1... | collective-permute-start | bytes 122888 | tf_op jit(solution)/shard_map/ppermute | solution.py:552

commit v7 on v6

--- a/solution.py
+++ b/solution.py
@@ -389,7 +389,7 @@
                 state[y, i, half] = value
         return carry
 
-    lax.fori_loop(0, PLANES, collide, 0)
+    lax.fori_loop(0, PLANES, collide, 0, unroll=8)
 
 
 def sideways(value, q, source):
@@ -488,11 +488,12 @@
         elif source >= PLANES:
             arrived = entry[INCOMING.index(q), part]
         else:
-            arrived = rolled(moved[source, q], cz, cx)
+            arrived = rolled(rolled(moved[source, q], cz, 0)[part], 0, cx)
             if cx:
-                edge, value = sideways(moved_side[q], q, source)
-                arrived = jnp.where(edge, value, arrived)
-            arrived = arrived[part]
+                lane_to = 0 if cx > 0 else 127
+                value = rolled(moved_side[q], cz, 0)[part]
+                value = rolled(value, 0, lane_to - (4 * source - (1 if cx > 0 else 0)))
+                arrived = jnp.where(lane[part] == lane_to, value, arrived)
             if source < 2:
                 arrived = jnp.where(hits[source, q, part] > 0.5, moved[y, OPPOSITE[q], part], arrived)
         if y < 2:
@@ -513,14 +514,14 @@
             arrived = jnp.where(((lane - 26) & 127) < 4, entry_side[INCOMING.index(q)], arrived)
         return jnp.where(flags_side[...] > 0.5, first_side[q], arrived)
 
-    lax.fori_loop(0, PLANES, push, 0)
+    lax.fori_loop(0, PLANES, push, 0, unroll=8)
     push_side()
     for y in range(PLANES):
         for q in range(Q):
             now[y, q] = arrive(y, q, slice(0, 16))
     for q in range(Q):
         now_side[q] = arrive_side(q)
-    lax.fori_loop(0, PLANES, collide, 0)
+    lax.fori_loop(0, PLANES, collide, 0, unroll=8)
     collide_side()
     copies = []
     for y in range(PLANES):

time: 71.6 us -> 71 us (level)
  no operation moved by 1% of the time
where the time goes in v7:
time: 71 us; the launch traced here: 70.6 us
  starting transfers between devices  28.2 us (40%)
  blocking collectives  27.2 us (38%)
  waiting for transfers between devices  9.46 us (13%)
  Pallas kernels  5.67 us (8%)
    all_to_all x1, blocking collectives, local(): sums = lax.all_to_all(sums, 'gx', 0, 0, tiled=True)  27.2 us
    ppermute x3, starting transfers between devices, swapped(): lax.ppermute(second, axis, others)  15.5 us
    ppermute x3, starting transfers between devices, swapped(): lax.ppermute(first, axis, pairs)  7.97 us
    ppermute x3, waiting for transfers between devices, swapped(): lax.ppermute(second, axis, others)  4.94 us
    all_to_all x1, starting transfers between devices, local(): sums = lax.all_to_all(sums, 'gz', 0, 0, tiled=True)  4.72 us
    all_to_all x1, waiting for transfers between devices, local(): sums = lax.all_to_all(sums, 'gz', 0, 0, tiled=True)  4.29 us
    pallas_call x8, Pallas kernels, kernel_call(): pl.pallas_call(body, in_specs=[pl.BlockSpec(memory_space=memory)] * len(o...  3.69 us
    pallas_call x1, Pallas kernels, local(): pl.pallas_call(lambda *refs: advance(node_total, *refs), in_specs=[pl.Blo...  1.97 us
  transfers between devices with their start and end apart: 7, of which 4 were waited for; matrix products, arithmetic and copies ran while one was open for 0% of the time, Pallas kernels for 3%

profile of v7, /device:TPU:1, one launch (start us, length us, event | category | flops | bytes accessed | tf_op | source)
XLA Modules:
  0.0 70.6 jit_solution(6164400790114375369)
XLA Ops:
  0.0 1.2 %shard_map.37 = (f32[8,128]{1,0:T(8,128)S(1)}, f32[8,128]{1,0:T(8,128)S(1)}, f32[19,8,8,128]{3,2,1,0:T(8,128)S(1)}, s32[8,8,128]{2,1,0:T(8,128)S(1)}, f32[5,8,128]{2,1,0:T(8,128)S(1)}) custom-call(f32[19,8,8,128]{3,2,1,0:T(8,128)} %pops_hbm.1, s32[8,8,128]{2,1,0:T(8,128)} %solid_hbm.1, f32[5,8,128]{2,1,0:T(8,128)} %inflow_hbm.1), custom_call_target="tpu_custom_call" | custom-call | tf_op jit(solution)/shard_map/pallas_call | solution.py:537
  1.2 0.3 shard_map.38
  1.5 4.1 %collective-permute-start = (f32[40,8,128]{2,1,0:T(8,128)S(1)}, f32[40,8,128]{2,1,0:T(8,128)S(1)}, u32[]{:S(2)}, u32[]{:S(2)}) collective-permute-start(f32[40,8,128]{2,1,0:T(8,128)S(1)} %get-tuple-element.35), channel_id=1, source_target_pairs={{0,1},{1,0},{2,3},{3,2},{4,5},{5,4},{6,7},{7,6},{8,9},{9,8},{10,11... | collective-permute-start | bytes 491528 | tf_op jit(solution)/shard_map/ppermute | solution.py:553
  5.6 8.6 %collective-permute-start.1 = (f32[40,8,128]{2,1,0:T(8,128)S(1)}, f32[40,8,128]{2,1,0:T(8,128)S(1)}, u32[]{:S(2)}, u32[]{:S(2)}) collective-permute-start(f32[40,8,128]{2,1,0:T(8,128)S(1)} %get-tuple-element.36), channel_id=1, source_target_pairs={{0,31},{1,2},{2,1},{3,4},{4,3},{5,6},{6,5},{7,8},{8,7},{9,10},{10,... | collective-permute-start | bytes 491528 | tf_op jit(solution)/shard_map/ppermute | solution.py:553
  14.3 1.9 %collective-permute-start.2 = (f32[8,128]{1,0:T(8,128)S(1)}, f32[8,128]{1,0:T(8,128)S(1)}, u32[]{:S(2)}, u32[]{:S(2)}) collective-permute-start(f32[8,128]{1,0:T(8,128)S(1)} %get-tuple-element.37), channel_id=1, source_target_pairs={{0,1},{1,0},{2,3},{3,2},{4,5},{5,4},{6,7},{7,6},{8,9},{9,8},{10,11... | collective-permute-start | bytes 12296 | tf_op jit(solution)/shard_map/ppermute | solution.py:553
  16.2 3.8 %collective-permute-start.3 = (f32[8,128]{1,0:T(8,128)S(1)}, f32[8,128]{1,0:T(8,128)S(1)}, u32[]{:S(2)}, u32[]{:S(2)}) collective-permute-start(f32[8,128]{1,0:T(8,128)S(1)} %get-tuple-element.38), channel_id=1, source_target_pairs={{0,31},{1,2},{2,1},{3,4},{4,3},{5,6},{6,5},{7,8},{8,7},{9,10},{10,... | collective-permute-start | bytes 12296 | tf_op jit(solution)/shard_map/ppermute | solution.py:553
  20.0 0.3 shard_map.39
  20.3 0.0 collective-permute-done.2.first.first_flags
  20.3 4.5 %collective-permute-done.3.second.second_flags = f32[8,128]{1,0:T(8,128)S(1)} collective-permute-done((f32[8,128]{1,0:T(8,128)S(1)}, f32[8,128]{1,0:T(8,128)S(1)}, u32[]{:S(2)}, u32[]{:S(2)}) %collective-permute-start.3) | collective-permute-done | bytes 4128 | tf_op jit(solution)/shard_map/ppermute | solution.py:553
  24.8 0.1 shard_map.40
  24.9 27.2 %all_to_all.10 = f32[32,1,256]{2,1,0:T(1,128)S(1)} all-to-all(f32[32,1,256]{2,1,0:T(1,128)S(1)} %shard_map.40), channel_id=1, replica_groups=mesh['gx'=32,'gz'=32] {'gx'}, dimensions={0} | all-to-all | bytes 65536 | tf_op jit(solution)/shard_map/all_to_all | solution.py:572
  52.1 0.7 %shard_map.41.after = f32[32,1,256]{2,1,0:T(1,128)} custom-call(f32[32,256]{1,0:T(8,128)S(1)} %bitcast.3), custom_call_target="tpu_custom_call" | custom-call | tf_op jit(solution)/shard_map/pallas_call | solution.py:537
  52.8 4.7 %all-to-all-start.1 = ((f32[32,1,256]{2,1,0:T(1,128)}), f32[32,1,256]{2,1,0:T(1,128)S(1)}, u32[]{:S(2)}, u32[]{:S(2)}) async-start(f32[32,1,256]{2,1,0:T(1,128)} %shard_map.41.after), calls=%async_computation.1 | async-start | bytes 65536 | tf_op jit(solution)/shard_map/all_to_all | solution.py:585
  57.5 0.0 collective-permute-done.first
  57.5 0.0 collective-permute-done.1.second
  57.5 0.3 shard_map.42
  57.9 3.1 %collective-permute-start.5 = (f32[5,16,128]{2,1,0:T(8,128)S(1)}, f32[5,16,128]{2,1,0:T(8,128)S(1)}, u32[]{:S(2)}, u32[]{:S(2)}) collective-permute-start(f32[5,16,128]{2,1,0:T(8,128)S(1)} %get-tuple-element.46.after), channel_id=1, source_target_pairs={{0,992},{32,64},{64,32},{96,128},{128,96},{160,192},{192,160},{224... | collective-permute-start | bytes 122888 | tf_op jit(solution)/shard_map/ppermute | solution.py:553
  60.9 1.9 %collective-permute-start.4 = (f32[5,16,128]{2,1,0:T(8,128)S(1)}, f32[5,16,128]{2,1,0:T(8,128)S(1)}, u32[]{:S(2)}, u32[]{:S(2)}) collective-permute-start(f32[5,16,128]{2,1,0:T(8,128)S(1)} %get-tuple-element.46.after), channel_id=1, source_target_pairs={{0,32},{32,0},{64,96},{96,64},{128,160},{160,128},{192,224},{224,1... | collective-permute-start | bytes 122888 | tf_op jit(solution)/shard_map/ppermute | solution.py:553
  62.8 0.5 shard_map.43
  63.3 0.5 collective-permute-done.5.far
  63.8 0.2 collective-permute-done.4.near
  64.0 0.3 shard_map.44
  64.3 4.3 %all-to-all-done.1.refs_12_ = f32[32,1,256]{2,1,0:T(1,128)S(1)} async-done(((f32[32,1,256]{2,1,0:T(1,128)}), f32[32,1,256]{2,1,0:T(1,128)S(1)}, u32[]{:S(2)}, u32[]{:S(2)}) %all-to-all-start.1) | async-done | bytes 32800 | tf_op jit(solution)/shard_map/all_to_all | solution.py:585
  68.6 2.0 %shard_map.45 = f32[19,8,8,128]{3,2,1,0:T(8,128)} custom-call(f32[2,19,16,128]{3,2,1,0:T(8,128)S(1)} %get-tuple-element.47.refs_0_, f32[8,19,16,128]{3,2,1,0:T(8,128)S(1)} %get-tuple-element.48.refs_1_, f32[8,4,16,128]{3,2,1,0:T(8,128)S(1)} %get-tuple-element.49.refs_2_, f32[2,16,128]{2,1,0:T(8,128)S(1)} %get-tuple-element.50.flags.refs_3_, ...), custom_call_target="tpu_custom_call" | custom-call | tf_op jit(solution)/shard_map/pallas_call | solution.py:604
  (1 shorter events, 0.0 us)
Async XLA Ops:
  1.5 56.0 %collective-permute-start = (f32[40,8,128]{2,1,0:T(8,128)S(1)}, f32[40,8,128]{2,1,0:T(8,128)S(1)}, u32[]{:S(2)}, u32[]{:S(2)}) collective-permute-start(f32[40,8,128]{2,1,0:T(8,128)S(1)} %get-tuple-element.35), channel_id=1, source_target_pairs={{0,1},{1,0},{2,3},{3,2},{4,5},{5,4},{6,7},{7,6},{8,9},{9,8},{10,11... | collective-permute-start | bytes 491528 | tf_op jit(solution)/shard_map/ppermute | solution.py:553
  5.6 51.9 %collective-permute-start.1 = (f32[40,8,128]{2,1,0:T(8,128)S(1)}, f32[40,8,128]{2,1,0:T(8,128)S(1)}, u32[]{:S(2)}, u32[]{:S(2)}) collective-permute-start(f32[40,8,128]{2,1,0:T(8,128)S(1)} %get-tuple-element.36), channel_id=1, source_target_pairs={{0,31},{1,2},{2,1},{3,4},{4,3},{5,6},{6,5},{7,8},{8,7},{9,10},{10,... | collective-permute-start | bytes 491528 | tf_op jit(solution)/shard_map/ppermute | solution.py:553
  14.3 6.0 %collective-permute-start.2 = (f32[8,128]{1,0:T(8,128)S(1)}, f32[8,128]{1,0:T(8,128)S(1)}, u32[]{:S(2)}, u32[]{:S(2)}) collective-permute-start(f32[8,128]{1,0:T(8,128)S(1)} %get-tuple-element.37), channel_id=1, source_target_pairs={{0,1},{1,0},{2,3},{3,2},{4,5},{5,4},{6,7},{7,6},{8,9},{9,8},{10,11... | collective-permute-start | bytes 12296 | tf_op jit(solution)/shard_map/ppermute | solution.py:553
  16.2 8.6 %collective-permute-start.3 = (f32[8,128]{1,0:T(8,128)S(1)}, f32[8,128]{1,0:T(8,128)S(1)}, u32[]{:S(2)}, u32[]{:S(2)}) collective-permute-start(f32[8,128]{1,0:T(8,128)S(1)} %get-tuple-element.38), channel_id=1, source_target_pairs={{0,31},{1,2},{2,1},{3,4},{4,3},{5,6},{6,5},{7,8},{8,7},{9,10},{10,... | collective-permute-start | bytes 12296 | tf_op jit(solution)/shard_map/ppermute | solution.py:553
  52.8 15.8 %all-to-all-start.1 = ((f32[32,1,256]{2,1,0:T(1,128)}), f32[32,1,256]{2,1,0:T(1,128)S(1)}, u32[]{:S(2)}, u32[]{:S(2)}) async-start(f32[32,1,256]{2,1,0:T(1,128)} %shard_map.41.after), calls=%async_computation.1 | async-start | bytes 65536 | tf_op jit(solution)/shard_map/all_to_all | solution.py:585
  57.9 5.9 %collective-permute-start.5 = (f32[5,16,128]{2,1,0:T(8,128)S(1)}, f32[5,16,128]{2,1,0:T(8,128)S(1)}, u32[]{:S(2)}, u32[]{:S(2)}) collective-permute-start(f32[5,16,128]{2,1,0:T(8,128)S(1)} %get-tuple-element.46.after), channel_id=1, source_target_pairs={{0,992},{32,64},{64,32},{96,128},{128,96},{160,192},{192,160},{224... | collective-permute-start | bytes 122888 | tf_op jit(solution)/shard_map/ppermute | solution.py:553
  60.9 3.1 %collective-permute-start.4 = (f32[5,16,128]{2,1,0:T(8,128)S(1)}, f32[5,16,128]{2,1,0:T(8,128)S(1)}, u32[]{:S(2)}, u32[]{:S(2)}) collective-permute-start(f32[5,16,128]{2,1,0:T(8,128)S(1)} %get-tuple-element.46.after), channel_id=1, source_target_pairs={{0,32},{32,0},{64,96},{96,64},{128,160},{160,128},{192,224},{224,1... | collective-permute-start | bytes 122888 | tf_op jit(solution)/shard_map/ppermute | solution.py:553

commit v8 on v7

--- a/solution.py
+++ b/solution.py
@@ -546,10 +546,14 @@
     )(*operands, *after)
 
 
-def swapped(axis, first, second):
+def pairings(axis):
     count = lax.axis_size(axis)
     pairs = [(i, i ^ 1) for i in range(count)]
-    others = [(i, (i + 1 if i % 2 else i - 1) % count) for i in range(count)]
+    return pairs, [(i, (i + 1 if i % 2 else i - 1) % count) for i in range(count)]
+
+
+def swapped(axis, first, second):
+    pairs, others = pairings(axis)
     return lax.ppermute(first, axis, pairs), lax.ppermute(second, axis, others)
 
 
@@ -570,7 +574,9 @@
     own = kernel_call(tally, [(8, 128)] * 5, [], *block)
     (sums,) = kernel_call(announce, [(along_x, 1, 256)], [], *flags, *own)
     sums = lax.all_to_all(sums, "gx", 0, 0, tiled=True)
-    halo = swapped("gz", *rows)
+    pairs, others = pairings("gz")
+    near_rows = lax.ppermute(rows[0], "gz", pairs)
+    halo = near_rows, lax.ppermute(rows[1], "gz", others)
     (sums,) = kernel_call(cross, [(along_z, 1, 256)], [], sums.reshape(along_x, 256))
     laid, flags, entry, edges = kernel_call(
         lay_out,

time: 71 us -> 71 us (level)
    ppermute x0 -> x2, starting transfers between devices: none -> 12.7 us  [the longest x1 8.62 us: local(): halo = (near_rows, lax.ppermute(rows[1], 'gz', others))]
    ppermute x3 -> x2, starting transfers between devices: 15.5 us -> 6.86 us  [swapped(): lax.ppermute(second, axis, others)]
    ppermute x3 -> x2, starting transfers between devices: 7.97 us -> 3.84 us  [swapped(): lax.ppermute(first, axis, pairs)]
    ppermute x3 -> x2, waiting for transfers between devices: 4.94 us -> 4.94 us  [swapped(): lax.ppermute(second, axis, others)]
where the time goes in v8:
time: 71 us; the launch traced here: 70.6 us
  starting transfers between devices  28.2 us (40%)
  blocking collectives  27.2 us (38%)
  waiting for transfers between devices  9.46 us (13%)
  Pallas kernels  5.67 us (8%)
    all_to_all x1, blocking collectives, local(): sums = lax.all_to_all(sums, 'gx', 0, 0, tiled=True)  27.2 us
    ppermute x1, starting transfers between devices, local(): halo = (near_rows, lax.ppermute(rows[1], 'gz', others))  8.62 us
    ppermute x2, starting transfers between devices, swapped(): lax.ppermute(second, axis, others)  6.86 us
    ppermute x2, waiting for transfers between devices, swapped(): lax.ppermute(second, axis, others)  4.94 us
    all_to_all x1, starting transfers between devices, local(): sums = lax.all_to_all(sums, 'gz', 0, 0, tiled=True)  4.72 us
    all_to_all x1, waiting for transfers between devices, local(): sums = lax.all_to_all(sums, 'gz', 0, 0, tiled=True)  4.29 us
    ppermute x1, starting transfers between devices, local(): near_rows = lax.ppermute(rows[0], 'gz', pairs)  4.13 us
    ppermute x2, starting transfers between devices, swapped(): lax.ppermute(first, axis, pairs)  3.84 us
  transfers between devices with their start and end apart: 7, of which 4 were waited for; matrix products, arithmetic and copies ran while one was open for 0% of the time, Pallas kernels for 3%

profile of v8, /device:TPU:1, one launch (start us, length us, event | category | flops | bytes accessed | tf_op | source)
XLA Modules:
  0.0 70.6 jit_solution(6164400790114375369)
XLA Ops:
  0.0 1.2 %shard_map.37 = (f32[8,128]{1,0:T(8,128)S(1)}, f32[8,128]{1,0:T(8,128)S(1)}, f32[19,8,8,128]{3,2,1,0:T(8,128)S(1)}, s32[8,8,128]{2,1,0:T(8,128)S(1)}, f32[5,8,128]{2,1,0:T(8,128)S(1)}) custom-call(f32[19,8,8,128]{3,2,1,0:T(8,128)} %pops_hbm.1, s32[8,8,128]{2,1,0:T(8,128)} %solid_hbm.1, f32[5,8,128]{2,1,0:T(8,128)} %inflow_hbm.1), custom_call_target="tpu_custom_call" | custom-call | tf_op jit(solution)/shard_map/pallas_call | solution.py:537
  1.2 0.3 shard_map.38
  1.5 4.1 %collective-permute-start = (f32[40,8,128]{2,1,0:T(8,128)S(1)}, f32[40,8,128]{2,1,0:T(8,128)S(1)}, u32[]{:S(2)}, u32[]{:S(2)}) collective-permute-start(f32[40,8,128]{2,1,0:T(8,128)S(1)} %get-tuple-element.35), channel_id=1, source_target_pairs={{0,1},{1,0},{2,3},{3,2},{4,5},{5,4},{6,7},{7,6},{8,9},{9,8},{10,11... | collective-permute-start | bytes 491528 | tf_op jit(solution)/shard_map/ppermute | solution.py:578
  5.6 8.6 %collective-permute-start.1 = (f32[40,8,128]{2,1,0:T(8,128)S(1)}, f32[40,8,128]{2,1,0:T(8,128)S(1)}, u32[]{:S(2)}, u32[]{:S(2)}) collective-permute-start(f32[40,8,128]{2,1,0:T(8,128)S(1)} %get-tuple-element.36), channel_id=1, source_target_pairs={{0,31},{1,2},{2,1},{3,4},{4,3},{5,6},{6,5},{7,8},{8,7},{9,10},{10,... | collective-permute-start | bytes 491528 | tf_op jit(solution)/shard_map/ppermute | solution.py:579
  14.3 1.9 %collective-permute-start.2 = (f32[8,128]{1,0:T(8,128)S(1)}, f32[8,128]{1,0:T(8,128)S(1)}, u32[]{:S(2)}, u32[]{:S(2)}) collective-permute-start(f32[8,128]{1,0:T(8,128)S(1)} %get-tuple-element.37), channel_id=1, source_target_pairs={{0,1},{1,0},{2,3},{3,2},{4,5},{5,4},{6,7},{7,6},{8,9},{9,8},{10,11... | collective-permute-start | bytes 12296 | tf_op jit(solution)/shard_map/ppermute | solution.py:557
  16.2 3.8 %collective-permute-start.3 = (f32[8,128]{1,0:T(8,128)S(1)}, f32[8,128]{1,0:T(8,128)S(1)}, u32[]{:S(2)}, u32[]{:S(2)}) collective-permute-start(f32[8,128]{1,0:T(8,128)S(1)} %get-tuple-element.38), channel_id=1, source_target_pairs={{0,31},{1,2},{2,1},{3,4},{4,3},{5,6},{6,5},{7,8},{8,7},{9,10},{10,... | collective-permute-start | bytes 12296 | tf_op jit(solution)/shard_map/ppermute | solution.py:557
  20.0 0.3 shard_map.39
  20.3 0.0 collective-permute-done.2.first.first_flags
  20.3 4.5 %collective-permute-done.3.second.second_flags = f32[8,128]{1,0:T(8,128)S(1)} collective-permute-done((f32[8,128]{1,0:T(8,128)S(1)}, f32[8,128]{1,0:T(8,128)S(1)}, u32[]{:S(2)}, u32[]{:S(2)}) %collective-permute-start.3) | collective-permute-done | bytes 4128 | tf_op jit(solution)/shard_map/ppermute | solution.py:557
  24.8 0.1 shard_map.40
  24.9 27.2 %all_to_all.10 = f32[32,1,256]{2,1,0:T(1,128)S(1)} all-to-all(f32[32,1,256]{2,1,0:T(1,128)S(1)} %shard_map.40), channel_id=1, replica_groups=mesh['gx'=32,'gz'=32] {'gx'}, dimensions={0} | all-to-all | bytes 65536 | tf_op jit(solution)/shard_map/all_to_all | solution.py:576
  52.1 0.7 %shard_map.41.after = f32[32,1,256]{2,1,0:T(1,128)} custom-call(f32[32,256]{1,0:T(8,128)S(1)} %bitcast.3), custom_call_target="tpu_custom_call" | custom-call | tf_op jit(solution)/shard_map/pallas_call | solution.py:537
  52.8 4.7 %all-to-all-start.1 = ((f32[32,1,256]{2,1,0:T(1,128)}), f32[32,1,256]{2,1,0:T(1,128)S(1)}, u32[]{:S(2)}, u32[]{:S(2)}) async-start(f32[32,1,256]{2,1,0:T(1,128)} %shard_map.41.after), calls=%async_computation.1 | async-start | bytes 65536 | tf_op jit(solution)/shard_map/all_to_all | solution.py:591
  57.5 0.0 collective-permute-done.first
  57.5 0.0 collective-permute-done.1.second
  57.5 0.3 shard_map.42
  57.9 3.1 %collective-permute-start.5 = (f32[5,16,128]{2,1,0:T(8,128)S(1)}, f32[5,16,128]{2,1,0:T(8,128)S(1)}, u32[]{:S(2)}, u32[]{:S(2)}) collective-permute-start(f32[5,16,128]{2,1,0:T(8,128)S(1)} %get-tuple-element.46.after), channel_id=1, source_target_pairs={{0,992},{32,64},{64,32},{96,128},{128,96},{160,192},{192,160},{224... | collective-permute-start | bytes 122888 | tf_op jit(solution)/shard_map/ppermute | solution.py:557
  60.9 1.9 %collective-permute-start.4 = (f32[5,16,128]{2,1,0:T(8,128)S(1)}, f32[5,16,128]{2,1,0:T(8,128)S(1)}, u32[]{:S(2)}, u32[]{:S(2)}) collective-permute-start(f32[5,16,128]{2,1,0:T(8,128)S(1)} %get-tuple-element.46.after), channel_id=1, source_target_pairs={{0,32},{32,0},{64,96},{96,64},{128,160},{160,128},{192,224},{224,1... | collective-permute-start | bytes 122888 | tf_op jit(solution)/shard_map/ppermute | solution.py:557
  62.8 0.5 shard_map.43
  63.3 0.5 collective-permute-done.5.far
  63.8 0.2 collective-permute-done.4.near
  64.0 0.3 shard_map.44
  64.3 4.3 %all-to-all-done.1.refs_12_ = f32[32,1,256]{2,1,0:T(1,128)S(1)} async-done(((f32[32,1,256]{2,1,0:T(1,128)}), f32[32,1,256]{2,1,0:T(1,128)S(1)}, u32[]{:S(2)}, u32[]{:S(2)}) %all-to-all-start.1) | async-done | bytes 32800 | tf_op jit(solution)/shard_map/all_to_all | solution.py:591
  68.6 2.0 %shard_map.45 = f32[19,8,8,128]{3,2,1,0:T(8,128)} custom-call(f32[2,19,16,128]{3,2,1,0:T(8,128)S(1)} %get-tuple-element.47.refs_0_, f32[8,19,16,128]{3,2,1,0:T(8,128)S(1)} %get-tuple-element.48.refs_1_, f32[8,4,16,128]{3,2,1,0:T(8,128)S(1)} %get-tuple-element.49.refs_2_, f32[2,16,128]{2,1,0:T(8,128)S(1)} %get-tuple-element.50.flags.refs_3_, ...), custom_call_target="tpu_custom_call" | custom-call | tf_op jit(solution)/shard_map/pallas_call | solution.py:610
  (1 shorter events, 0.0 us)
Async XLA Ops:
  1.5 56.0 %collective-permute-start = (f32[40,8,128]{2,1,0:T(8,128)S(1)}, f32[40,8,128]{2,1,0:T(8,128)S(1)}, u32[]{:S(2)}, u32[]{:S(2)}) collective-permute-start(f32[40,8,128]{2,1,0:T(8,128)S(1)} %get-tuple-element.35), channel_id=1, source_target_pairs={{0,1},{1,0},{2,3},{3,2},{4,5},{5,4},{6,7},{7,6},{8,9},{9,8},{10,11... | collective-permute-start | bytes 491528 | tf_op jit(solution)/shard_map/ppermute | solution.py:578
  5.6 51.9 %collective-permute-start.1 = (f32[40,8,128]{2,1,0:T(8,128)S(1)}, f32[40,8,128]{2,1,0:T(8,128)S(1)}, u32[]{:S(2)}, u32[]{:S(2)}) collective-permute-start(f32[40,8,128]{2,1,0:T(8,128)S(1)} %get-tuple-element.36), channel_id=1, source_target_pairs={{0,31},{1,2},{2,1},{3,4},{4,3},{5,6},{6,5},{7,8},{8,7},{9,10},{10,... | collective-permute-start | bytes 491528 | tf_op jit(solution)/shard_map/ppermute | solution.py:579
  14.3 6.0 %collective-permute-start.2 = (f32[8,128]{1,0:T(8,128)S(1)}, f32[8,128]{1,0:T(8,128)S(1)}, u32[]{:S(2)}, u32[]{:S(2)}) collective-permute-start(f32[8,128]{1,0:T(8,128)S(1)} %get-tuple-element.37), channel_id=1, source_target_pairs={{0,1},{1,0},{2,3},{3,2},{4,5},{5,4},{6,7},{7,6},{8,9},{9,8},{10,11... | collective-permute-start | bytes 12296 | tf_op jit(solution)/shard_map/ppermute | solution.py:557
  16.2 8.6 %collective-permute-start.3 = (f32[8,128]{1,0:T(8,128)S(1)}, f32[8,128]{1,0:T(8,128)S(1)}, u32[]{:S(2)}, u32[]{:S(2)}) collective-permute-start(f32[8,128]{1,0:T(8,128)S(1)} %get-tuple-element.38), channel_id=1, source_target_pairs={{0,31},{1,2},{2,1},{3,4},{4,3},{5,6},{6,5},{7,8},{8,7},{9,10},{10,... | collective-permute-start | bytes 12296 | tf_op jit(solution)/shard_map/ppermute | solution.py:557
  52.8 15.8 %all-to-all-start.1 = ((f32[32,1,256]{2,1,0:T(1,128)}), f32[32,1,256]{2,1,0:T(1,128)S(1)}, u32[]{:S(2)}, u32[]{:S(2)}) async-start(f32[32,1,256]{2,1,0:T(1,128)} %shard_map.41.after), calls=%async_computation.1 | async-start | bytes 65536 | tf_op jit(solution)/shard_map/all_to_all | solution.py:591
  57.9 5.9 %collective-permute-start.5 = (f32[5,16,128]{2,1,0:T(8,128)S(1)}, f32[5,16,128]{2,1,0:T(8,128)S(1)}, u32[]{:S(2)}, u32[]{:S(2)}) collective-permute-start(f32[5,16,128]{2,1,0:T(8,128)S(1)} %get-tuple-element.46.after), channel_id=1, source_target_pairs={{0,992},{32,64},{64,32},{96,128},{128,96},{160,192},{192,160},{224... | collective-permute-start | bytes 122888 | tf_op jit(solution)/shard_map/ppermute | solution.py:557
  60.9 3.1 %collective-permute-start.4 = (f32[5,16,128]{2,1,0:T(8,128)S(1)}, f32[5,16,128]{2,1,0:T(8,128)S(1)}, u32[]{:S(2)}, u32[]{:S(2)}) collective-permute-start(f32[5,16,128]{2,1,0:T(8,128)S(1)} %get-tuple-element.46.after), channel_id=1, source_target_pairs={{0,32},{32,0},{64,96},{96,64},{128,160},{160,128},{192,224},{224,1... | collective-permute-start | bytes 122888 | tf_op jit(solution)/shard_map/ppermute | solution.py:557
